TPU v7x, 32 devices: a whole 2x2x4 slice. The times are simulated.
32 devices in a mesh: groups: 2 (over x), blk: 16 (over z, y, core).
Axes of the slice: x: 2, y: 2, z: 4, core: 2. Of those that a mesh axis runs over, the one named last changes fastest.
Arguments:
- pair_elements: float32 [12288, 1024], P(('groups', 'blk')), parts along dimension 0, may hold values from -0.8 to 0.8
- gmap: int32 [12288], P(('groups', 'blk')), parts along dimension 0, may hold values from 0 to 6143, as said below
- w_screened: float32 [12288, 6144], P('groups', 'blk'), parts along dimension 0, as said below
- coulomb: float32 [12288], P(('groups', 'blk')), parts along dimension 0, may hold values from 0.001 to 0.02
Outputs:
- screened: float32 [12288, 1024], P(('groups', 'blk')), parts along dimension 0
- pair_sigma: float32 [2048], P(('groups', 'blk')), parts along dimension 0
There are 2 independent parts, one for each index of `groups`. A program takes and returns all parts, laid end to end along the dimension named above; each array names one. Nothing has to cross between parts.
Inputs may be any that keep to these rules, and one draw needn't show every extreme that they name: `gmap`: each aligned block of 384 entries is a permutation of that block's own indices. `w_screened`: symmetric.
All inputs are finite; a program needn't handle non-finite values.
Results may differ from a plain program's by a relative error of at most 0.00013.
Values sent between devices are 32-bit elements; how exact they have to be, the bound alone decides.
No kernel may reach another device: no remote copies, remote signals or barrier semaphores. Data moves between devices by JAX's collectives and lax.ppermute only.
A program may use at most 256 MiB of HBM per device.

v0:
```python
import functools

import jax
import jax.numpy as jnp
from jax import lax
from jax.experimental import pallas as pl
from jax.experimental.pallas import tpu as pltpu
from jax.sharding import PartitionSpec as P


NB = 64
OCC = 4
LIMIT = 20 << 20
DOTS_LIMIT = 46 << 20


def chip_ring(mesh):
    row = mesh.devices.reshape(mesh.shape["groups"], -1)[0]
    places = [tuple(getattr(d, "coords", (0, 0, i // 2))) for i, d in enumerate(row)]
    chips = {}
    for index, place in enumerate(places):
        chips.setdefault(place, []).append(index)
    ordered = []
    spread = [len({p[k] for p in chips}) for k in range(3)]
    long = max(range(3), key=lambda k: spread[k])
    lanes = {}
    for p in chips:
        lanes.setdefault(tuple(v for k, v in enumerate(p) if k != long), []).append(p)
    for number, lane in enumerate(sorted(lanes)):
        line = sorted(lanes[lane], key=lambda p: p[long])
        ordered += line[::-1] if number % 2 else line
    return [chips[p] for p in ordered]


def split(x):
    high = x.astype(jnp.bfloat16)
    return high, (x - high.astype(jnp.float32)).astype(jnp.bfloat16)


def dots_kernel(at, first, watch, blocks, x0, x1, w_own, w_partner, *refs):
    left, landed, sems = refs[-3:]
    refs = refs[:-3]
    out = refs[-watch - 1]
    rows = landed.shape[1]
    wide = x0.shape[0]

    def copies(way):
        here = pl.ds(pl.multiple_of(blocks[at + way] * rows, rows), rows)
        for k, w in enumerate((w_own, w_partner)):
            yield pltpu.make_async_copy(
                w.at[here], landed.at[way, :, k * rows : (k + 1) * rows], sems.at[way, k]
            )

    for way in (0, 1):
        for copy in copies(way):
            copy.start()
    for way, x in enumerate((x0, x1)):
        xh, xl = split(x[...])
        for i, part in enumerate((xh, xl, xh)):
            left[way, :, i * rows : (i + 1) * rows] = part

    def product(way):
        for copy in copies(way):
            copy.wait()
        wh, wl = split(landed[way])
        total = jnp.dot(left[way], jnp.concatenate([wh, wh, wl], 0), preferred_element_type=jnp.float32)
        mine = pl.ds(way * wide if isinstance(way, int) else pl.multiple_of(way * wide, wide), wide)
        if not first:
            total = refs[0][mine, :] + total
        out[mine, :] = total
        return total

    if watch:
        for way in (0, 1):
            seen = product(way) * jnp.concatenate([refs[1 + way][...], refs[3 + way][...]], 1)
            seen = functools.reduce(lambda p, q: p + q, [seen[:, i : i + 128] for i in range(0, 2 * rows, 128)])
            refs[-1][way * wide : (way + 1) * wide, :] = seen
    else:

        @pl.loop(0, 2)
        def _(way):
            product(way)


def dots(blocks, at, pieces, w_own, w_partner, total=None, start=None):
    wide, rows = pieces[0].shape
    vmem = pl.BlockSpec(memory_space=pltpu.VMEM)
    hbm = pl.BlockSpec(memory_space=pltpu.HBM)
    more = [] if total is None else [total]
    watch = [] if start is None else list(start)
    shape = jax.ShapeDtypeStruct((2 * wide, 2 * rows), jnp.float32)
    form = jax.ShapeDtypeStruct((2 * wide, 128), jnp.float32)
    out = pl.pallas_call(
        functools.partial(dots_kernel, at, total is None, int(start is not None)),
        out_shape=(shape, form) if watch else (shape,),
        in_specs=[pl.BlockSpec(memory_space=pltpu.SMEM), vmem, vmem, hbm, hbm] + [vmem] * (len(more) + len(watch)),
        out_specs=(vmem, vmem)[: 2 if watch else 1],
        scratch_shapes=[
            pltpu.VMEM((2, wide, 3 * rows), jnp.bfloat16),
            pltpu.VMEM((2, rows, 2 * rows), jnp.float32),
            pltpu.SemaphoreType.DMA((2, 2)),
        ],
        input_output_aliases={5: 0} if more else {},
        cost_estimate=pl.CostEstimate(
            flops=24 * rows * rows * wide, bytes_accessed=16 * rows * rows, transcendentals=0
        ),
        compiler_params=pltpu.CompilerParams(vmem_limit_bytes=DOTS_LIMIT),
        name="dots",
    )(blocks, *pieces, w_own, w_partner, *more, *watch)
    return out if watch else (out[0], None)


def fetch_kernel(at, blocks, w_own, w_partner, out, landed, sems):
    rows = landed.shape[1]
    copies = []
    for k, w in enumerate((w_partner, w_own)):
        for way in (0, 1):
            here = pl.ds(pl.multiple_of(blocks[at + way] * rows, rows), rows)
            copies.append(pltpu.make_async_copy(w.at[here], landed.at[2 * k + way], sems.at[2 * k + way]))
    for copy in copies:
        copy.start()
    for i, copy in enumerate(copies):
        copy.wait()
        high, low = split(landed[i])
        out[i] = jnp.concatenate([high, low], 0)


def fetch(blocks, at, w_own, w_partner):
    rows = w_own.shape[1]
    hbm = pl.BlockSpec(memory_space=pltpu.HBM)
    return pl.pallas_call(
        functools.partial(fetch_kernel, at),
        out_shape=jax.ShapeDtypeStruct((4, 2 * rows, rows), jnp.bfloat16),
        in_specs=[pl.BlockSpec(memory_space=pltpu.SMEM), hbm, hbm],
        out_specs=pl.BlockSpec(memory_space=pltpu.VMEM),
        scratch_shapes=[pltpu.VMEM((4, rows, rows), jnp.float32), pltpu.SemaphoreType.DMA((4,))],
        cost_estimate=pl.CostEstimate(flops=8 * rows * rows, bytes_accessed=40 * rows * rows, transcendentals=0),
        compiler_params=pltpu.CompilerParams(vmem_limit_bytes=DOTS_LIMIT),
        name="fetch",
    )(blocks, w_own, w_partner)


def last_part(k, way, x, right, total):
    wide, rows = x.shape
    xh, xl = split(x[...])
    at = 2 * (1 - k) + way
    high, low = right[at, :rows], right[at, rows:]
    part = jnp.dot(
        jnp.concatenate([xh, xl, xh], 1), jnp.concatenate([high, high, low], 0), preferred_element_type=jnp.float32
    )
    return total[way * wide : (way + 1) * wide, k * rows : (k + 1) * rows] + part


def give_kernel(x0, x1, right, total, out):
    wide = x0.shape[0]
    for way, x in enumerate((x0, x1)):
        out[way * wide : (way + 1) * wide, :] = last_part(1, way, x, right, total)


def finish_partner(pieces, right, total):
    wide, rows = pieces[0].shape
    vmem = pl.BlockSpec(memory_space=pltpu.VMEM)
    return pl.pallas_call(
        give_kernel,
        out_shape=jax.ShapeDtypeStruct((2 * wide, rows), jnp.float32),
        in_specs=[vmem] * 4,
        out_specs=vmem,
        cost_estimate=pl.CostEstimate(flops=12 * rows * rows * wide, bytes_accessed=16 * rows * rows, transcendentals=0),
        compiler_params=pltpu.CompilerParams(vmem_limit_bytes=DOTS_LIMIT),
        name="finish",
    )(*pieces, right, total)


def send_out(value, way, base, turned, sems, out):
    wide = value.shape[0]
    turned[way] = value.T
    columns = pl.ds(pl.multiple_of(base + way * wide, wide), wide)
    copy = pltpu.make_async_copy(turned.at[way], out.at[:, columns], sems.at[way])
    copy.start()
    return copy


def own_kernel(core, x0, x1, right, total, out, turned, sems):
    wide = x0.shape[0]
    copies = [
        send_out(last_part(0, way, x, right, total), way, core[0] * 2 * wide, turned, sems, out)
        for way, x in enumerate((x0, x1))
    ]
    for copy in copies:
        copy.wait()


def finish_own(core, pieces, right, total):
    wide, rows = pieces[0].shape
    vmem = pl.BlockSpec(memory_space=pltpu.VMEM)
    return pl.pallas_call(
        own_kernel,
        out_shape=jax.ShapeDtypeStruct((rows, 4 * wide), jnp.float32),
        in_specs=[pl.BlockSpec(memory_space=pltpu.SMEM)] + [vmem] * 4,
        out_specs=pl.BlockSpec(memory_space=pl.ANY),
        scratch_shapes=[pltpu.VMEM((2, rows, wide), jnp.float32), pltpu.SemaphoreType.DMA((2,))],
        cost_estimate=pl.CostEstimate(flops=12 * rows * rows * wide, bytes_accessed=16 * rows * rows, transcendentals=0),
        compiler_params=pltpu.CompilerParams(vmem_limit_bytes=DOTS_LIMIT),
        name="finish_own",
    )(core.reshape(1), *pieces, right, total)


def other_kernel(core, x, _, out, turned, sems):
    wide = turned.shape[2]
    count = turned.shape[0]
    copies = [
        send_out(x[i * wide : (i + 1) * wide, :], i, (1 - core[0]) * count * wide, turned, sems, out)
        for i in range(count)
    ]
    for copy in copies:
        copy.wait()


def place_other(core, other, out):
    half, rows = other.shape
    return pl.pallas_call(
        other_kernel,
        out_shape=jax.ShapeDtypeStruct((rows, 2 * half), jnp.float32),
        in_specs=[
            pl.BlockSpec(memory_space=pltpu.SMEM),
            pl.BlockSpec(memory_space=pltpu.VMEM),
            pl.BlockSpec(memory_space=pl.ANY),
        ],
        out_specs=pl.BlockSpec(memory_space=pl.ANY),
        scratch_shapes=[pltpu.VMEM((4, rows, half // 4), jnp.float32), pltpu.SemaphoreType.DMA((4,))],
        input_output_aliases={2: 0},
        compiler_params=pltpu.CompilerParams(vmem_limit_bytes=DOTS_LIMIT),
        name="place",
    )(core.reshape(1), other, out)


def take_kernel(side, block, gmap, *refs):
    outs, landed, order, sems = refs[:-3], refs[-3], refs[-2], refs[-1]
    rows, width = block.shape
    quarter = width // 4
    copies = []
    for at in (0, 1):
        columns = pl.ds(pl.multiple_of((2 * side[0] + at) * quarter, quarter), quarter)
        copies.append(pltpu.make_async_copy(block.at[:, columns], landed.at[at], sems.at[at]))
    ordered = pltpu.make_async_copy(gmap, order, sems.at[2])
    for copy in (copies[0], ordered, copies[1]):
        copy.start()
    ordered.wait()
    pick = (lax.broadcasted_iota(jnp.int32, (rows, rows), 0) == lax.rem(order[...], rows)[None, :]).astype(jnp.bfloat16)
    pick = jnp.concatenate([pick, pick, pick], 0)
    for at in (0, 1):
        copies[at].wait()
        x = landed[at].T
        high, rest = split(x)
        rest = x - high.astype(jnp.float32)
        mid, low = split(rest)
        got = jnp.dot(jnp.concatenate([high, mid, low], 1), pick, preferred_element_type=jnp.float32)
        if len(outs) == 2:
            outs[at][...] = got
        else:
            outs[0][at * quarter : (at + 1) * quarter, :] = got


def take(side, pair_elements, gmap, pieces):
    rows, width = pair_elements.shape
    piece = jax.ShapeDtypeStruct((width // 2 // pieces, rows), jnp.float32)
    hbm = pl.BlockSpec(memory_space=pltpu.HBM)
    return pl.pallas_call(
        take_kernel,
        out_shape=(piece,) * pieces,
        in_specs=[pl.BlockSpec(memory_space=pltpu.SMEM), hbm, hbm],
        out_specs=(pl.BlockSpec(memory_space=pltpu.VMEM),) * pieces,
        scratch_shapes=[
            pltpu.VMEM((2, rows, width // 4), jnp.float32),
            pltpu.VMEM((rows,), jnp.int32),
            pltpu.SemaphoreType.DMA((3,)),
        ],
        cost_estimate=pl.CostEstimate(flops=3 * rows * rows * width, bytes_accessed=4 * rows * width, transcendentals=0),
        compiler_params=pltpu.CompilerParams(vmem_limit_bytes=LIMIT),
        name="take",
    )(side.reshape(1), *(pltpu.with_memory_space_constraint(x, pltpu.HBM) for x in (pair_elements, gmap)))


def solution(mesh):
    ring = chip_ring(mesh)
    n = len(ring)
    size = 2 * n
    ahead = [(a, b) for i in range(n) for a, b in zip(ring[i], ring[(i + 1) % n])]
    back = [(b, a) for a, b in ahead]
    partner = [(i, i ^ 1) for i in range(size)]
    spot_of = {index: i for i, chip in enumerate(ring) for index in chip}
    sources = [
        [[ring[(spot_of[d] - step * way) % n][0] // 2 for step in range(n)] for way in (1, -1)] for d in range(size)
    ]

    bits = [1 << i for i in range(size.bit_length() - 1)]
    phases = [(bit,) for bit in bits[:-2]] + [(bits[-1], bits[-2])]

    def local(pair_elements, gmap, w_screened, coulomb):
        _, width = pair_elements.shape
        half = width // 2
        wide = half // 2
        me = lax.axis_index("blk")
        core = me % 2
        source = lax.dynamic_index_in_dim(jnp.array(sources, jnp.int32), me, 0, keepdims=False)
        blocks = (2 * source.T[:, None, :] + ((core + jnp.arange(2)) % 2)[None, :, None]).reshape(n * 4)
        here = core * half
        mine = list(take(core, pair_elements, gmap, 2))
        (away,) = take(1 - core, pair_elements, gmap, 1)
        given = lax.ppermute(away, "blk", partner)
        w_late, _ = lax.optimization_barrier((w_screened, away))
        w_partner = lax.ppermute(w_late, "blk", partner)
        held = [mine, [given[way * wide : (way + 1) * wide] for way in (0, 1)]]
        start = list(held)

        band = (here + jnp.arange(half, dtype=jnp.int32)) % NB
        coef = jnp.where(band < OCC, -0.5, 0.5).astype(jnp.float32)
        start = [x for pair in start for x in pair]
        total = None
        form = None
        terms = None

        def exchange(terms, bits, left):
            at = [left.index(bit) for bit in bits]
            terms = terms.reshape((2,) * len(left) + (-1,))
            terms = jnp.moveaxis(terms, at, range(len(at))).reshape(1 << len(at), -1)
            mine = sum(((me // bit) % 2) << (len(bits) - 1 - i) for i, bit in enumerate(bits))
            kept = lax.dynamic_index_in_dim(terms, mine, 0, keepdims=False)
            for x in range(1, 1 << len(bits)):
                mask = sum(bit for i, bit in enumerate(bits) if (x >> (len(bits) - 1 - i)) & 1)
                sent = lax.dynamic_index_in_dim(terms, mine ^ x, 0, keepdims=False)
                kept = kept + lax.ppermute(sent, "blk", [(b, b ^ mask) for b in range(size)])
            return kept

        for step in range(n):
            for c in (0, 1):
                if step:
                    held[c] = [lax.ppermute(held[c][way], "blk", back if way else ahead) for way in (0, 1)]
                look = c == 1 and step in (0, n // 2 - 1, n // 2)
                use = held[c]
                if step == n - 1 and c == 1:
                    terms, *use = lax.optimization_barrier((terms, *use))
                    other = finish_partner(use, right, total)
                    other = lax.ppermute(other, "blk", partner)
                    screened = finish_own(core, use, right, total)
                    break
                total, seen = dots(blocks, 4 * step + 2 * c, use, w_screened, w_partner, total, start if look else None)
                if step == n - 1:
                    right = fetch(blocks, 4 * step + 2, w_screened, w_partner)
                if look:
                    form = -seen if step == 0 else form + seen
            if step == n // 2:
                own_bare = -0.5 * jnp.sum(jnp.concatenate(mine, 0) ** 2 * coulomb[None, :], axis=1)
                away_bare = -0.5 * jnp.sum(away * away * coulomb[None, :], axis=1)
                form = own_bare + coef * jnp.sum(form, axis=1)
                terms = jnp.where(core == 0, jnp.concatenate([form, away_bare]), jnp.concatenate([away_bare, form]))
                left = [bit for phase in reversed(phases) for bit in phase]
                for phase in phases:
                    terms = exchange(terms, phase, left)
                    left = [bit for bit in left if bit not in phase]
        screened = place_other(core, other, screened)
        return screened, terms

    in_specs = (
        P(("groups", "blk"), None),
        P(("groups", "blk")),
        P("groups", "blk"),
        P(("groups", "blk")),
    )
    out_specs = (P(("groups", "blk"), None), P(("groups", "blk")))
    return jax.shard_map(local, mesh=mesh, in_specs=in_specs, out_specs=out_specs, check_vma=False)
```

profile of v0, /device:TPU:0, one launch (start us, length us, event | category | flops | bytes accessed | tf_op | source)
XLA Modules:
  0.0 193.8 jit_solution(3077177419018304390)
XLA Ops:
  0.6 2.2 %take.3 = f32[512,384]{1,0:T(8,128)S(1)} custom-call(s32[1]{0:T(128)} %bitcast.3.side, f32[384,1024]{1,0:T(8,128)} %block.3, s32[384]{0:T(512)} %gmap.3), custom_call_target="tpu_custom_call" | custom-call | flops 452984832 | bytes 1572864 | tf_op jit(solution)/shard_map/take/pallas_call | solution.py:268
  3.5 2.2 %take.2 = (f32[256,384]{1,0:T(8,128)S(1)}, f32[256,384]{1,0:T(8,128)S(1)}) custom-call(s32[1]{0:T(128)} %bitcast.side.core, f32[384,1024]{1,0:T(8,128)} %block.3, s32[384]{0:T(512)} %gmap.3), custom_call_target="tpu_custom_call" | custom-call | flops 452984832 | bytes 1572864 | tf_op jit(solution)/shard_map/take/pallas_call | solution.py:268
  5.6 3.0 %collective-permute-start.11 = (f32[256,384]{1,0:T(8,128)S(1)}, f32[256,384]{1,0:T(8,128)S(1)}, u32[]{:S(2)}, u32[]{:S(2)}) collective-permute-start(f32[256,384]{1,0:T(8,128)S(1)} %get-tuple-element.15.x1.refs_2_), channel_id=1, source_target_pairs={{4,0},{5,1},{8,4},{9,5},{12,8},{13,9},{14,12},{15,13},{10,14},{11,... | collective-permute-start | bytes 1179656 | tf_op jit(solution)/shard_map/ppermute | solution.py:338
  8.8 10.2 %collective-permute-done = f32[512,384]{1,0:T(8,128)S(1)} collective-permute-done((f32[512,384]{1,0:T(8,128)S(1)}, f32[512,384]{1,0:T(8,128)S(1)}, u32[]{:S(2)}, u32[]{:S(2)}) %collective-permute-start) | collective-permute-done | bytes 786464 | tf_op jit(solution)/shard_map/ppermute | solution.py:310
  19.1 3.0 %collective-permute-start.2 = (f32[256,384]{1,0:T(8,128)S(1)}, f32[256,384]{1,0:T(8,128)S(1)}, u32[]{:S(2)}, u32[]{:S(2)}) collective-permute-start(f32[256,384]{1,0:T(8,128)S(1)} %get-tuple-element.29.x0.refs_3_), channel_id=1, source_target_pairs={{0,4},{1,5},{4,8},{5,9},{8,12},{9,13},{12,14},{13,15},{14,10},{15,... | collective-permute-start | bytes 1179656 | tf_op jit(solution)/shard_map/ppermute | solution.py:338
  22.1 2.0 %collective-permute-start.9 = (f32[256,384]{1,0:T(8,128)S(1)}, f32[256,384]{1,0:T(8,128)S(1)}, u32[]{:S(2)}, u32[]{:S(2)}) collective-permute-start(f32[256,384]{1,0:T(8,128)S(1)} %collective-permute-done.8.x0), channel_id=1, source_target_pairs={{0,4},{1,5},{4,8},{5,9},{8,12},{9,13},{12,14},{13,15},{14,10},{15,... | collective-permute-start | bytes 1179656 | tf_op jit(solution)/shard_map/ppermute | solution.py:338
  24.1 7.8 %collective-permute-done.2.x0 = f32[256,384]{1,0:T(8,128)S(1)} collective-permute-done((f32[256,384]{1,0:T(8,128)S(1)}, f32[256,384]{1,0:T(8,128)S(1)}, u32[]{:S(2)}, u32[]{:S(2)}) %collective-permute-start.2) | collective-permute-done | bytes 393248 | tf_op jit(solution)/shard_map/ppermute | solution.py:338
  31.9 2.1 %collective-permute-start.3 = (f32[256,384]{1,0:T(8,128)S(1)}, f32[256,384]{1,0:T(8,128)S(1)}, u32[]{:S(2)}, u32[]{:S(2)}) collective-permute-start(f32[256,384]{1,0:T(8,128)S(1)} %collective-permute-done.2.x0), channel_id=1, source_target_pairs={{0,4},{1,5},{4,8},{5,9},{8,12},{9,13},{12,14},{13,15},{14,10},{15,... | collective-permute-start | bytes 1179656 | tf_op jit(solution)/shard_map/ppermute | solution.py:338
  35.6 4.8 %collective-permute-done.9.x0 = f32[256,384]{1,0:T(8,128)S(1)} collective-permute-done((f32[256,384]{1,0:T(8,128)S(1)}, f32[256,384]{1,0:T(8,128)S(1)}, u32[]{:S(2)}, u32[]{:S(2)}) %collective-permute-start.9) | collective-permute-done | bytes 393248 | tf_op jit(solution)/shard_map/ppermute | solution.py:338
  40.4 2.1 %collective-permute-start.10 = (f32[256,384]{1,0:T(8,128)S(1)}, f32[256,384]{1,0:T(8,128)S(1)}, u32[]{:S(2)}, u32[]{:S(2)}) collective-permute-start(f32[256,384]{1,0:T(8,128)S(1)} %collective-permute-done.9.x0), channel_id=1, source_target_pairs={{0,4},{1,5},{4,8},{5,9},{8,12},{9,13},{12,14},{13,15},{14,10},{15,... | collective-permute-start | bytes 1179656 | tf_op jit(solution)/shard_map/ppermute | solution.py:338
  44.0 4.8 %collective-permute-done.3.x0 = f32[256,384]{1,0:T(8,128)S(1)} collective-permute-done((f32[256,384]{1,0:T(8,128)S(1)}, f32[256,384]{1,0:T(8,128)S(1)}, u32[]{:S(2)}, u32[]{:S(2)}) %collective-permute-start.3) | collective-permute-done | bytes 393248 | tf_op jit(solution)/shard_map/ppermute | solution.py:338
  48.8 2.1 %collective-permute-start.4 = (f32[256,384]{1,0:T(8,128)S(1)}, f32[256,384]{1,0:T(8,128)}, u32[]{:S(2)}, u32[]{:S(2)}) collective-permute-start(f32[256,384]{1,0:T(8,128)S(1)} %collective-permute-done.3.x0), channel_id=1, source_target_pairs={{0,4},{1,5},{4,8},{5,9},{8,12},{9,13},{12,14},{13,15},{14,10},{15,... | collective-permute-start | bytes 1179656 | tf_op jit(solution)/shard_map/ppermute | solution.py:338
  52.4 4.8 %collective-permute-done.10.x0 = f32[256,384]{1,0:T(8,128)S(1)} collective-permute-done((f32[256,384]{1,0:T(8,128)S(1)}, f32[256,384]{1,0:T(8,128)S(1)}, u32[]{:S(2)}, u32[]{:S(2)}) %collective-permute-start.10) | collective-permute-done | bytes 393248 | tf_op jit(solution)/shard_map/ppermute | solution.py:338
  57.2 2.1 %collective-permute-start.16 = (f32[256,384]{1,0:T(8,128)S(1)}, f32[256,384]{1,0:T(8,128)}, u32[]{:S(2)}, u32[]{:S(2)}) collective-permute-start(f32[256,384]{1,0:T(8,128)S(1)} %collective-permute-done.10.x0), channel_id=1, source_target_pairs={{0,4},{1,5},{4,8},{5,9},{8,12},{9,13},{12,14},{13,15},{14,10},{15,... | collective-permute-start | bytes 1179656 | tf_op jit(solution)/shard_map/ppermute | solution.py:338
  59.4 6.3 %collective-permute-done.4.x0 = f32[256,384]{1,0:T(8,128)} collective-permute-done((f32[256,384]{1,0:T(8,128)S(1)}, f32[256,384]{1,0:T(8,128)}, u32[]{:S(2)}, u32[]{:S(2)}) %collective-permute-start.4) | collective-permute-done | bytes 393248 | tf_op jit(solution)/shard_map/ppermute | solution.py:338
  65.7 2.1 %collective-permute-start.14 = (f32[256,384]{1,0:T(8,128)}, f32[256,384]{1,0:T(8,128)}, u32[]{:S(2)}, u32[]{:S(2)}) collective-permute-start(f32[256,384]{1,0:T(8,128)} %collective-permute-done.4.x0), channel_id=1, source_target_pairs={{0,4},{1,5},{4,8},{5,9},{8,12},{9,13},{12,14},{13,15},{14,10},{15,... | collective-permute-start | bytes 1179656 | tf_op jit(solution)/shard_map/ppermute | solution.py:338
  67.8 6.3 %collective-permute-done.16.x0 = f32[256,384]{1,0:T(8,128)} collective-permute-done((f32[256,384]{1,0:T(8,128)S(1)}, f32[256,384]{1,0:T(8,128)}, u32[]{:S(2)}, u32[]{:S(2)}) %collective-permute-start.16) | collective-permute-done | bytes 393248 | tf_op jit(solution)/shard_map/ppermute | solution.py:338
  74.2 2.1 %collective-permute-start.29 = (f32[256,384]{1,0:T(8,128)}, f32[256,384]{1,0:T(8,128)}, u32[]{:S(2)}, u32[]{:S(2)}) collective-permute-start(f32[256,384]{1,0:T(8,128)} %collective-permute-done.16.x0), channel_id=1, source_target_pairs={{0,4},{1,5},{4,8},{5,9},{8,12},{9,13},{12,14},{13,15},{14,10},{15,... | collective-permute-start | bytes 1179656 | tf_op jit(solution)/shard_map/ppermute | solution.py:338
  76.3 6.3 %collective-permute-done.14.x0 = f32[256,384]{1,0:T(8,128)} collective-permute-done((f32[256,384]{1,0:T(8,128)}, f32[256,384]{1,0:T(8,128)}, u32[]{:S(2)}, u32[]{:S(2)}) %collective-permute-start.14) | collective-permute-done | bytes 393248 | tf_op jit(solution)/shard_map/ppermute | solution.py:338
  82.6 2.1 %collective-permute-start.23 = (f32[256,384]{1,0:T(8,128)}, f32[256,384]{1,0:T(8,128)}, u32[]{:S(2)}, u32[]{:S(2)}) collective-permute-start(f32[256,384]{1,0:T(8,128)} %collective-permute-done.14.x0), channel_id=1, source_target_pairs={{0,4},{1,5},{4,8},{5,9},{8,12},{9,13},{12,14},{13,15},{14,10},{15,... | collective-permute-start | bytes 1179656 | tf_op jit(solution)/shard_map/ppermute | solution.py:338
  85.6 5.4 %collective-permute-done.29.x0 = f32[256,384]{1,0:T(8,128)} collective-permute-done((f32[256,384]{1,0:T(8,128)}, f32[256,384]{1,0:T(8,128)}, u32[]{:S(2)}, u32[]{:S(2)}) %collective-permute-start.29) | collective-permute-done | bytes 393248 | tf_op jit(solution)/shard_map/ppermute | solution.py:338
  91.0 2.1 %collective-permute-start.30 = (f32[256,384]{1,0:T(8,128)}, f32[256,384]{1,0:T(8,128)}, u32[]{:S(2)}, u32[]{:S(2)}) collective-permute-start(f32[256,384]{1,0:T(8,128)} %collective-permute-done.29.x0), channel_id=1, source_target_pairs={{0,4},{1,5},{4,8},{5,9},{8,12},{9,13},{12,14},{13,15},{14,10},{15,... | collective-permute-start | bytes 1179656 | tf_op jit(solution)/shard_map/ppermute | solution.py:338
  93.1 6.3 %collective-permute-done.23.x0 = f32[256,384]{1,0:T(8,128)} collective-permute-done((f32[256,384]{1,0:T(8,128)}, f32[256,384]{1,0:T(8,128)}, u32[]{:S(2)}, u32[]{:S(2)}) %collective-permute-start.23) | collective-permute-done | bytes 393248 | tf_op jit(solution)/shard_map/ppermute | solution.py:338
  99.5 2.1 %collective-permute-start.24 = (f32[256,384]{1,0:T(8,128)}, f32[256,384]{1,0:T(8,128)}, u32[]{:S(2)}, u32[]{:S(2)}) collective-permute-start(f32[256,384]{1,0:T(8,128)} %collective-permute-done.23.x0), channel_id=1, source_target_pairs={{0,4},{1,5},{4,8},{5,9},{8,12},{9,13},{12,14},{13,15},{14,10},{15,... | collective-permute-start | bytes 1179656 | tf_op jit(solution)/shard_map/ppermute | solution.py:338
  102.0 5.9 %collective-permute-done.30.x0 = f32[256,384]{1,0:T(8,128)} collective-permute-done((f32[256,384]{1,0:T(8,128)}, f32[256,384]{1,0:T(8,128)}, u32[]{:S(2)}, u32[]{:S(2)}) %collective-permute-start.30) | collective-permute-done | bytes 393248 | tf_op jit(solution)/shard_map/ppermute | solution.py:338
  107.9 2.1 %collective-permute-start.31 = (f32[256,384]{1,0:T(8,128)}, f32[256,384]{1,0:T(8,128)}, u32[]{:S(2)}, u32[]{:S(2)}) collective-permute-start(f32[256,384]{1,0:T(8,128)} %collective-permute-done.30.x0), channel_id=1, source_target_pairs={{0,4},{1,5},{4,8},{5,9},{8,12},{9,13},{12,14},{13,15},{14,10},{15,... | collective-permute-start | bytes 1179656 | tf_op jit(solution)/shard_map/ppermute | solution.py:338
  110.0 6.3 %collective-permute-done.24.x0 = f32[256,384]{1,0:T(8,128)} collective-permute-done((f32[256,384]{1,0:T(8,128)}, f32[256,384]{1,0:T(8,128)}, u32[]{:S(2)}, u32[]{:S(2)}) %collective-permute-start.24) | collective-permute-done | bytes 393248 | tf_op jit(solution)/shard_map/ppermute | solution.py:338
  116.3 2.1 %collective-permute-start.25 = (f32[256,384]{1,0:T(8,128)}, f32[256,384]{1,0:T(8,128)S(1)}, u32[]{:S(2)}, u32[]{:S(2)}) collective-permute-start(f32[256,384]{1,0:T(8,128)} %collective-permute-done.24.x0), channel_id=1, source_target_pairs={{0,4},{1,5},{4,8},{5,9},{8,12},{9,13},{12,14},{13,15},{14,10},{15,... | collective-permute-start | bytes 1179656 | tf_op jit(solution)/shard_map/ppermute | solution.py:338
  118.4 3.2 %dots.15.refs_0_ = f32[512,768]{1,0:T(8,128)S(1)} custom-call(s32[32]{0:T(128)S(1)} %add.166.blocks, f32[256,384]{1,0:T(8,128)S(1)} %get-tuple-element.14.x0.refs_1_, f32[256,384]{1,0:T(8,128)S(1)} %get-tuple-element.15.x1.refs_2_, f32[6144,384]{1,0:T(8,128)} %w_own.31, f32[6144,384]{1,0:T(8,128)} %collective-permute-done.1.w_partner), custom_call_target="tpu_custom_call" | custom-call | flops 905969664 | bytes 2359296 | tf_op jit(solution)/shard_map/dots/pallas_call | solution.py:93
  121.6 3.8 %dots.16 = (f32[512,768]{1,0:T(8,128)S(1)}, f32[512,128]{1,0:T(8,128)S(1)}) custom-call(s32[32]{0:T(128)S(1)} %add.166.blocks, f32[256,384]{1,0:T(8,128)S(1)} %get-tuple-element.29.x0.refs_3_, f32[256,384]{1,0:T(8,128)S(1)} %get-tuple-element.28.x1.refs_4_, f32[6144,384]{1,0:T(8,128)} %w_own.31, ...), custom_call_target="tpu_custom_call", output_to_operand_aliasing={{0}: (5, {})} | custom-call | flops 905969664 | bytes 2359296 | tf_op jit(solution)/shard_map/dots/pallas_call | solution.py:93
  125.5 3.3 %dots.17.refs_0_ = f32[512,768]{1,0:T(8,128)S(1)} custom-call(s32[32]{0:T(128)S(1)} %add.166.blocks, f32[256,384]{1,0:T(8,128)S(1)} %copy-done.3, f32[256,384]{1,0:T(8,128)S(1)} %copy-done.1, f32[6144,384]{1,0:T(8,128)} %w_own.31, f32[6144,384]{1,0:T(8,128)} %collective-permute-done.1.w_partner, ...), custom_call_target="tpu_custom_call", output_to_operand_aliasing={{}: (5, {})} | custom-call | flops 905969664 | bytes 2359296 | tf_op jit(solution)/shard_map/dots/pallas_call | solution.py:93
  128.9 3.3 %dots.18.refs_0_ = f32[512,768]{1,0:T(8,128)S(1)} custom-call(s32[32]{0:T(128)S(1)} %add.166.blocks, f32[256,384]{1,0:T(8,128)S(1)} %copy-done.5, f32[256,384]{1,0:T(8,128)S(1)} %copy-done.7, f32[6144,384]{1,0:T(8,128)} %w_own.31, f32[6144,384]{1,0:T(8,128)} %collective-permute-done.1.w_partner, ...), custom_call_target="tpu_custom_call", output_to_operand_aliasing={{}: (5, {})} | custom-call | flops 905969664 | bytes 2359296 | tf_op jit(solution)/shard_map/dots/pallas_call | solution.py:93
  132.3 3.3 %dots.19.refs_0_ = f32[512,768]{1,0:T(8,128)S(1)} custom-call(s32[32]{0:T(128)S(1)} %add.166.blocks, f32[256,384]{1,0:T(8,128)S(1)} %copy-done.9, f32[256,384]{1,0:T(8,128)S(1)} %copy-done.11, f32[6144,384]{1,0:T(8,128)} %w_own.31, f32[6144,384]{1,0:T(8,128)} %collective-permute-done.1.w_partner, ...), custom_call_target="tpu_custom_call", output_to_operand_aliasing={{}: (5, {})} | custom-call | flops 905969664 | bytes 2359296 | tf_op jit(solution)/shard_map/dots/pallas_call | solution.py:93
  135.6 3.3 %dots.20.refs_0_ = f32[512,768]{1,0:T(8,128)S(1)} custom-call(s32[32]{0:T(128)S(1)} %add.166.blocks, f32[256,384]{1,0:T(8,128)S(1)} %copy-done.13, f32[256,384]{1,0:T(8,128)S(1)} %copy-done.15, f32[6144,384]{1,0:T(8,128)} %w_own.31, f32[6144,384]{1,0:T(8,128)} %collective-permute-done.1.w_partner, ...), custom_call_target="tpu_custom_call", output_to_operand_aliasing={{}: (5, {})} | custom-call | flops 905969664 | bytes 2359296 | tf_op jit(solution)/shard_map/dots/pallas_call | solution.py:93
  139.0 3.8 %dots.21.refs_0_ = f32[512,768]{1,0:T(8,128)S(1)} custom-call(s32[32]{0:T(128)S(1)} %add.166.blocks, f32[256,384]{1,0:T(8,128)S(1)} %copy-done.17, f32[256,384]{1,0:T(8,128)} %collective-permute-done.13.x1, f32[6144,384]{1,0:T(8,128)} %w_own.31, f32[6144,384]{1,0:T(8,128)} %collective-permute-done.1.w_partner, ...), custom_call_target="tpu_custom_call", output_to_operand_aliasing={{}: (5, {})} | custom-call | flops 905969664 | bytes 2359296 | tf_op jit(solution)/shard_map/dots/pallas_call | solution.py:93
  142.8 4.4 %dots.22 = (f32[512,768]{1,0:T(8,128)S(1)}, f32[512,128]{1,0:T(8,128)S(1)}) custom-call(s32[32]{0:T(128)S(1)} %add.166.blocks, f32[256,384]{1,0:T(8,128)} %collective-permute-done.4.x0, f32[256,384]{1,0:T(8,128)} %collective-permute-done.7.x1, f32[6144,384]{1,0:T(8,128)} %w_own.31, ...), custom_call_target="tpu_custom_call", output_to_operand_aliasing={{0}: (5, {})} | custom-call | flops 905969664 | bytes 2359296 | tf_op jit(solution)/shard_map/dots/pallas_call | solution.py:93
  147.2 3.9 %dots.23.refs_0_ = f32[512,768]{1,0:T(8,128)S(1)} custom-call(s32[32]{0:T(128)S(1)} %add.166.blocks, f32[256,384]{1,0:T(8,128)} %collective-permute-done.16.x0, f32[256,384]{1,0:T(8,128)} %collective-permute-done.17.x1, f32[6144,384]{1,0:T(8,128)} %w_own.31, f32[6144,384]{1,0:T(8,128)} %collective-permute-done.1.w_partner, ...), custom_call_target="tpu_custom_call", output_to_operand_aliasing={{}: (5, {})} | custom-call | flops 905969664 | bytes 2359296 | tf_op jit(solution)/shard_map/dots/pallas_call | solution.py:93
  151.1 4.4 %dots.24 = (f32[512,768]{1,0:T(8,128)S(1)}, f32[512,128]{1,0:T(8,128)S(1)}) custom-call(s32[32]{0:T(128)S(1)} %add.166.blocks, f32[256,384]{1,0:T(8,128)} %collective-permute-done.14.x0, f32[256,384]{1,0:T(8,128)} %collective-permute-done.15.x1, f32[6144,384]{1,0:T(8,128)} %w_own.31, ...), custom_call_target="tpu_custom_call", output_to_operand_aliasing={{0}: (5, {})} | custom-call | flops 905969664 | bytes 2359296 | tf_op jit(solution)/shard_map/dots/pallas_call | solution.py:93
  156.0 3.9 %dots.25.refs_0_ = f32[512,768]{1,0:T(8,128)S(1)} custom-call(s32[32]{0:T(128)S(1)} %add.166.blocks, f32[256,384]{1,0:T(8,128)} %collective-permute-done.29.x0, f32[256,384]{1,0:T(8,128)} %collective-permute-done.32.x1, f32[6144,384]{1,0:T(8,128)} %w_own.31, f32[6144,384]{1,0:T(8,128)} %collective-permute-done.1.w_partner, ...), custom_call_target="tpu_custom_call", output_to_operand_aliasing={{}: (5, {})} | custom-call | flops 905969664 | bytes 2359296 | tf_op jit(solution)/shard_map/dots/pallas_call | solution.py:93
  159.9 3.9 %dots.26.refs_0_ = f32[512,768]{1,0:T(8,128)S(1)} custom-call(s32[32]{0:T(128)S(1)} %add.166.blocks, f32[256,384]{1,0:T(8,128)} %collective-permute-done.23.x0, f32[256,384]{1,0:T(8,128)} %collective-permute-done.26.x1, f32[6144,384]{1,0:T(8,128)} %w_own.31, f32[6144,384]{1,0:T(8,128)} %collective-permute-done.1.w_partner, ...), custom_call_target="tpu_custom_call", output_to_operand_aliasing={{}: (5, {})} | custom-call | flops 905969664 | bytes 2359296 | tf_op jit(solution)/shard_map/dots/pallas_call | solution.py:93
  163.8 3.9 %dots.27.refs_0_ = f32[512,768]{1,0:T(8,128)S(1)} custom-call(s32[32]{0:T(128)S(1)} %add.166.blocks, f32[256,384]{1,0:T(8,128)} %collective-permute-done.30.x0, f32[256,384]{1,0:T(8,128)} %collective-permute-done.33.x1, f32[6144,384]{1,0:T(8,128)} %w_own.31, f32[6144,384]{1,0:T(8,128)} %collective-permute-done.1.w_partner, ...), custom_call_target="tpu_custom_call", output_to_operand_aliasing={{}: (5, {})} | custom-call | flops 905969664 | bytes 2359296 | tf_op jit(solution)/shard_map/dots/pallas_call | solution.py:93
  167.7 3.9 %dots.28.refs_0_ = f32[512,768]{1,0:T(8,128)S(1)} custom-call(s32[32]{0:T(128)S(1)} %add.166.blocks, f32[256,384]{1,0:T(8,128)} %collective-permute-done.24.x0, f32[256,384]{1,0:T(8,128)} %collective-permute-done.27.x1, f32[6144,384]{1,0:T(8,128)} %w_own.31, f32[6144,384]{1,0:T(8,128)} %collective-permute-done.1.w_partner, ...), custom_call_target="tpu_custom_call", output_to_operand_aliasing={{}: (5, {})} | custom-call | flops 905969664 | bytes 2359296 | tf_op jit(solution)/shard_map/dots/pallas_call | solution.py:93
  171.9 2.0 %collective-permute-start.19 = (f32[256]{0:T(256)S(1)}, f32[256]{0:T(256)S(1)}, u32[]{:S(2)}, u32[]{:S(2)}) collective-permute-start(f32[256]{0:T(256)S(1)} %bitcast.31), channel_id=1, source_target_pairs={{0,2},{1,3},{2,0},{3,1},{4,6},{5,7},{6,4},{7,5},{8,10},{9,11},{10,... | collective-permute-start | bytes 3080 | tf_op jit(solution)/shard_map/ppermute | solution.py:332
  173.8 3.9 %dots.29.total = f32[512,768]{1,0:T(8,128)S(1)} custom-call(s32[32]{0:T(128)S(1)} %add.166.blocks, f32[256,384]{1,0:T(8,128)} %collective-permute-done.31.x0, f32[256,384]{1,0:T(8,128)} %collective-permute-done.34.x1, f32[6144,384]{1,0:T(8,128)} %w_own.31, f32[6144,384]{1,0:T(8,128)} %collective-permute-done.1.w_partner, ...), custom_call_target="tpu_custom_call", output_to_operand_aliasing={{}: (5, {})} | custom-call | flops 905969664 | bytes 2359296 | tf_op jit(solution)/shard_map/dots/pallas_call | solution.py:93
  179.5 2.6 %collective-permute-start.21 = (f32[64]{0:T(128)S(1)}, f32[64]{0:T(128)S(1)}, u32[]{:S(2)}, u32[]{:S(2)}) collective-permute-start(f32[64]{0:T(128)S(1)} %get-tuple-element.34), channel_id=1, source_target_pairs={{0,8},{1,9},{2,10},{3,11},{4,12},{5,13},{6,14},{7,15},{8,0},{9,1},... | collective-permute-start | bytes 776 | tf_op jit(solution)/shard_map/ppermute | solution.py:332
  182.3 2.3 %fetch.1.right = bf16[4,768,384]{2,1,0:T(8,128)(2,1)S(1)} custom-call(s32[32]{0:T(128)S(1)} %add.166.blocks, f32[6144,384]{1,0:T(8,128)} %w_own.31, f32[6144,384]{1,0:T(8,128)} %collective-permute-done.1.w_partner), custom_call_target="tpu_custom_call" | custom-call | flops 1179648 | bytes 5898240 | tf_op jit(solution)/shard_map/fetch/pallas_call | solution.py:131
  184.6 2.8 %collective-permute-done.22 = f32[64]{0:T(128)S(1)} collective-permute-done((f32[64]{0:T(128)S(1)}, f32[64]{0:T(128)S(1)}, u32[]{:S(2)}, u32[]{:S(2)}) %collective-permute-start.22) | collective-permute-done | bytes 288 | tf_op jit(solution)/shard_map/ppermute | solution.py:332
  189.9 2.7 %finish_own.1._ = f32[384,1024]{1,0:T(8,128)} custom-call(s32[1]{0:T(128)} %bitcast.side.core, f32[256,384]{1,0:T(8,128)S(1)} %collective-permute-done.25.x0, f32[256,384]{1,0:T(8,128)} %collective-permute-done.28.x1, bf16[4,768,384]{2,1,0:T(8,128)(2,1)S(1)} %fetch.1.right, f32[512,768]{1,0:T(8,128)S(1)} %dots.29.total), custom_call_target="tpu_custom_call" | custom-call | flops 452984832 | bytes 2359296 | tf_op jit(solution)/shard_map/finish_own/pallas_call | solution.py:196
  (109 shorter events, 13.1 us)
Async XLA Ops:
  2.8 115.6 %collective-permute-start.1 = (f32[6144,384]{1,0:T(8,128)}, f32[6144,384]{1,0:T(8,128)}, u32[]{:S(2)}, u32[]{:S(2)}) collective-permute-start(f32[6144,384]{1,0:T(8,128)} %w_own.31), channel_id=1, source_target_pairs={{0,1},{1,0},{2,3},{3,2},{4,5},{5,4},{6,7},{7,6},{8,9},{9,8},{10,11... | collective-permute-start | bytes 28311560 | tf_op jit(solution)/shard_map/ppermute | solution.py:312
  3.4 15.6 %collective-permute-start = (f32[512,384]{1,0:T(8,128)S(1)}, f32[512,384]{1,0:T(8,128)S(1)}, u32[]{:S(2)}, u32[]{:S(2)}) collective-permute-start(f32[512,384]{1,0:T(8,128)S(1)} %take.3), channel_id=1, source_target_pairs={{0,1},{1,0},{2,3},{3,2},{4,5},{5,4},{6,7},{7,6},{8,9},{9,8},{10,11... | collective-permute-start | bytes 2359304 | tf_op jit(solution)/shard_map/ppermute | solution.py:310
  3.5 98.1 %copy-start.18 = (f32[384]{0:T(512)S(1)}, f32[384]{0:T(512)}, u32[]{:S(2)}) copy-start(f32[384]{0:T(512)} %param.8) | copy-start | bytes 4612
  5.6 18.4 %collective-permute-start.11 = (f32[256,384]{1,0:T(8,128)S(1)}, f32[256,384]{1,0:T(8,128)S(1)}, u32[]{:S(2)}, u32[]{:S(2)}) collective-permute-start(f32[256,384]{1,0:T(8,128)S(1)} %get-tuple-element.15.x1.refs_2_), channel_id=1, source_target_pairs={{4,0},{5,1},{8,4},{9,5},{12,8},{13,9},{14,12},{15,13},{10,14},{11,... | collective-permute-start | bytes 1179656 | tf_op jit(solution)/shard_map/ppermute | solution.py:338
  8.6 13.4 %collective-permute-start.8 = (f32[256,384]{1,0:T(8,128)S(1)}, f32[256,384]{1,0:T(8,128)S(1)}, u32[]{:S(2)}, u32[]{:S(2)}) collective-permute-start(f32[256,384]{1,0:T(8,128)S(1)} %get-tuple-element.14.x0.refs_1_), channel_id=1, source_target_pairs={{0,4},{1,5},{4,8},{5,9},{8,12},{9,13},{12,14},{13,15},{14,10},{15,... | collective-permute-start | bytes 1179656 | tf_op jit(solution)/shard_map/ppermute | solution.py:338
  19.1 12.9 %collective-permute-start.2 = (f32[256,384]{1,0:T(8,128)S(1)}, f32[256,384]{1,0:T(8,128)S(1)}, u32[]{:S(2)}, u32[]{:S(2)}) collective-permute-start(f32[256,384]{1,0:T(8,128)S(1)} %get-tuple-element.29.x0.refs_3_), channel_id=1, source_target_pairs={{0,4},{1,5},{4,8},{5,9},{8,12},{9,13},{12,14},{13,15},{14,10},{15,... | collective-permute-start | bytes 1179656 | tf_op jit(solution)/shard_map/ppermute | solution.py:338
  22.0 12.7 %collective-permute-start.5 = (f32[256,384]{1,0:T(8,128)S(1)}, f32[256,384]{1,0:T(8,128)S(1)}, u32[]{:S(2)}, u32[]{:S(2)}) collective-permute-start(f32[256,384]{1,0:T(8,128)S(1)} %get-tuple-element.28.x1.refs_4_), channel_id=1, source_target_pairs={{4,0},{5,1},{8,4},{9,5},{12,8},{13,9},{14,12},{15,13},{10,14},{11,... | collective-permute-start | bytes 1179656 | tf_op jit(solution)/shard_map/ppermute | solution.py:338
  22.0 96.4 %copy-start.2 = (f32[256,384]{1,0:T(8,128)}, f32[256,384]{1,0:T(8,128)S(1)}, u32[]{:S(2)}) copy-start(f32[256,384]{1,0:T(8,128)S(1)} %collective-permute-done.8.x0) | copy-start | bytes 1179652
  22.1 18.3 %collective-permute-start.9 = (f32[256,384]{1,0:T(8,128)S(1)}, f32[256,384]{1,0:T(8,128)S(1)}, u32[]{:S(2)}, u32[]{:S(2)}) collective-permute-start(f32[256,384]{1,0:T(8,128)S(1)} %collective-permute-done.8.x0), channel_id=1, source_target_pairs={{0,4},{1,5},{4,8},{5,9},{8,12},{9,13},{12,14},{13,15},{14,10},{15,... | collective-permute-start | bytes 1179656 | tf_op jit(solution)/shard_map/ppermute | solution.py:338
  24.1 94.3 %copy-start = (f32[256,384]{1,0:T(8,128)}, f32[256,384]{1,0:T(8,128)S(1)}, u32[]{:S(2)}) copy-start(f32[256,384]{1,0:T(8,128)S(1)} %collective-permute-done.11.x1) | copy-start | bytes 1179652
  24.1 19.1 %collective-permute-start.12 = (f32[256,384]{1,0:T(8,128)S(1)}, f32[256,384]{1,0:T(8,128)S(1)}, u32[]{:S(2)}, u32[]{:S(2)}) collective-permute-start(f32[256,384]{1,0:T(8,128)S(1)} %collective-permute-done.11.x1), channel_id=1, source_target_pairs={{4,0},{5,1},{8,4},{9,5},{12,8},{13,9},{14,12},{15,13},{10,14},{11,... | collective-permute-start | bytes 1179656 | tf_op jit(solution)/shard_map/ppermute | solution.py:338
  31.9 16.9 %collective-permute-start.3 = (f32[256,384]{1,0:T(8,128)S(1)}, f32[256,384]{1,0:T(8,128)S(1)}, u32[]{:S(2)}, u32[]{:S(2)}) collective-permute-start(f32[256,384]{1,0:T(8,128)S(1)} %collective-permute-done.2.x0), channel_id=1, source_target_pairs={{0,4},{1,5},{4,8},{5,9},{8,12},{9,13},{12,14},{13,15},{14,10},{15,... | collective-permute-start | bytes 1179656 | tf_op jit(solution)/shard_map/ppermute | solution.py:338
  34.8 16.9 %collective-permute-start.6 = (f32[256,384]{1,0:T(8,128)S(1)}, f32[256,384]{1,0:T(8,128)S(1)}, u32[]{:S(2)}, u32[]{:S(2)}) collective-permute-start(f32[256,384]{1,0:T(8,128)S(1)} %collective-permute-done.5.x1), channel_id=1, source_target_pairs={{4,0},{5,1},{8,4},{9,5},{12,8},{13,9},{14,12},{15,13},{10,14},{11,... | collective-permute-start | bytes 1179656 | tf_op jit(solution)/shard_map/ppermute | solution.py:338
  40.4 16.9 %collective-permute-start.10 = (f32[256,384]{1,0:T(8,128)S(1)}, f32[256,384]{1,0:T(8,128)S(1)}, u32[]{:S(2)}, u32[]{:S(2)}) collective-permute-start(f32[256,384]{1,0:T(8,128)S(1)} %collective-permute-done.9.x0), channel_id=1, source_target_pairs={{0,4},{1,5},{4,8},{5,9},{8,12},{9,13},{12,14},{13,15},{14,10},{15,... | collective-permute-start | bytes 1179656 | tf_op jit(solution)/shard_map/ppermute | solution.py:338
  43.2 16.2 %collective-permute-start.13 = (f32[256,384]{1,0:T(8,128)S(1)}, f32[256,384]{1,0:T(8,128)}, u32[]{:S(2)}, u32[]{:S(2)}) collective-permute-start(f32[256,384]{1,0:T(8,128)S(1)} %collective-permute-done.12.x1), channel_id=1, source_target_pairs={{4,0},{5,1},{8,4},{9,5},{12,8},{13,9},{14,12},{15,13},{10,14},{11,... | collective-permute-start | bytes 1179656 | tf_op jit(solution)/shard_map/ppermute | solution.py:338
  48.8 17.0 %collective-permute-start.4 = (f32[256,384]{1,0:T(8,128)S(1)}, f32[256,384]{1,0:T(8,128)}, u32[]{:S(2)}, u32[]{:S(2)}) collective-permute-start(f32[256,384]{1,0:T(8,128)S(1)} %collective-permute-done.3.x0), channel_id=1, source_target_pairs={{0,4},{1,5},{4,8},{5,9},{8,12},{9,13},{12,14},{13,15},{14,10},{15,... | collective-permute-start | bytes 1179656 | tf_op jit(solution)/shard_map/ppermute | solution.py:338
  51.7 16.2 %collective-permute-start.7 = (f32[256,384]{1,0:T(8,128)S(1)}, f32[256,384]{1,0:T(8,128)}, u32[]{:S(2)}, u32[]{:S(2)}) collective-permute-start(f32[256,384]{1,0:T(8,128)S(1)} %collective-permute-done.6.x1), channel_id=1, source_target_pairs={{4,0},{5,1},{8,4},{9,5},{12,8},{13,9},{14,12},{15,13},{10,14},{11,... | collective-permute-start | bytes 1179656 | tf_op jit(solution)/shard_map/ppermute | solution.py:338
  57.2 52.8 %copy-start.16 = (f32[256,384]{1,0:T(8,128)}, f32[256,384]{1,0:T(8,128)S(1)}, u32[]{:S(2)}) copy-start(f32[256,384]{1,0:T(8,128)S(1)} %collective-permute-done.10.x0) | copy-start | bytes 1179652
  57.2 17.0 %collective-permute-start.16 = (f32[256,384]{1,0:T(8,128)S(1)}, f32[256,384]{1,0:T(8,128)}, u32[]{:S(2)}, u32[]{:S(2)}) collective-permute-start(f32[256,384]{1,0:T(8,128)S(1)} %collective-permute-done.10.x0), channel_id=1, source_target_pairs={{0,4},{1,5},{4,8},{5,9},{8,12},{9,13},{12,14},{13,15},{14,10},{15,... | collective-permute-start | bytes 1179656 | tf_op jit(solution)/shard_map/ppermute | solution.py:338
  59.4 16.9 %collective-permute-start.17 = (f32[256,384]{1,0:T(8,128)}, f32[256,384]{1,0:T(8,128)}, u32[]{:S(2)}, u32[]{:S(2)}) collective-permute-start(f32[256,384]{1,0:T(8,128)} %collective-permute-done.13.x1), channel_id=1, source_target_pairs={{4,0},{5,1},{8,4},{9,5},{12,8},{13,9},{14,12},{15,13},{10,14},{11,... | collective-permute-start | bytes 1179656 | tf_op jit(solution)/shard_map/ppermute | solution.py:338
  65.7 16.9 %collective-permute-start.14 = (f32[256,384]{1,0:T(8,128)}, f32[256,384]{1,0:T(8,128)}, u32[]{:S(2)}, u32[]{:S(2)}) collective-permute-start(f32[256,384]{1,0:T(8,128)} %collective-permute-done.4.x0), channel_id=1, source_target_pairs={{0,4},{1,5},{4,8},{5,9},{8,12},{9,13},{12,14},{13,15},{14,10},{15,... | collective-permute-start | bytes 1179656 | tf_op jit(solution)/shard_map/ppermute | solution.py:338
  67.8 16.9 %collective-permute-start.15 = (f32[256,384]{1,0:T(8,128)}, f32[256,384]{1,0:T(8,128)}, u32[]{:S(2)}, u32[]{:S(2)}) collective-permute-start(f32[256,384]{1,0:T(8,128)} %collective-permute-done.7.x1), channel_id=1, source_target_pairs={{4,0},{5,1},{8,4},{9,5},{12,8},{13,9},{14,12},{15,13},{10,14},{11,... | collective-permute-start | bytes 1179656 | tf_op jit(solution)/shard_map/ppermute | solution.py:338
  74.2 16.9 %collective-permute-start.29 = (f32[256,384]{1,0:T(8,128)}, f32[256,384]{1,0:T(8,128)}, u32[]{:S(2)}, u32[]{:S(2)}) collective-permute-start(f32[256,384]{1,0:T(8,128)} %collective-permute-done.16.x0), channel_id=1, source_target_pairs={{0,4},{1,5},{4,8},{5,9},{8,12},{9,13},{12,14},{13,15},{14,10},{15,... | collective-permute-start | bytes 1179656 | tf_op jit(solution)/shard_map/ppermute | solution.py:338
  76.3 16.9 %collective-permute-start.32 = (f32[256,384]{1,0:T(8,128)}, f32[256,384]{1,0:T(8,128)}, u32[]{:S(2)}, u32[]{:S(2)}) collective-permute-start(f32[256,384]{1,0:T(8,128)} %collective-permute-done.17.x1), channel_id=1, source_target_pairs={{4,0},{5,1},{8,4},{9,5},{12,8},{13,9},{14,12},{15,13},{10,14},{11,... | collective-permute-start | bytes 1179656 | tf_op jit(solution)/shard_map/ppermute | solution.py:338
  82.6 16.9 %collective-permute-start.23 = (f32[256,384]{1,0:T(8,128)}, f32[256,384]{1,0:T(8,128)}, u32[]{:S(2)}, u32[]{:S(2)}) collective-permute-start(f32[256,384]{1,0:T(8,128)} %collective-permute-done.14.x0), channel_id=1, source_target_pairs={{0,4},{1,5},{4,8},{5,9},{8,12},{9,13},{12,14},{13,15},{14,10},{15,... | collective-permute-start | bytes 1179656 | tf_op jit(solution)/shard_map/ppermute | solution.py:338
  84.7 16.9 %collective-permute-start.26 = (f32[256,384]{1,0:T(8,128)}, f32[256,384]{1,0:T(8,128)}, u32[]{:S(2)}, u32[]{:S(2)}) collective-permute-start(f32[256,384]{1,0:T(8,128)} %collective-permute-done.15.x1), channel_id=1, source_target_pairs={{4,0},{5,1},{8,4},{9,5},{12,8},{13,9},{14,12},{15,13},{10,14},{11,... | collective-permute-start | bytes 1179656 | tf_op jit(solution)/shard_map/ppermute | solution.py:338
  91.0 16.9 %collective-permute-start.30 = (f32[256,384]{1,0:T(8,128)}, f32[256,384]{1,0:T(8,128)}, u32[]{:S(2)}, u32[]{:S(2)}) collective-permute-start(f32[256,384]{1,0:T(8,128)} %collective-permute-done.29.x0), channel_id=1, source_target_pairs={{0,4},{1,5},{4,8},{5,9},{8,12},{9,13},{12,14},{13,15},{14,10},{15,... | collective-permute-start | bytes 1179656 | tf_op jit(solution)/shard_map/ppermute | solution.py:338
  93.1 16.9 %collective-permute-start.33 = (f32[256,384]{1,0:T(8,128)}, f32[256,384]{1,0:T(8,128)}, u32[]{:S(2)}, u32[]{:S(2)}) collective-permute-start(f32[256,384]{1,0:T(8,128)} %collective-permute-done.32.x1), channel_id=1, source_target_pairs={{4,0},{5,1},{8,4},{9,5},{12,8},{13,9},{14,12},{15,13},{10,14},{11,... | collective-permute-start | bytes 1179656 | tf_op jit(solution)/shard_map/ppermute | solution.py:338
  99.5 16.9 %collective-permute-start.24 = (f32[256,384]{1,0:T(8,128)}, f32[256,384]{1,0:T(8,128)}, u32[]{:S(2)}, u32[]{:S(2)}) collective-permute-start(f32[256,384]{1,0:T(8,128)} %collective-permute-done.23.x0), channel_id=1, source_target_pairs={{0,4},{1,5},{4,8},{5,9},{8,12},{9,13},{12,14},{13,15},{14,10},{15,... | collective-permute-start | bytes 1179656 | tf_op jit(solution)/shard_map/ppermute | solution.py:338
  101.5 16.9 %collective-permute-start.27 = (f32[256,384]{1,0:T(8,128)}, f32[256,384]{1,0:T(8,128)}, u32[]{:S(2)}, u32[]{:S(2)}) collective-permute-start(f32[256,384]{1,0:T(8,128)} %collective-permute-done.26.x1), channel_id=1, source_target_pairs={{4,0},{5,1},{8,4},{9,5},{12,8},{13,9},{14,12},{15,13},{10,14},{11,... | collective-permute-start | bytes 1179656 | tf_op jit(solution)/shard_map/ppermute | solution.py:338
  107.9 66.0 %collective-permute-start.31 = (f32[256,384]{1,0:T(8,128)}, f32[256,384]{1,0:T(8,128)}, u32[]{:S(2)}, u32[]{:S(2)}) collective-permute-start(f32[256,384]{1,0:T(8,128)} %collective-permute-done.30.x0), channel_id=1, source_target_pairs={{0,4},{1,5},{4,8},{5,9},{8,12},{9,13},{12,14},{13,15},{14,10},{15,... | collective-permute-start | bytes 1179656 | tf_op jit(solution)/shard_map/ppermute | solution.py:338
  110.0 63.9 %collective-permute-start.34 = (f32[256,384]{1,0:T(8,128)}, f32[256,384]{1,0:T(8,128)}, u32[]{:S(2)}, u32[]{:S(2)}) collective-permute-start(f32[256,384]{1,0:T(8,128)} %collective-permute-done.33.x1), channel_id=1, source_target_pairs={{4,0},{5,1},{8,4},{9,5},{12,8},{13,9},{14,12},{15,13},{10,14},{11,... | collective-permute-start | bytes 1179656 | tf_op jit(solution)/shard_map/ppermute | solution.py:338
  116.3 71.7 %collective-permute-start.25 = (f32[256,384]{1,0:T(8,128)}, f32[256,384]{1,0:T(8,128)S(1)}, u32[]{:S(2)}, u32[]{:S(2)}) collective-permute-start(f32[256,384]{1,0:T(8,128)} %collective-permute-done.24.x0), channel_id=1, source_target_pairs={{0,4},{1,5},{4,8},{5,9},{8,12},{9,13},{12,14},{13,15},{14,10},{15,... | collective-permute-start | bytes 1179656 | tf_op jit(solution)/shard_map/ppermute | solution.py:338
  118.4 69.6 %collective-permute-start.28 = (f32[256,384]{1,0:T(8,128)}, f32[256,384]{1,0:T(8,128)}, u32[]{:S(2)}, u32[]{:S(2)}) collective-permute-start(f32[256,384]{1,0:T(8,128)} %collective-permute-done.27.x1), channel_id=1, source_target_pairs={{4,0},{5,1},{8,4},{9,5},{12,8},{13,9},{14,12},{15,13},{10,14},{11,... | collective-permute-start | bytes 1179656 | tf_op jit(solution)/shard_map/ppermute | solution.py:338
  121.6 3.9 %copy-start.1 = (f32[256,384]{1,0:T(8,128)S(1)}, f32[256,384]{1,0:T(8,128)}, u32[]{:S(2)}) copy-start(f32[256,384]{1,0:T(8,128)} %copy-done) | copy-start | bytes 1179652
  121.6 3.9 %copy-start.3 = (f32[256,384]{1,0:T(8,128)S(1)}, f32[256,384]{1,0:T(8,128)}, u32[]{:S(2)}) copy-start(f32[256,384]{1,0:T(8,128)} %copy-done.2) | copy-start | bytes 1179652
  125.5 3.4 %copy-start.5 = (f32[256,384]{1,0:T(8,128)S(1)}, f32[256,384]{1,0:T(8,128)}, u32[]{:S(2)}) copy-start(f32[256,384]{1,0:T(8,128)} %copy-done.4) | copy-start | bytes 1179652
  125.5 3.4 %copy-start.7 = (f32[256,384]{1,0:T(8,128)S(1)}, f32[256,384]{1,0:T(8,128)}, u32[]{:S(2)}) copy-start(f32[256,384]{1,0:T(8,128)} %copy-done.6) | copy-start | bytes 1179652
  128.9 3.4 %copy-start.9 = (f32[256,384]{1,0:T(8,128)S(1)}, f32[256,384]{1,0:T(8,128)}, u32[]{:S(2)}) copy-start(f32[256,384]{1,0:T(8,128)} %copy-done.8) | copy-start | bytes 1179652
  128.9 3.4 %copy-start.11 = (f32[256,384]{1,0:T(8,128)S(1)}, f32[256,384]{1,0:T(8,128)}, u32[]{:S(2)}) copy-start(f32[256,384]{1,0:T(8,128)} %copy-done.10) | copy-start | bytes 1179652
  132.2 3.4 %copy-start.13 = (f32[256,384]{1,0:T(8,128)S(1)}, f32[256,384]{1,0:T(8,128)}, u32[]{:S(2)}) copy-start(f32[256,384]{1,0:T(8,128)} %copy-done.12) | copy-start | bytes 1179652
  132.3 3.4 %copy-start.15 = (f32[256,384]{1,0:T(8,128)S(1)}, f32[256,384]{1,0:T(8,128)}, u32[]{:S(2)}) copy-start(f32[256,384]{1,0:T(8,128)} %copy-done.14) | copy-start | bytes 1179652
  155.9 15.8 %collective-permute-start.18 = (f32[512]{0:T(512)S(1)}, f32[512]{0:T(512)S(1)}, u32[]{:S(2)}, u32[]{:S(2)}) collective-permute-start(f32[512]{0:T(512)S(1)} %bitcast.30), channel_id=1, source_target_pairs={{0,1},{1,0},{2,3},{3,2},{4,5},{5,4},{6,7},{7,6},{8,9},{9,8},{10,11... | collective-permute-start | bytes 6152 | tf_op jit(solution)/shard_map/ppermute | solution.py:332
  171.9 5.9 %collective-permute-start.19 = (f32[256]{0:T(256)S(1)}, f32[256]{0:T(256)S(1)}, u32[]{:S(2)}, u32[]{:S(2)}) collective-permute-start(f32[256]{0:T(256)S(1)} %bitcast.31), channel_id=1, source_target_pairs={{0,2},{1,3},{2,0},{3,1},{4,6},{5,7},{6,4},{7,5},{8,10},{9,11},{10,... | collective-permute-start | bytes 3080 | tf_op jit(solution)/shard_map/ppermute | solution.py:332
  177.9 6.7 %collective-permute-start.20 = (f32[64]{0:T(128)S(1)}, f32[64]{0:T(128)S(1)}, u32[]{:S(2)}, u32[]{:S(2)}) collective-permute-start(f32[64]{0:T(128)S(1)} %get-tuple-element.32), channel_id=1, source_target_pairs={{0,4},{1,5},{2,6},{3,7},{4,0},{5,1},{6,2},{7,3},{8,12},{9,13},{10,... | collective-permute-start | bytes 776 | tf_op jit(solution)/shard_map/ppermute | solution.py:332
  179.5 5.1 %collective-permute-start.21 = (f32[64]{0:T(128)S(1)}, f32[64]{0:T(128)S(1)}, u32[]{:S(2)}, u32[]{:S(2)}) collective-permute-start(f32[64]{0:T(128)S(1)} %get-tuple-element.34), channel_id=1, source_target_pairs={{0,8},{1,9},{2,10},{3,11},{4,12},{5,13},{6,14},{7,15},{8,0},{9,1},... | collective-permute-start | bytes 776 | tf_op jit(solution)/shard_map/ppermute | solution.py:332
  182.1 5.4 %collective-permute-start.22 = (f32[64]{0:T(128)S(1)}, f32[64]{0:T(128)S(1)}, u32[]{:S(2)}, u32[]{:S(2)}) collective-permute-start(f32[64]{0:T(128)S(1)} %get-tuple-element.33), channel_id=1, source_target_pairs={{0,12},{1,13},{2,14},{3,15},{4,8},{5,9},{6,10},{7,11},{8,4},{9,5},... | collective-permute-start | bytes 776 | tf_op jit(solution)/shard_map/ppermute | solution.py:332
  189.8 2.8 %collective-permute-start.35 = (f32[512,384]{1,0:T(8,128)S(1)}, f32[512,384]{1,0:T(8,128)S(1)}, u32[]{:S(2)}, u32[]{:S(2)}) collective-permute-start(f32[512,384]{1,0:T(8,128)S(1)} %finish.1), channel_id=1, source_target_pairs={{0,1},{1,0},{2,3},{3,2},{4,5},{5,4},{6,7},{7,6},{8,9},{9,8},{10,11... | collective-permute-start | bytes 2359304 | tf_op jit(solution)/shard_map/ppermute | solution.py:344
  (7 other events, 7.9 us)
where the time goes:
time: 195 us; the launch traced here: 194 us
  waiting for transfers between devices  78.4 us (40%)
  Pallas kernels  68.5 us (35%)
  starting transfers between devices  38.4 us (20%)
  local copies, waits for them, and re-layouts  5.48 us (3%)
    ppermute x28, waiting for transfers between devices, local(): lax.ppermute(held[c][way], 'blk', back if way else ahead)  65.3 us
    pallas_call x15, Pallas kernels, dots(): pl.pallas_call(functools.partial(dots_kernel, at, total is None, int(star...  56.4 us
    ppermute x28, starting transfers between devices, local(): lax.ppermute(held[c][way], 'blk', back if way else ahead)  31.2 us
    ppermute x1, waiting for transfers between devices, local(): given = lax.ppermute(away, 'blk', partner)  10.2 us
    ppermute x5, starting transfers between devices, exchange(): lax.ppermute(sent, 'blk', [(b, b ^ mask) for b in range(size)])  6.5 us
    unnamed x38, local copies, waits for them, and re-layouts  4.62 us
    pallas_call x2, Pallas kernels, take(): pl.pallas_call(take_kernel, out_shape=(piece,) * pieces, in_specs=[pl.Blo...  4.34 us
  transfers between devices with their start and end apart: 36, of which 14 were waited for; matrix products, arithmetic and copies ran while one was open for 1% of the time, Pallas kernels for 33%

commit v1 on v0

--- a/solution.py
+++ b/solution.py
@@ -10,6 +10,7 @@
 
 NB = 64
 OCC = 4
+PARTS = 2
 LIMIT = 20 << 20
 DOTS_LIMIT = 46 << 20
 
@@ -140,28 +141,29 @@
     )(blocks, w_own, w_partner)
 
 
-def last_part(k, way, x, right, total):
+def last_part(k, at, way, x, right, total):
     wide, rows = x.shape
     xh, xl = split(x[...])
-    at = 2 * (1 - k) + way
-    high, low = right[at, :rows], right[at, rows:]
+    block = 2 * (1 - k) + way
+    high, low = right[block, :rows], right[block, rows:]
     part = jnp.dot(
         jnp.concatenate([xh, xl, xh], 1), jnp.concatenate([high, high, low], 0), preferred_element_type=jnp.float32
     )
-    return total[way * wide : (way + 1) * wide, k * rows : (k + 1) * rows] + part
-
-
-def give_kernel(x0, x1, right, total, out):
+    top = way * total.shape[0] // 2 + at * wide
+    return total[top : top + wide, k * rows : (k + 1) * rows] + part
+
+
+def partner_kernel(at, x0, x1, right, total, out):
     wide = x0.shape[0]
     for way, x in enumerate((x0, x1)):
-        out[way * wide : (way + 1) * wide, :] = last_part(1, way, x, right, total)
-
-
-def finish_partner(pieces, right, total):
+        out[way * wide : (way + 1) * wide, :] = last_part(1, at, way, x, right, total)
+
+
+def finish_partner(at, pieces, right, total):
     wide, rows = pieces[0].shape
     vmem = pl.BlockSpec(memory_space=pltpu.VMEM)
     return pl.pallas_call(
-        give_kernel,
+        functools.partial(partner_kernel, at),
         out_shape=jax.ShapeDtypeStruct((2 * wide, rows), jnp.float32),
         in_specs=[vmem] * 4,
         out_specs=vmem,
@@ -171,67 +173,67 @@
     )(*pieces, right, total)
 
 
-def send_out(value, way, base, turned, sems, out):
+def send_out(value, half, way, at, turned, sems, out):
     wide = value.shape[0]
-    turned[way] = value.T
-    columns = pl.ds(pl.multiple_of(base + way * wide, wide), wide)
-    copy = pltpu.make_async_copy(turned.at[way], out.at[:, columns], sems.at[way])
+    turned[way, at] = value.T
+    quarter = out.shape[1] // 4
+    columns = pl.ds(pl.multiple_of((2 * half + way) * quarter + at * wide, wide), wide)
+    copy = pltpu.make_async_copy(turned.at[way, at], out.at[:, columns], sems.at[way, at])
     copy.start()
     return copy
 
 
-def own_kernel(core, x0, x1, right, total, out, turned, sems):
-    wide = x0.shape[0]
+def own_kernel(core, *refs):
+    late, right, total, out, turned, sems = refs[:-5], *refs[-5:]
     copies = [
-        send_out(last_part(0, way, x, right, total), way, core[0] * 2 * wide, turned, sems, out)
-        for way, x in enumerate((x0, x1))
+        send_out(last_part(0, i // 2, i % 2, x, right, total), core[0], i % 2, i // 2, turned, sems, out)
+        for i, x in enumerate(late)
     ]
     for copy in copies:
         copy.wait()
 
 
-def finish_own(core, pieces, right, total):
-    wide, rows = pieces[0].shape
+def finish_own(core, late, right, total):
+    wide, rows = late[0].shape
     vmem = pl.BlockSpec(memory_space=pltpu.VMEM)
     return pl.pallas_call(
         own_kernel,
-        out_shape=jax.ShapeDtypeStruct((rows, 4 * wide), jnp.float32),
-        in_specs=[pl.BlockSpec(memory_space=pltpu.SMEM)] + [vmem] * 4,
+        out_shape=jax.ShapeDtypeStruct((rows, 2 * total.shape[0]), jnp.float32),
+        in_specs=[pl.BlockSpec(memory_space=pltpu.SMEM)] + [vmem] * (len(late) + 2),
         out_specs=pl.BlockSpec(memory_space=pl.ANY),
-        scratch_shapes=[pltpu.VMEM((2, rows, wide), jnp.float32), pltpu.SemaphoreType.DMA((2,))],
-        cost_estimate=pl.CostEstimate(flops=12 * rows * rows * wide, bytes_accessed=16 * rows * rows, transcendentals=0),
+        scratch_shapes=[pltpu.VMEM((2, PARTS, rows, wide), jnp.float32), pltpu.SemaphoreType.DMA((2, PARTS))],
+        cost_estimate=pl.CostEstimate(flops=24 * rows * rows * wide, bytes_accessed=16 * rows * rows, transcendentals=0),
         compiler_params=pltpu.CompilerParams(vmem_limit_bytes=DOTS_LIMIT),
         name="finish_own",
-    )(core.reshape(1), *pieces, right, total)
-
-
-def other_kernel(core, x, _, out, turned, sems):
-    wide = turned.shape[2]
-    count = turned.shape[0]
+    )(core.reshape(1), *late, right, total)
+
+
+def place_kernel(core, *refs):
+    others, out, turned, sems = refs[:PARTS], *refs[-3:]
+    wide = turned.shape[3]
     copies = [
-        send_out(x[i * wide : (i + 1) * wide, :], i, (1 - core[0]) * count * wide, turned, sems, out)
-        for i in range(count)
+        send_out(x[way * wide : (way + 1) * wide, :], 1 - core[0], way, at, turned, sems, out)
+        for at, x in enumerate(others)
+        for way in (0, 1)
     ]
     for copy in copies:
         copy.wait()
 
 
-def place_other(core, other, out):
-    half, rows = other.shape
-    return pl.pallas_call(
-        other_kernel,
-        out_shape=jax.ShapeDtypeStruct((rows, 2 * half), jnp.float32),
-        in_specs=[
-            pl.BlockSpec(memory_space=pltpu.SMEM),
-            pl.BlockSpec(memory_space=pltpu.VMEM),
-            pl.BlockSpec(memory_space=pl.ANY),
-        ],
+def place(core, others, out):
+    both, rows = others[0].shape
+    return pl.pallas_call(
+        place_kernel,
+        out_shape=jax.ShapeDtypeStruct(out.shape, jnp.float32),
+        in_specs=[pl.BlockSpec(memory_space=pltpu.SMEM)]
+        + [pl.BlockSpec(memory_space=pltpu.VMEM)] * PARTS
+        + [pl.BlockSpec(memory_space=pl.ANY)],
         out_specs=pl.BlockSpec(memory_space=pl.ANY),
-        scratch_shapes=[pltpu.VMEM((4, rows, half // 4), jnp.float32), pltpu.SemaphoreType.DMA((4,))],
-        input_output_aliases={2: 0},
+        scratch_shapes=[pltpu.VMEM((2, PARTS, rows, both // 2), jnp.float32), pltpu.SemaphoreType.DMA((2, PARTS))],
+        input_output_aliases={1 + PARTS: 0},
         compiler_params=pltpu.CompilerParams(vmem_limit_bytes=DOTS_LIMIT),
         name="place",
-    )(core.reshape(1), other, out)
+    )(core.reshape(1), *others, out)
 
 
 def take_kernel(side, block, gmap, *refs):
@@ -294,7 +296,7 @@
     ]
 
     bits = [1 << i for i in range(size.bit_length() - 1)]
-    phases = [(bit,) for bit in bits[:-2]] + [(bits[-1], bits[-2])]
+    phases = [tuple(reversed(bits[i : i + 2])) for i in range(0, len(bits), 2)]
 
     def local(pair_elements, gmap, w_screened, coulomb):
         _, width = pair_elements.shape
@@ -334,16 +336,27 @@
 
         for step in range(n):
             for c in (0, 1):
+                if step == n - 1 and c == 1:
+                    part = wide // PARTS
+                    late, others = [], []
+                    for at in range(PARTS):
+                        late.append(
+                            [
+                                lax.ppermute(x[at * part : (at + 1) * part], "blk", back if way else ahead)
+                                for way, x in enumerate(held[c])
+                            ]
+                        )
+                    terms, *late[0] = lax.optimization_barrier((terms, *late[0]))
+                    for at, use in enumerate(late):
+                        other = finish_partner(at, use, right, total)
+                        others.append(lax.ppermute(other, "blk", partner))
+                    screened = finish_own(core, [x for use in late for x in use], right, total)
+                    screened = place(core, others, screened)
+                    break
                 if step:
                     held[c] = [lax.ppermute(held[c][way], "blk", back if way else ahead) for way in (0, 1)]
                 look = c == 1 and step in (0, n // 2 - 1, n // 2)
                 use = held[c]
-                if step == n - 1 and c == 1:
-                    terms, *use = lax.optimization_barrier((terms, *use))
-                    other = finish_partner(use, right, total)
-                    other = lax.ppermute(other, "blk", partner)
-                    screened = finish_own(core, use, right, total)
-                    break
                 total, seen = dots(blocks, 4 * step + 2 * c, use, w_screened, w_partner, total, start if look else None)
                 if step == n - 1:
                     right = fetch(blocks, 4 * step + 2, w_screened, w_partner)
@@ -358,7 +371,6 @@
                 for phase in phases:
                     terms = exchange(terms, phase, left)
                     left = [bit for bit in left if bit not in phase]
-        screened = place_other(core, other, screened)
         return screened, terms
 
     in_specs = (

time: 195 us -> 205 us (1.051)
  local copies, waits for them, and re-layouts: 5.48 us -> 10.7 us
  starting transfers between devices: 38.4 us -> 43.2 us
    ppermute x1 -> x6, starting transfers between devices: 0.07 us -> 4.26 us  [the longest x4 4.12 us: local(): lax.ppermute(x[at * part:(at + 1) * part], 'blk', back if way else ahead)]
    unnamed x38 -> x50, local copies, waits for them, and re-layouts: 4.62 us -> 8.46 us
    ppermute x1 -> x6, waiting for transfers between devices: 0.01 us -> 3.11 us  [the longest x4 3.11 us: local(): lax.ppermute(x[at * part:(at + 1) * part], 'blk', back if way else ahead)]
    ppermute x5 -> x6, starting transfers between devices: 6.5 us -> 9.12 us  [exchange(): lax.ppermute(sent, 'blk', [(b, b ^ mask) for b in range(size)])]
    ppermute x28 -> x26, starting transfers between devices: 31.2 us -> 29.2 us  [local(): lax.ppermute(held[c][way], 'blk', back if way else ahead)]
    ppermute x28 -> x26, waiting for transfers between devices: 65.3 us -> 64.4 us  [local(): lax.ppermute(held[c][way], 'blk', back if way else ahead)]
    pallas_call x3 -> x4, Pallas kernels: 5.51 us -> 5.77 us  [the longest x1 2.7 us: finish_own(): pl.pallas_call(own_kernel, out_shape=jax.ShapeDtypeStruct((rows, 2 * tota...]
  transfers between devices with their start and end apart: 36 -> 40, of which waited for: 14 -> 14; matrix products, arithmetic and copies ran while one was open for 1% -> 2% of each run, Pallas kernels for 33% -> 32%
where the time goes in v1:
time: 205 us; the launch traced here: 204 us
  waiting for transfers between devices  78.6 us (38%)
  Pallas kernels  68.8 us (34%)
  starting transfers between devices  43.2 us (21%)
  local copies, waits for them, and re-layouts  10.7 us (5%)
    ppermute x26, waiting for transfers between devices, local(): lax.ppermute(held[c][way], 'blk', back if way else ahead)  64.4 us
    pallas_call x15, Pallas kernels, dots(): pl.pallas_call(functools.partial(dots_kernel, at, total is None, int(star...  56.4 us
    ppermute x26, starting transfers between devices, local(): lax.ppermute(held[c][way], 'blk', back if way else ahead)  29.2 us
    ppermute x1, waiting for transfers between devices, local(): given = lax.ppermute(away, 'blk', partner)  10.3 us
    ppermute x6, starting transfers between devices, exchange(): lax.ppermute(sent, 'blk', [(b, b ^ mask) for b in range(size)])  9.12 us
    unnamed x50, local copies, waits for them, and re-layouts  8.46 us
    pallas_call x2, Pallas kernels, take(): pl.pallas_call(take_kernel, out_shape=(piece,) * pieces, in_specs=[pl.Blo...  4.34 us
    ppermute x4, starting transfers between devices, local(): lax.ppermute(x[at * part:(at + 1) * part], 'blk', back if way else ahead)  4.12 us
  transfers between devices with their start and end apart: 40, of which 14 were waited for; matrix products, arithmetic and copies ran while one was open for 2% of the time, Pallas kernels for 32%

profile of v1, /device:TPU:0, one launch (start us, length us, event | category | flops | bytes accessed | tf_op | source)
XLA Modules:
  0.0 204.3 jit_solution(15040151776790132412)
XLA Ops:
  0.6 2.2 %take.3 = f32[512,384]{1,0:T(8,128)S(1)} custom-call(s32[1]{0:T(128)} %bitcast.3.side, f32[384,1024]{1,0:T(8,128)} %block.3, s32[384]{0:T(512)} %gmap.3), custom_call_target="tpu_custom_call" | custom-call | flops 452984832 | bytes 1572864 | tf_op jit(solution)/shard_map/take/pallas_call | solution.py:270
  3.5 2.2 %take.2 = (f32[256,384]{1,0:T(8,128)S(1)}, f32[256,384]{1,0:T(8,128)S(1)}) custom-call(s32[1]{0:T(128)} %bitcast.side.core, f32[384,1024]{1,0:T(8,128)} %block.3, s32[384]{0:T(512)} %gmap.3), custom_call_target="tpu_custom_call" | custom-call | flops 452984832 | bytes 1572864 | tf_op jit(solution)/shard_map/take/pallas_call | solution.py:270
  5.6 3.0 %collective-permute-start.11 = (f32[256,384]{1,0:T(8,128)S(1)}, f32[256,384]{1,0:T(8,128)S(1)}, u32[]{:S(2)}, u32[]{:S(2)}) collective-permute-start(f32[256,384]{1,0:T(8,128)S(1)} %get-tuple-element.15.x1.refs_2_), channel_id=1, source_target_pairs={{4,0},{5,1},{8,4},{9,5},{12,8},{13,9},{14,12},{15,13},{10,14},{11,... | collective-permute-start | bytes 1179656 | tf_op jit(solution)/shard_map/ppermute | solution.py:357
  8.7 10.3 %collective-permute-done = f32[512,384]{1,0:T(8,128)S(1)} collective-permute-done((f32[512,384]{1,0:T(8,128)S(1)}, f32[512,384]{1,0:T(8,128)S(1)}, u32[]{:S(2)}, u32[]{:S(2)}) %collective-permute-start) | collective-permute-done | bytes 786464 | tf_op jit(solution)/shard_map/ppermute | solution.py:312
  19.1 3.0 %collective-permute-start.2 = (f32[256,384]{1,0:T(8,128)S(1)}, f32[256,384]{1,0:T(8,128)S(1)}, u32[]{:S(2)}, u32[]{:S(2)}) collective-permute-start(f32[256,384]{1,0:T(8,128)S(1)} %get-tuple-element.29.x0.refs_3_), channel_id=1, source_target_pairs={{0,4},{1,5},{4,8},{5,9},{8,12},{9,13},{12,14},{13,15},{14,10},{15,... | collective-permute-start | bytes 1179656 | tf_op jit(solution)/shard_map/ppermute | solution.py:357
  22.1 2.0 collective-permute-start.9
  24.1 7.8 %collective-permute-done.2.x0 = f32[256,384]{1,0:T(8,128)S(1)} collective-permute-done((f32[256,384]{1,0:T(8,128)S(1)}, f32[256,384]{1,0:T(8,128)S(1)}, u32[]{:S(2)}, u32[]{:S(2)}) %collective-permute-start.2) | collective-permute-done | bytes 393248 | tf_op jit(solution)/shard_map/ppermute | solution.py:357
  31.9 2.1 %collective-permute-start.3 = (f32[256,384]{1,0:T(8,128)S(1)}, f32[256,384]{1,0:T(8,128)S(1)}, u32[]{:S(2)}, u32[]{:S(2)}) collective-permute-start(f32[256,384]{1,0:T(8,128)S(1)} %collective-permute-done.2.x0), channel_id=1, source_target_pairs={{0,4},{1,5},{4,8},{5,9},{8,12},{9,13},{12,14},{13,15},{14,10},{15,... | collective-permute-start | bytes 1179656 | tf_op jit(solution)/shard_map/ppermute | solution.py:357
  35.5 4.8 %collective-permute-done.9.x0 = f32[256,384]{1,0:T(8,128)S(1)} collective-permute-done((f32[256,384]{1,0:T(8,128)S(1)}, f32[256,384]{1,0:T(8,128)S(1)}, u32[]{:S(2)}, u32[]{:S(2)}) %collective-permute-start.9) | collective-permute-done | bytes 393248 | tf_op jit(solution)/shard_map/ppermute | solution.py:357
  40.4 2.1 %collective-permute-start.10 = (f32[256,384]{1,0:T(8,128)S(1)}, f32[256,384]{1,0:T(8,128)S(1)}, u32[]{:S(2)}, u32[]{:S(2)}) collective-permute-start(f32[256,384]{1,0:T(8,128)S(1)} %collective-permute-done.9.x0), channel_id=1, source_target_pairs={{0,4},{1,5},{4,8},{5,9},{8,12},{9,13},{12,14},{13,15},{14,10},{15,... | collective-permute-start | bytes 1179656 | tf_op jit(solution)/shard_map/ppermute | solution.py:357
  44.0 4.8 %collective-permute-done.3.x0 = f32[256,384]{1,0:T(8,128)S(1)} collective-permute-done((f32[256,384]{1,0:T(8,128)S(1)}, f32[256,384]{1,0:T(8,128)S(1)}, u32[]{:S(2)}, u32[]{:S(2)}) %collective-permute-start.3) | collective-permute-done | bytes 393248 | tf_op jit(solution)/shard_map/ppermute | solution.py:357
  48.8 2.1 %collective-permute-start.4 = (f32[256,384]{1,0:T(8,128)S(1)}, f32[256,384]{1,0:T(8,128)}, u32[]{:S(2)}, u32[]{:S(2)}) collective-permute-start(f32[256,384]{1,0:T(8,128)S(1)} %collective-permute-done.3.x0), channel_id=1, source_target_pairs={{0,4},{1,5},{4,8},{5,9},{8,12},{9,13},{12,14},{13,15},{14,10},{15,... | collective-permute-start | bytes 1179656 | tf_op jit(solution)/shard_map/ppermute | solution.py:357
  52.4 4.8 %collective-permute-done.10.x0 = f32[256,384]{1,0:T(8,128)S(1)} collective-permute-done((f32[256,384]{1,0:T(8,128)S(1)}, f32[256,384]{1,0:T(8,128)S(1)}, u32[]{:S(2)}, u32[]{:S(2)}) %collective-permute-start.10) | collective-permute-done | bytes 393248 | tf_op jit(solution)/shard_map/ppermute | solution.py:357
  57.2 2.1 %collective-permute-start.16 = (f32[256,384]{1,0:T(8,128)S(1)}, f32[256,384]{1,0:T(8,128)}, u32[]{:S(2)}, u32[]{:S(2)}) collective-permute-start(f32[256,384]{1,0:T(8,128)S(1)} %collective-permute-done.10.x0), channel_id=1, source_target_pairs={{0,4},{1,5},{4,8},{5,9},{8,12},{9,13},{12,14},{13,15},{14,10},{15,... | collective-permute-start | bytes 1179656 | tf_op jit(solution)/shard_map/ppermute | solution.py:357
  60.1 5.7 %collective-permute-done.4.x0 = f32[256,384]{1,0:T(8,128)} collective-permute-done((f32[256,384]{1,0:T(8,128)S(1)}, f32[256,384]{1,0:T(8,128)}, u32[]{:S(2)}, u32[]{:S(2)}) %collective-permute-start.4) | collective-permute-done | bytes 393248 | tf_op jit(solution)/shard_map/ppermute | solution.py:357
  65.7 2.1 %collective-permute-start.14 = (f32[256,384]{1,0:T(8,128)}, f32[256,384]{1,0:T(8,128)}, u32[]{:S(2)}, u32[]{:S(2)}) collective-permute-start(f32[256,384]{1,0:T(8,128)} %collective-permute-done.4.x0), channel_id=1, source_target_pairs={{0,4},{1,5},{4,8},{5,9},{8,12},{9,13},{12,14},{13,15},{14,10},{15,... | collective-permute-start | bytes 1179656 | tf_op jit(solution)/shard_map/ppermute | solution.py:357
  67.8 6.3 %collective-permute-done.16.x0 = f32[256,384]{1,0:T(8,128)} collective-permute-done((f32[256,384]{1,0:T(8,128)S(1)}, f32[256,384]{1,0:T(8,128)}, u32[]{:S(2)}, u32[]{:S(2)}) %collective-permute-start.16) | collective-permute-done | bytes 393248 | tf_op jit(solution)/shard_map/ppermute | solution.py:357
  74.2 2.1 %collective-permute-start.30 = (f32[256,384]{1,0:T(8,128)}, f32[256,384]{1,0:T(8,128)}, u32[]{:S(2)}, u32[]{:S(2)}) collective-permute-start(f32[256,384]{1,0:T(8,128)} %collective-permute-done.16.x0), channel_id=1, source_target_pairs={{0,4},{1,5},{4,8},{5,9},{8,12},{9,13},{12,14},{13,15},{14,10},{15,... | collective-permute-start | bytes 1179656 | tf_op jit(solution)/shard_map/ppermute | solution.py:357
  76.3 6.3 %collective-permute-done.14.x0 = f32[256,384]{1,0:T(8,128)} collective-permute-done((f32[256,384]{1,0:T(8,128)}, f32[256,384]{1,0:T(8,128)}, u32[]{:S(2)}, u32[]{:S(2)}) %collective-permute-start.14) | collective-permute-done | bytes 393248 | tf_op jit(solution)/shard_map/ppermute | solution.py:357
  82.6 2.1 %collective-permute-start.24 = (f32[256,384]{1,0:T(8,128)}, f32[256,384]{1,0:T(8,128)}, u32[]{:S(2)}, u32[]{:S(2)}) collective-permute-start(f32[256,384]{1,0:T(8,128)} %collective-permute-done.14.x0), channel_id=1, source_target_pairs={{0,4},{1,5},{4,8},{5,9},{8,12},{9,13},{12,14},{13,15},{14,10},{15,... | collective-permute-start | bytes 1179656 | tf_op jit(solution)/shard_map/ppermute | solution.py:357
  85.7 5.3 %collective-permute-done.30.x0 = f32[256,384]{1,0:T(8,128)} collective-permute-done((f32[256,384]{1,0:T(8,128)}, f32[256,384]{1,0:T(8,128)}, u32[]{:S(2)}, u32[]{:S(2)}) %collective-permute-start.30) | collective-permute-done | bytes 393248 | tf_op jit(solution)/shard_map/ppermute | solution.py:357
  91.0 2.1 %collective-permute-start.31 = (f32[256,384]{1,0:T(8,128)}, f32[256,384]{1,0:T(8,128)}, u32[]{:S(2)}, u32[]{:S(2)}) collective-permute-start(f32[256,384]{1,0:T(8,128)} %collective-permute-done.30.x0), channel_id=1, source_target_pairs={{0,4},{1,5},{4,8},{5,9},{8,12},{9,13},{12,14},{13,15},{14,10},{15,... | collective-permute-start | bytes 1179656 | tf_op jit(solution)/shard_map/ppermute | solution.py:357
  93.1 6.3 %collective-permute-done.24.x0 = f32[256,384]{1,0:T(8,128)} collective-permute-done((f32[256,384]{1,0:T(8,128)}, f32[256,384]{1,0:T(8,128)}, u32[]{:S(2)}, u32[]{:S(2)}) %collective-permute-start.24) | collective-permute-done | bytes 393248 | tf_op jit(solution)/shard_map/ppermute | solution.py:357
  99.5 2.1 %collective-permute-start.25 = (f32[256,384]{1,0:T(8,128)}, f32[256,384]{1,0:T(8,128)S(1)}, u32[]{:S(2)}, u32[]{:S(2)}) collective-permute-start(f32[256,384]{1,0:T(8,128)} %collective-permute-done.24.x0), channel_id=1, source_target_pairs={{0,4},{1,5},{4,8},{5,9},{8,12},{9,13},{12,14},{13,15},{14,10},{15,... | collective-permute-start | bytes 1179656 | tf_op jit(solution)/shard_map/ppermute | solution.py:357
  102.0 5.9 %collective-permute-done.31.x0 = f32[256,384]{1,0:T(8,128)} collective-permute-done((f32[256,384]{1,0:T(8,128)}, f32[256,384]{1,0:T(8,128)}, u32[]{:S(2)}, u32[]{:S(2)}) %collective-permute-start.31) | collective-permute-done | bytes 393248 | tf_op jit(solution)/shard_map/ppermute | solution.py:357
  107.9 2.1 %collective-permute-start.32 = (f32[256,384]{1,0:T(8,128)}, f32[256,384]{1,0:T(8,128)}, u32[]{:S(2)}, u32[]{:S(2)}) collective-permute-start(f32[256,384]{1,0:T(8,128)} %collective-permute-done.31.x0), channel_id=1, source_target_pairs={{0,4},{1,5},{4,8},{5,9},{8,12},{9,13},{12,14},{13,15},{14,10},{15,... | collective-permute-start | bytes 1179656 | tf_op jit(solution)/shard_map/ppermute | solution.py:357
  110.0 6.2 %collective-permute-done.25.x0 = f32[256,384]{1,0:T(8,128)S(1)} collective-permute-done((f32[256,384]{1,0:T(8,128)}, f32[256,384]{1,0:T(8,128)S(1)}, u32[]{:S(2)}, u32[]{:S(2)}) %collective-permute-start.25) | collective-permute-done | bytes 393248 | tf_op jit(solution)/shard_map/ppermute | solution.py:357
  117.0 2.1 %collective-permute-start.26 = (f32[128,384]{1,0:T(8,128)}, f32[128,384]{1,0:T(8,128)}, u32[]{:S(2)}, u32[]{:S(2)}) collective-permute-start(f32[128,384]{1,0:T(8,128)} %get-tuple-element.33), channel_id=1, source_target_pairs={{0,4},{1,5},{4,8},{5,9},{8,12},{9,13},{12,14},{13,15},{14,10},{15,... | collective-permute-start | bytes 589832 | tf_op jit(solution)/shard_map/ppermute | solution.py:345
  119.9 3.2 %dots.15.refs_0_ = f32[512,768]{1,0:T(8,128)S(1)} custom-call(s32[32]{0:T(128)S(1)} %add.171.blocks, f32[256,384]{1,0:T(8,128)S(1)} %get-tuple-element.14.x0.refs_1_, f32[256,384]{1,0:T(8,128)S(1)} %get-tuple-element.15.x1.refs_2_, f32[6144,384]{1,0:T(8,128)} %w_own.31, f32[6144,384]{1,0:T(8,128)} %collective-permute-done.1.w_partner), custom_call_target="tpu_custom_call" | custom-call | flops 905969664 | bytes 2359296 | tf_op jit(solution)/shard_map/dots/pallas_call | solution.py:94
  123.2 3.8 %dots.16 = (f32[512,768]{1,0:T(8,128)S(1)}, f32[512,128]{1,0:T(8,128)S(1)}) custom-call(s32[32]{0:T(128)S(1)} %add.171.blocks, f32[256,384]{1,0:T(8,128)S(1)} %get-tuple-element.29.x0.refs_3_, f32[256,384]{1,0:T(8,128)S(1)} %get-tuple-element.28.x1.refs_4_, f32[6144,384]{1,0:T(8,128)} %w_own.31, ...), custom_call_target="tpu_custom_call", output_to_operand_aliasing={{0}: (5, {})} | custom-call | flops 905969664 | bytes 2359296 | tf_op jit(solution)/shard_map/dots/pallas_call | solution.py:94
  127.1 3.4 %dots.17.refs_0_ = f32[512,768]{1,0:T(8,128)S(1)} custom-call(s32[32]{0:T(128)S(1)} %add.171.blocks, f32[256,384]{1,0:T(8,128)S(1)} %copy-done.7, f32[256,384]{1,0:T(8,128)S(1)} %copy-done.5, f32[6144,384]{1,0:T(8,128)} %w_own.31, f32[6144,384]{1,0:T(8,128)} %collective-permute-done.1.w_partner, ...), custom_call_target="tpu_custom_call", output_to_operand_aliasing={{}: (5, {})} | custom-call | flops 905969664 | bytes 2359296 | tf_op jit(solution)/shard_map/dots/pallas_call | solution.py:94
  130.5 3.4 %dots.18.refs_0_ = f32[512,768]{1,0:T(8,128)S(1)} custom-call(s32[32]{0:T(128)S(1)} %add.171.blocks, f32[256,384]{1,0:T(8,128)S(1)} %copy-done.9, f32[256,384]{1,0:T(8,128)S(1)} %copy-done.11, f32[6144,384]{1,0:T(8,128)} %w_own.31, f32[6144,384]{1,0:T(8,128)} %collective-permute-done.1.w_partner, ...), custom_call_target="tpu_custom_call", output_to_operand_aliasing={{}: (5, {})} | custom-call | flops 905969664 | bytes 2359296 | tf_op jit(solution)/shard_map/dots/pallas_call | solution.py:94
  133.9 3.4 %dots.19.refs_0_ = f32[512,768]{1,0:T(8,128)S(1)} custom-call(s32[32]{0:T(128)S(1)} %add.171.blocks, f32[256,384]{1,0:T(8,128)S(1)} %copy-done.13, f32[256,384]{1,0:T(8,128)S(1)} %copy-done.15, f32[6144,384]{1,0:T(8,128)} %w_own.31, f32[6144,384]{1,0:T(8,128)} %collective-permute-done.1.w_partner, ...), custom_call_target="tpu_custom_call", output_to_operand_aliasing={{}: (5, {})} | custom-call | flops 905969664 | bytes 2359296 | tf_op jit(solution)/shard_map/dots/pallas_call | solution.py:94
  137.3 3.4 %dots.20.refs_0_ = f32[512,768]{1,0:T(8,128)S(1)} custom-call(s32[32]{0:T(128)S(1)} %add.171.blocks, f32[256,384]{1,0:T(8,128)S(1)} %copy-done.17, f32[256,384]{1,0:T(8,128)S(1)} %copy-done.19, f32[6144,384]{1,0:T(8,128)} %w_own.31, f32[6144,384]{1,0:T(8,128)} %collective-permute-done.1.w_partner, ...), custom_call_target="tpu_custom_call", output_to_operand_aliasing={{}: (5, {})} | custom-call | flops 905969664 | bytes 2359296 | tf_op jit(solution)/shard_map/dots/pallas_call | solution.py:94
  140.7 3.8 %dots.21.refs_0_ = f32[512,768]{1,0:T(8,128)S(1)} custom-call(s32[32]{0:T(128)S(1)} %add.171.blocks, f32[256,384]{1,0:T(8,128)S(1)} %copy-done.21, f32[256,384]{1,0:T(8,128)} %collective-permute-done.13.x1, f32[6144,384]{1,0:T(8,128)} %w_own.31, f32[6144,384]{1,0:T(8,128)} %collective-permute-done.1.w_partner, ...), custom_call_target="tpu_custom_call", output_to_operand_aliasing={{}: (5, {})} | custom-call | flops 905969664 | bytes 2359296 | tf_op jit(solution)/shard_map/dots/pallas_call | solution.py:94
  144.5 4.4 %dots.22 = (f32[512,768]{1,0:T(8,128)S(1)}, f32[512,128]{1,0:T(8,128)S(1)}) custom-call(s32[32]{0:T(128)S(1)} %add.171.blocks, f32[256,384]{1,0:T(8,128)} %collective-permute-done.4.x0, f32[256,384]{1,0:T(8,128)} %collective-permute-done.7.x1, f32[6144,384]{1,0:T(8,128)} %w_own.31, ...), custom_call_target="tpu_custom_call", output_to_operand_aliasing={{0}: (5, {})} | custom-call | flops 905969664 | bytes 2359296 | tf_op jit(solution)/shard_map/dots/pallas_call | solution.py:94
  148.9 4.0 %dots.23.refs_0_ = f32[512,768]{1,0:T(8,128)S(1)} custom-call(s32[32]{0:T(128)S(1)} %add.171.blocks, f32[256,384]{1,0:T(8,128)} %collective-permute-done.16.x0, f32[256,384]{1,0:T(8,128)} %collective-permute-done.17.x1, f32[6144,384]{1,0:T(8,128)} %w_own.31, f32[6144,384]{1,0:T(8,128)} %collective-permute-done.1.w_partner, ...), custom_call_target="tpu_custom_call", output_to_operand_aliasing={{}: (5, {})} | custom-call | flops 905969664 | bytes 2359296 | tf_op jit(solution)/shard_map/dots/pallas_call | solution.py:94
  152.9 4.4 %dots.24 = (f32[512,768]{1,0:T(8,128)S(1)}, f32[512,128]{1,0:T(8,128)S(1)}) custom-call(s32[32]{0:T(128)S(1)} %add.171.blocks, f32[256,384]{1,0:T(8,128)} %collective-permute-done.14.x0, f32[256,384]{1,0:T(8,128)} %collective-permute-done.15.x1, f32[6144,384]{1,0:T(8,128)} %w_own.31, ...), custom_call_target="tpu_custom_call", output_to_operand_aliasing={{0}: (5, {})} | custom-call | flops 905969664 | bytes 2359296 | tf_op jit(solution)/shard_map/dots/pallas_call | solution.py:94
  157.8 4.0 %dots.25.refs_0_ = f32[512,768]{1,0:T(8,128)S(1)} custom-call(s32[32]{0:T(128)S(1)} %add.171.blocks, f32[256,384]{1,0:T(8,128)} %collective-permute-done.30.x0, f32[256,384]{1,0:T(8,128)} %collective-permute-done.33.x1, f32[6144,384]{1,0:T(8,128)} %w_own.31, f32[6144,384]{1,0:T(8,128)} %collective-permute-done.1.w_partner, ...), custom_call_target="tpu_custom_call", output_to_operand_aliasing={{}: (5, {})} | custom-call | flops 905969664 | bytes 2359296 | tf_op jit(solution)/shard_map/dots/pallas_call | solution.py:94
  161.8 4.0 %dots.26.refs_0_ = f32[512,768]{1,0:T(8,128)S(1)} custom-call(s32[32]{0:T(128)S(1)} %add.171.blocks, f32[256,384]{1,0:T(8,128)} %collective-permute-done.24.x0, f32[256,384]{1,0:T(8,128)} %collective-permute-done.27.x1, f32[6144,384]{1,0:T(8,128)} %w_own.31, f32[6144,384]{1,0:T(8,128)} %collective-permute-done.1.w_partner, ...), custom_call_target="tpu_custom_call", output_to_operand_aliasing={{}: (5, {})} | custom-call | flops 905969664 | bytes 2359296 | tf_op jit(solution)/shard_map/dots/pallas_call | solution.py:94
  165.7 4.0 %dots.27.refs_0_ = f32[512,768]{1,0:T(8,128)S(1)} custom-call(s32[32]{0:T(128)S(1)} %add.171.blocks, f32[256,384]{1,0:T(8,128)} %collective-permute-done.31.x0, f32[256,384]{1,0:T(8,128)} %collective-permute-done.34.x1, f32[6144,384]{1,0:T(8,128)} %w_own.31, f32[6144,384]{1,0:T(8,128)} %collective-permute-done.1.w_partner, ...), custom_call_target="tpu_custom_call", output_to_operand_aliasing={{}: (5, {})} | custom-call | flops 905969664 | bytes 2359296 | tf_op jit(solution)/shard_map/dots/pallas_call | solution.py:94
  169.8 3.4 %dots.28.refs_0_ = f32[512,768]{1,0:T(8,128)S(1)} custom-call(s32[32]{0:T(128)S(1)} %add.171.blocks, f32[256,384]{1,0:T(8,128)S(1)} %collective-permute-done.25.x0, f32[256,384]{1,0:T(8,128)S(1)} %copy-done.3, f32[6144,384]{1,0:T(8,128)} %w_own.31, f32[6144,384]{1,0:T(8,128)} %collective-permute-done.1.w_partner, ...), custom_call_target="tpu_custom_call", output_to_operand_aliasing={{}: (5, {})} | custom-call | flops 905969664 | bytes 2359296 | tf_op jit(solution)/shard_map/dots/pallas_call | solution.py:94
  175.3 4.0 %dots.29.total.refs_5_ = f32[512,768]{1,0:T(8,128)S(1)} custom-call(s32[32]{0:T(128)S(1)} %add.171.blocks, f32[256,384]{1,0:T(8,128)} %collective-permute-done.32.x0, f32[256,384]{1,0:T(8,128)} %collective-permute-done.35.x1, f32[6144,384]{1,0:T(8,128)} %w_own.31, f32[6144,384]{1,0:T(8,128)} %collective-permute-done.1.w_partner, ...), custom_call_target="tpu_custom_call", output_to_operand_aliasing={{}: (5, {})} | custom-call | flops 905969664 | bytes 2359296 | tf_op jit(solution)/shard_map/dots/pallas_call | solution.py:94
  179.3 2.3 %fetch.1.right.refs_4_ = bf16[4,768,384]{2,1,0:T(8,128)(2,1)S(1)} custom-call(s32[32]{0:T(128)S(1)} %add.171.blocks, f32[6144,384]{1,0:T(8,128)} %w_own.31, f32[6144,384]{1,0:T(8,128)} %collective-permute-done.1.w_partner), custom_call_target="tpu_custom_call" | custom-call | flops 1179648 | bytes 5898240 | tf_op jit(solution)/shard_map/fetch/pallas_call | solution.py:132
  187.0 3.1 %collective-permute-done.37.x0.refs_2_ = f32[128,384]{1,0:T(8,128)S(1)} collective-permute-done((f32[128,384]{1,0:T(8,128)S(1)}, f32[128,384]{1,0:T(8,128)S(1)}, u32[]{:S(2)}, u32[]{:S(2)}) %collective-permute-start.37) | collective-permute-done | bytes 196640 | tf_op jit(solution)/shard_map/ppermute | solution.py:345
  190.1 2.8 %collective-permute-start.22 = (f32[64]{0:T(128)S(1)}, f32[64]{0:T(128)S(1)}, u32[]{:S(2)}, u32[]{:S(2)}) collective-permute-start(f32[64]{0:T(128)S(1)} %get-tuple-element.40), channel_id=1, source_target_pairs={{0,8},{1,9},{2,10},{3,11},{4,12},{5,13},{6,14},{7,15},{8,0},{9,1},... | collective-permute-start | bytes 776 | tf_op jit(solution)/shard_map/ppermute | solution.py:334
  192.9 2.3 %collective-permute-start.23 = (f32[64]{0:T(128)S(1)}, f32[64]{0:T(128)S(1)}, u32[]{:S(2)}, u32[]{:S(2)}) collective-permute-start(f32[64]{0:T(128)S(1)} %get-tuple-element.39), channel_id=1, source_target_pairs={{0,12},{1,13},{2,14},{3,15},{4,8},{5,9},{6,10},{7,11},{8,4},{9,5},... | collective-permute-start | bytes 776 | tf_op jit(solution)/shard_map/ppermute | solution.py:334
  200.4 2.7 %finish_own.1.refs_2_ = f32[384,1024]{1,0:T(8,128)} custom-call(s32[1]{0:T(128)} %bitcast.side.core, f32[128,384]{1,0:T(8,128)} %collective-permute-done.26.x0.refs_0_, f32[128,384]{1,0:T(8,128)} %collective-permute-done.29.x1.refs_1_, f32[128,384]{1,0:T(8,128)S(1)} %collective-permute-done.37.x0.refs_2_, f32[128,384]{1,0:T(8,128)S(1)} %collective-permute-done.38.x1.refs_3_, ...), custom_call_target="tpu_custom_call" | custom-call | flops 452984832 | bytes 2359296 | tf_op jit(solution)/shard_map/finish_own/pallas_call | solution.py:199
  (127 shorter events, 23.6 us)
Async XLA Ops:
  2.8 117.1 %collective-permute-start.1 = (f32[6144,384]{1,0:T(8,128)}, f32[6144,384]{1,0:T(8,128)}, u32[]{:S(2)}, u32[]{:S(2)}) collective-permute-start(f32[6144,384]{1,0:T(8,128)} %w_own.31), channel_id=1, source_target_pairs={{0,1},{1,0},{2,3},{3,2},{4,5},{5,4},{6,7},{7,6},{8,9},{9,8},{10,11... | collective-permute-start | bytes 28311560 | tf_op jit(solution)/shard_map/ppermute | solution.py:314
  3.4 15.6 %collective-permute-start = (f32[512,384]{1,0:T(8,128)S(1)}, f32[512,384]{1,0:T(8,128)S(1)}, u32[]{:S(2)}, u32[]{:S(2)}) collective-permute-start(f32[512,384]{1,0:T(8,128)S(1)} %take.3), channel_id=1, source_target_pairs={{0,1},{1,0},{2,3},{3,2},{4,5},{5,4},{6,7},{7,6},{8,9},{9,8},{10,11... | collective-permute-start | bytes 2359304 | tf_op jit(solution)/shard_map/ppermute | solution.py:312
  3.5 98.1 %copy-start.24 = (f32[384]{0:T(512)S(1)}, f32[384]{0:T(512)}, u32[]{:S(2)}) copy-start(f32[384]{0:T(512)} %param.8) | copy-start | bytes 4612
  5.6 18.4 %collective-permute-start.11 = (f32[256,384]{1,0:T(8,128)S(1)}, f32[256,384]{1,0:T(8,128)S(1)}, u32[]{:S(2)}, u32[]{:S(2)}) collective-permute-start(f32[256,384]{1,0:T(8,128)S(1)} %get-tuple-element.15.x1.refs_2_), channel_id=1, source_target_pairs={{4,0},{5,1},{8,4},{9,5},{12,8},{13,9},{14,12},{15,13},{10,14},{11,... | collective-permute-start | bytes 1179656 | tf_op jit(solution)/shard_map/ppermute | solution.py:357
  8.6 13.4 %collective-permute-start.8 = (f32[256,384]{1,0:T(8,128)S(1)}, f32[256,384]{1,0:T(8,128)S(1)}, u32[]{:S(2)}, u32[]{:S(2)}) collective-permute-start(f32[256,384]{1,0:T(8,128)S(1)} %get-tuple-element.14.x0.refs_1_), channel_id=1, source_target_pairs={{0,4},{1,5},{4,8},{5,9},{8,12},{9,13},{12,14},{13,15},{14,10},{15,... | collective-permute-start | bytes 1179656 | tf_op jit(solution)/shard_map/ppermute | solution.py:357
  19.1 12.9 %collective-permute-start.2 = (f32[256,384]{1,0:T(8,128)S(1)}, f32[256,384]{1,0:T(8,128)S(1)}, u32[]{:S(2)}, u32[]{:S(2)}) collective-permute-start(f32[256,384]{1,0:T(8,128)S(1)} %get-tuple-element.29.x0.refs_3_), channel_id=1, source_target_pairs={{0,4},{1,5},{4,8},{5,9},{8,12},{9,13},{12,14},{13,15},{14,10},{15,... | collective-permute-start | bytes 1179656 | tf_op jit(solution)/shard_map/ppermute | solution.py:357
  22.0 12.7 %collective-permute-start.5 = (f32[256,384]{1,0:T(8,128)S(1)}, f32[256,384]{1,0:T(8,128)S(1)}, u32[]{:S(2)}, u32[]{:S(2)}) collective-permute-start(f32[256,384]{1,0:T(8,128)S(1)} %get-tuple-element.28.x1.refs_4_), channel_id=1, source_target_pairs={{4,0},{5,1},{8,4},{9,5},{12,8},{13,9},{14,12},{15,13},{10,14},{11,... | collective-permute-start | bytes 1179656 | tf_op jit(solution)/shard_map/ppermute | solution.py:357
  22.0 97.8 %copy-start.6 = (f32[256,384]{1,0:T(8,128)}, f32[256,384]{1,0:T(8,128)S(1)}, u32[]{:S(2)}) copy-start(f32[256,384]{1,0:T(8,128)S(1)} %collective-permute-done.8.x0) | copy-start | bytes 1179652
  22.1 18.3 %collective-permute-start.9 = (f32[256,384]{1,0:T(8,128)S(1)}, f32[256,384]{1,0:T(8,128)S(1)}, u32[]{:S(2)}, u32[]{:S(2)}) collective-permute-start(f32[256,384]{1,0:T(8,128)S(1)} %collective-permute-done.8.x0), channel_id=1, source_target_pairs={{0,4},{1,5},{4,8},{5,9},{8,12},{9,13},{12,14},{13,15},{14,10},{15,... | collective-permute-start | bytes 1179656 | tf_op jit(solution)/shard_map/ppermute | solution.py:357
  24.1 95.8 %copy-start.4 = (f32[256,384]{1,0:T(8,128)}, f32[256,384]{1,0:T(8,128)S(1)}, u32[]{:S(2)}) copy-start(f32[256,384]{1,0:T(8,128)S(1)} %collective-permute-done.11.x1) | copy-start | bytes 1179652
  24.1 19.1 %collective-permute-start.12 = (f32[256,384]{1,0:T(8,128)S(1)}, f32[256,384]{1,0:T(8,128)S(1)}, u32[]{:S(2)}, u32[]{:S(2)}) collective-permute-start(f32[256,384]{1,0:T(8,128)S(1)} %collective-permute-done.11.x1), channel_id=1, source_target_pairs={{4,0},{5,1},{8,4},{9,5},{12,8},{13,9},{14,12},{15,13},{10,14},{11,... | collective-permute-start | bytes 1179656 | tf_op jit(solution)/shard_map/ppermute | solution.py:357
  31.9 16.9 %collective-permute-start.3 = (f32[256,384]{1,0:T(8,128)S(1)}, f32[256,384]{1,0:T(8,128)S(1)}, u32[]{:S(2)}, u32[]{:S(2)}) collective-permute-start(f32[256,384]{1,0:T(8,128)S(1)} %collective-permute-done.2.x0), channel_id=1, source_target_pairs={{0,4},{1,5},{4,8},{5,9},{8,12},{9,13},{12,14},{13,15},{14,10},{15,... | collective-permute-start | bytes 1179656 | tf_op jit(solution)/shard_map/ppermute | solution.py:357
  34.8 16.9 %collective-permute-start.6 = (f32[256,384]{1,0:T(8,128)S(1)}, f32[256,384]{1,0:T(8,128)S(1)}, u32[]{:S(2)}, u32[]{:S(2)}) collective-permute-start(f32[256,384]{1,0:T(8,128)S(1)} %collective-permute-done.5.x1), channel_id=1, source_target_pairs={{4,0},{5,1},{8,4},{9,5},{12,8},{13,9},{14,12},{15,13},{10,14},{11,... | collective-permute-start | bytes 1179656 | tf_op jit(solution)/shard_map/ppermute | solution.py:357
  40.4 16.9 %collective-permute-start.10 = (f32[256,384]{1,0:T(8,128)S(1)}, f32[256,384]{1,0:T(8,128)S(1)}, u32[]{:S(2)}, u32[]{:S(2)}) collective-permute-start(f32[256,384]{1,0:T(8,128)S(1)} %collective-permute-done.9.x0), channel_id=1, source_target_pairs={{0,4},{1,5},{4,8},{5,9},{8,12},{9,13},{12,14},{13,15},{14,10},{15,... | collective-permute-start | bytes 1179656 | tf_op jit(solution)/shard_map/ppermute | solution.py:357
  43.2 16.9 %collective-permute-start.13 = (f32[256,384]{1,0:T(8,128)S(1)}, f32[256,384]{1,0:T(8,128)}, u32[]{:S(2)}, u32[]{:S(2)}) collective-permute-start(f32[256,384]{1,0:T(8,128)S(1)} %collective-permute-done.12.x1), channel_id=1, source_target_pairs={{4,0},{5,1},{8,4},{9,5},{12,8},{13,9},{14,12},{15,13},{10,14},{11,... | collective-permute-start | bytes 1179656 | tf_op jit(solution)/shard_map/ppermute | solution.py:357
  48.8 17.0 %collective-permute-start.4 = (f32[256,384]{1,0:T(8,128)S(1)}, f32[256,384]{1,0:T(8,128)}, u32[]{:S(2)}, u32[]{:S(2)}) collective-permute-start(f32[256,384]{1,0:T(8,128)S(1)} %collective-permute-done.3.x0), channel_id=1, source_target_pairs={{0,4},{1,5},{4,8},{5,9},{8,12},{9,13},{12,14},{13,15},{14,10},{15,... | collective-permute-start | bytes 1179656 | tf_op jit(solution)/shard_map/ppermute | solution.py:357
  51.7 16.2 %collective-permute-start.7 = (f32[256,384]{1,0:T(8,128)S(1)}, f32[256,384]{1,0:T(8,128)}, u32[]{:S(2)}, u32[]{:S(2)}) collective-permute-start(f32[256,384]{1,0:T(8,128)S(1)} %collective-permute-done.6.x1), channel_id=1, source_target_pairs={{4,0},{5,1},{8,4},{9,5},{12,8},{13,9},{14,12},{15,13},{10,14},{11,... | collective-permute-start | bytes 1179656 | tf_op jit(solution)/shard_map/ppermute | solution.py:357
  57.2 17.0 %collective-permute-start.16 = (f32[256,384]{1,0:T(8,128)S(1)}, f32[256,384]{1,0:T(8,128)}, u32[]{:S(2)}, u32[]{:S(2)}) collective-permute-start(f32[256,384]{1,0:T(8,128)S(1)} %collective-permute-done.10.x0), channel_id=1, source_target_pairs={{0,4},{1,5},{4,8},{5,9},{8,12},{9,13},{12,14},{13,15},{14,10},{15,... | collective-permute-start | bytes 1179656 | tf_op jit(solution)/shard_map/ppermute | solution.py:357
  60.1 16.2 %collective-permute-start.17 = (f32[256,384]{1,0:T(8,128)}, f32[256,384]{1,0:T(8,128)}, u32[]{:S(2)}, u32[]{:S(2)}) collective-permute-start(f32[256,384]{1,0:T(8,128)} %collective-permute-done.13.x1), channel_id=1, source_target_pairs={{4,0},{5,1},{8,4},{9,5},{12,8},{13,9},{14,12},{15,13},{10,14},{11,... | collective-permute-start | bytes 1179656 | tf_op jit(solution)/shard_map/ppermute | solution.py:357
  65.7 16.9 %collective-permute-start.14 = (f32[256,384]{1,0:T(8,128)}, f32[256,384]{1,0:T(8,128)}, u32[]{:S(2)}, u32[]{:S(2)}) collective-permute-start(f32[256,384]{1,0:T(8,128)} %collective-permute-done.4.x0), channel_id=1, source_target_pairs={{0,4},{1,5},{4,8},{5,9},{8,12},{9,13},{12,14},{13,15},{14,10},{15,... | collective-permute-start | bytes 1179656 | tf_op jit(solution)/shard_map/ppermute | solution.py:357
  67.8 17.6 %collective-permute-start.15 = (f32[256,384]{1,0:T(8,128)}, f32[256,384]{1,0:T(8,128)}, u32[]{:S(2)}, u32[]{:S(2)}) collective-permute-start(f32[256,384]{1,0:T(8,128)} %collective-permute-done.7.x1), channel_id=1, source_target_pairs={{4,0},{5,1},{8,4},{9,5},{12,8},{13,9},{14,12},{15,13},{10,14},{11,... | collective-permute-start | bytes 1179656 | tf_op jit(solution)/shard_map/ppermute | solution.py:357
  74.2 16.9 %collective-permute-start.30 = (f32[256,384]{1,0:T(8,128)}, f32[256,384]{1,0:T(8,128)}, u32[]{:S(2)}, u32[]{:S(2)}) collective-permute-start(f32[256,384]{1,0:T(8,128)} %collective-permute-done.16.x0), channel_id=1, source_target_pairs={{0,4},{1,5},{4,8},{5,9},{8,12},{9,13},{12,14},{13,15},{14,10},{15,... | collective-permute-start | bytes 1179656 | tf_op jit(solution)/shard_map/ppermute | solution.py:357
  76.3 16.9 %collective-permute-start.33 = (f32[256,384]{1,0:T(8,128)}, f32[256,384]{1,0:T(8,128)}, u32[]{:S(2)}, u32[]{:S(2)}) collective-permute-start(f32[256,384]{1,0:T(8,128)} %collective-permute-done.17.x1), channel_id=1, source_target_pairs={{4,0},{5,1},{8,4},{9,5},{12,8},{13,9},{14,12},{15,13},{10,14},{11,... | collective-permute-start | bytes 1179656 | tf_op jit(solution)/shard_map/ppermute | solution.py:357
  82.6 16.9 %collective-permute-start.24 = (f32[256,384]{1,0:T(8,128)}, f32[256,384]{1,0:T(8,128)}, u32[]{:S(2)}, u32[]{:S(2)}) collective-permute-start(f32[256,384]{1,0:T(8,128)} %collective-permute-done.14.x0), channel_id=1, source_target_pairs={{0,4},{1,5},{4,8},{5,9},{8,12},{9,13},{12,14},{13,15},{14,10},{15,... | collective-permute-start | bytes 1179656 | tf_op jit(solution)/shard_map/ppermute | solution.py:357
  85.5 16.3 %collective-permute-start.27 = (f32[256,384]{1,0:T(8,128)}, f32[256,384]{1,0:T(8,128)}, u32[]{:S(2)}, u32[]{:S(2)}) collective-permute-start(f32[256,384]{1,0:T(8,128)} %collective-permute-done.15.x1), channel_id=1, source_target_pairs={{4,0},{5,1},{8,4},{9,5},{12,8},{13,9},{14,12},{15,13},{10,14},{11,... | collective-permute-start | bytes 1179656 | tf_op jit(solution)/shard_map/ppermute | solution.py:357
  91.0 16.9 %collective-permute-start.31 = (f32[256,384]{1,0:T(8,128)}, f32[256,384]{1,0:T(8,128)}, u32[]{:S(2)}, u32[]{:S(2)}) collective-permute-start(f32[256,384]{1,0:T(8,128)} %collective-permute-done.30.x0), channel_id=1, source_target_pairs={{0,4},{1,5},{4,8},{5,9},{8,12},{9,13},{12,14},{13,15},{14,10},{15,... | collective-permute-start | bytes 1179656 | tf_op jit(solution)/shard_map/ppermute | solution.py:357
  93.1 16.9 %collective-permute-start.34 = (f32[256,384]{1,0:T(8,128)}, f32[256,384]{1,0:T(8,128)}, u32[]{:S(2)}, u32[]{:S(2)}) collective-permute-start(f32[256,384]{1,0:T(8,128)} %collective-permute-done.33.x1), channel_id=1, source_target_pairs={{4,0},{5,1},{8,4},{9,5},{12,8},{13,9},{14,12},{15,13},{10,14},{11,... | collective-permute-start | bytes 1179656 | tf_op jit(solution)/shard_map/ppermute | solution.py:357
  99.5 16.7 %collective-permute-start.25 = (f32[256,384]{1,0:T(8,128)}, f32[256,384]{1,0:T(8,128)S(1)}, u32[]{:S(2)}, u32[]{:S(2)}) collective-permute-start(f32[256,384]{1,0:T(8,128)} %collective-permute-done.24.x0), channel_id=1, source_target_pairs={{0,4},{1,5},{4,8},{5,9},{8,12},{9,13},{12,14},{13,15},{14,10},{15,... | collective-permute-start | bytes 1179656 | tf_op jit(solution)/shard_map/ppermute | solution.py:357
  101.8 17.3 %collective-permute-start.28 = (f32[256,384]{1,0:T(8,128)}, f32[256,384]{1,0:T(8,128)S(1)}, u32[]{:S(2)}, u32[]{:S(2)}) collective-permute-start(f32[256,384]{1,0:T(8,128)} %collective-permute-done.27.x1), channel_id=1, source_target_pairs={{4,0},{5,1},{8,4},{9,5},{12,8},{13,9},{14,12},{15,13},{10,14},{11,... | collective-permute-start | bytes 1179656 | tf_op jit(solution)/shard_map/ppermute | solution.py:357
  107.9 65.3 %collective-permute-start.32 = (f32[256,384]{1,0:T(8,128)}, f32[256,384]{1,0:T(8,128)}, u32[]{:S(2)}, u32[]{:S(2)}) collective-permute-start(f32[256,384]{1,0:T(8,128)} %collective-permute-done.31.x0), channel_id=1, source_target_pairs={{0,4},{1,5},{4,8},{5,9},{8,12},{9,13},{12,14},{13,15},{14,10},{15,... | collective-permute-start | bytes 1179656 | tf_op jit(solution)/shard_map/ppermute | solution.py:357
  110.0 65.2 %collective-permute-start.35 = (f32[256,384]{1,0:T(8,128)}, f32[256,384]{1,0:T(8,128)}, u32[]{:S(2)}, u32[]{:S(2)}) collective-permute-start(f32[256,384]{1,0:T(8,128)} %collective-permute-done.34.x1), channel_id=1, source_target_pairs={{4,0},{5,1},{8,4},{9,5},{12,8},{13,9},{14,12},{15,13},{10,14},{11,... | collective-permute-start | bytes 1179656 | tf_op jit(solution)/shard_map/ppermute | solution.py:357
  117.0 81.8 %collective-permute-start.26 = (f32[128,384]{1,0:T(8,128)}, f32[128,384]{1,0:T(8,128)}, u32[]{:S(2)}, u32[]{:S(2)}) collective-permute-start(f32[128,384]{1,0:T(8,128)} %get-tuple-element.33), channel_id=1, source_target_pairs={{0,4},{1,5},{4,8},{5,9},{8,12},{9,13},{12,14},{13,15},{14,10},{15,... | collective-permute-start | bytes 589832 | tf_op jit(solution)/shard_map/ppermute | solution.py:345
  119.9 78.9 %collective-permute-start.29 = (f32[128,384]{1,0:T(8,128)}, f32[128,384]{1,0:T(8,128)}, u32[]{:S(2)}, u32[]{:S(2)}) collective-permute-start(f32[128,384]{1,0:T(8,128)} %get-tuple-element.31), channel_id=1, source_target_pairs={{4,0},{5,1},{8,4},{9,5},{12,8},{13,9},{14,12},{15,13},{10,14},{11,... | collective-permute-start | bytes 589832 | tf_op jit(solution)/shard_map/ppermute | solution.py:345
  123.2 3.9 %copy-start.5 = (f32[256,384]{1,0:T(8,128)S(1)}, f32[256,384]{1,0:T(8,128)}, u32[]{:S(2)}) copy-start(f32[256,384]{1,0:T(8,128)} %copy-done.4) | copy-start | bytes 1179652
  123.2 3.9 %copy-start.7 = (f32[256,384]{1,0:T(8,128)S(1)}, f32[256,384]{1,0:T(8,128)}, u32[]{:S(2)}) copy-start(f32[256,384]{1,0:T(8,128)} %copy-done.6) | copy-start | bytes 1179652
  157.7 25.3 %collective-permute-start.18 = (f32[256]{0:T(256)S(1)}, f32[256]{0:T(256)S(1)}, u32[]{:S(2)}, u32[]{:S(2)}) collective-permute-start(f32[256]{0:T(256)S(1)} %bitcast.29), channel_id=1, source_target_pairs={{0,1},{1,0},{2,3},{3,2},{4,5},{5,4},{6,7},{7,6},{8,9},{9,8},{10,11... | collective-permute-start | bytes 3080 | tf_op jit(solution)/shard_map/ppermute | solution.py:334
  165.7 4.0 %copy-start.3 = (f32[256,384]{1,0:T(8,128)S(1)}, f32[256,384]{1,0:T(8,128)}, u32[]{:S(2)}) copy-start(f32[256,384]{1,0:T(8,128)} %copy-done.2) | copy-start | bytes 1179652
  173.1 11.6 %collective-permute-start.19 = (f32[256]{0:T(256)S(1)}, f32[256]{0:T(256)S(1)}, u32[]{:S(2)}, u32[]{:S(2)}) collective-permute-start(f32[256]{0:T(256)S(1)} %bitcast.28), channel_id=1, source_target_pairs={{0,2},{1,3},{2,0},{3,1},{4,6},{5,7},{6,4},{7,5},{8,10},{9,11},{10,... | collective-permute-start | bytes 3080 | tf_op jit(solution)/shard_map/ppermute | solution.py:334
  175.2 9.9 %collective-permute-start.20 = (f32[256]{0:T(256)S(1)}, f32[256]{0:T(256)S(1)}, u32[]{:S(2)}, u32[]{:S(2)}) collective-permute-start(f32[256]{0:T(256)S(1)} %bitcast.27), channel_id=1, source_target_pairs={{0,3},{1,2},{2,1},{3,0},{4,7},{5,6},{6,5},{7,4},{8,11},{9,10},{10,... | collective-permute-start | bytes 3080 | tf_op jit(solution)/shard_map/ppermute | solution.py:334
  179.3 3.7 %copy-start.22 = (f32[128,384]{1,0:T(8,128)S(1)}, f32[128,384]{1,0:T(8,128)}, u32[]{:S(2)}) copy-start(f32[128,384]{1,0:T(8,128)} %get-tuple-element.32) | copy-start | bytes 589828
  179.3 5.4 %copy-start.23 = (f32[128,384]{1,0:T(8,128)S(1)}, f32[128,384]{1,0:T(8,128)}, u32[]{:S(2)}) copy-start(f32[128,384]{1,0:T(8,128)} %get-tuple-element.30) | copy-start | bytes 589828
  183.0 7.0 %collective-permute-start.37 = (f32[128,384]{1,0:T(8,128)S(1)}, f32[128,384]{1,0:T(8,128)S(1)}, u32[]{:S(2)}, u32[]{:S(2)}) collective-permute-start(f32[128,384]{1,0:T(8,128)S(1)} %copy-done.22), channel_id=1, source_target_pairs={{0,4},{1,5},{4,8},{5,9},{8,12},{9,13},{12,14},{13,15},{14,10},{15,... | collective-permute-start | bytes 589832 | tf_op jit(solution)/shard_map/ppermute | solution.py:345
  184.8 8.1 %collective-permute-start.38 = (f32[128,384]{1,0:T(8,128)S(1)}, f32[128,384]{1,0:T(8,128)S(1)}, u32[]{:S(2)}, u32[]{:S(2)}) collective-permute-start(f32[128,384]{1,0:T(8,128)S(1)} %copy-done.23), channel_id=1, source_target_pairs={{4,0},{5,1},{8,4},{9,5},{12,8},{13,9},{14,12},{15,13},{10,14},{11,... | collective-permute-start | bytes 589832 | tf_op jit(solution)/shard_map/ppermute | solution.py:345
  185.2 12.1 %collective-permute-start.21 = (f32[64]{0:T(128)S(1)}, f32[64]{0:T(128)S(1)}, u32[]{:S(2)}, u32[]{:S(2)}) collective-permute-start(f32[64]{0:T(128)S(1)} %get-tuple-element.38), channel_id=1, source_target_pairs={{0,4},{1,5},{2,6},{3,7},{4,0},{5,1},{6,2},{7,3},{8,12},{9,13},{10,... | collective-permute-start | bytes 776 | tf_op jit(solution)/shard_map/ppermute | solution.py:334
  190.1 7.4 %collective-permute-start.22 = (f32[64]{0:T(128)S(1)}, f32[64]{0:T(128)S(1)}, u32[]{:S(2)}, u32[]{:S(2)}) collective-permute-start(f32[64]{0:T(128)S(1)} %get-tuple-element.40), channel_id=1, source_target_pairs={{0,8},{1,9},{2,10},{3,11},{4,12},{5,13},{6,14},{7,15},{8,0},{9,1},... | collective-permute-start | bytes 776 | tf_op jit(solution)/shard_map/ppermute | solution.py:334
  192.9 5.4 %collective-permute-start.23 = (f32[64]{0:T(128)S(1)}, f32[64]{0:T(128)S(1)}, u32[]{:S(2)}, u32[]{:S(2)}) collective-permute-start(f32[64]{0:T(128)S(1)} %get-tuple-element.39), channel_id=1, source_target_pairs={{0,12},{1,13},{2,14},{3,15},{4,8},{5,9},{6,10},{7,11},{8,4},{9,5},... | collective-permute-start | bytes 776 | tf_op jit(solution)/shard_map/ppermute | solution.py:334
  197.3 5.8 %collective-permute-start.39 = (f32[256,384]{1,0:T(8,128)S(1)}, f32[256,384]{1,0:T(8,128)S(1)}, u32[]{:S(2)}, u32[]{:S(2)}) collective-permute-start(f32[256,384]{1,0:T(8,128)S(1)} %finish.3), channel_id=1, source_target_pairs={{0,1},{1,0},{2,3},{3,2},{4,5},{5,4},{6,7},{7,6},{8,9},{9,8},{10,11... | collective-permute-start | bytes 1179656 | tf_op jit(solution)/shard_map/ppermute | solution.py:352
  200.3 2.8 %collective-permute-start.36 = (f32[256,384]{1,0:T(8,128)S(1)}, f32[256,384]{1,0:T(8,128)S(1)}, u32[]{:S(2)}, u32[]{:S(2)}) collective-permute-start(f32[256,384]{1,0:T(8,128)S(1)} %finish.2), channel_id=1, source_target_pairs={{0,1},{1,0},{2,3},{3,2},{4,5},{5,4},{6,7},{7,6},{8,9},{9,8},{10,11... | collective-permute-start | bytes 1179656 | tf_op jit(solution)/shard_map/ppermute | solution.py:352
  (17 other events, 33.1 us)

commit v2 on v1

--- a/solution.py
+++ b/solution.py
@@ -38,10 +38,13 @@
     return high, (x - high.astype(jnp.float32)).astype(jnp.bfloat16)
 
 
-def dots_kernel(at, first, watch, blocks, x0, x1, w_own, w_partner, *refs):
+def dots_kernel(at, first, watch, ahead, blocks, x0, x1, w_own, w_partner, *refs):
+    if ahead:
+        fetched, fetch_sems = refs[-2:]
+        refs = refs[:-2]
     left, landed, sems = refs[-3:]
     refs = refs[:-3]
-    out = refs[-watch - 1]
+    out = refs[-watch - ahead - 1]
     rows = landed.shape[1]
     wide = x0.shape[0]
 
@@ -55,6 +58,14 @@
     for way in (0, 1):
         for copy in copies(way):
             copy.start()
+    later = []
+    if ahead:
+        for k, w in enumerate((w_partner, w_own)):
+            for way in (0, 1):
+                here = pl.ds(pl.multiple_of(blocks[at + 2 + way] * rows, rows), rows)
+                later.append(pltpu.make_async_copy(w.at[here], fetched.at[2 * k + way], fetch_sems.at[2 * k + way]))
+    for copy in later:
+        copy.start()
     for way, x in enumerate((x0, x1)):
         xh, xl = split(x[...])
         for i, part in enumerate((xh, xl, xh)):
@@ -82,8 +93,12 @@
         def _(way):
             product(way)
 
-
-def dots(blocks, at, pieces, w_own, w_partner, total=None, start=None):
+    for i, copy in enumerate(later):
+        copy.wait()
+        refs[-1][i] = jnp.concatenate(split(fetched[i]), 0)
+
+
+def dots(blocks, at, pieces, w_own, w_partner, total=None, start=None, ahead=False):
     wide, rows = pieces[0].shape
     vmem = pl.BlockSpec(memory_space=pltpu.VMEM)
     hbm = pl.BlockSpec(memory_space=pltpu.HBM)
@@ -91,15 +106,18 @@
     watch = [] if start is None else list(start)
     shape = jax.ShapeDtypeStruct((2 * wide, 2 * rows), jnp.float32)
     form = jax.ShapeDtypeStruct((2 * wide, 128), jnp.float32)
+    right = jax.ShapeDtypeStruct((4, 2 * rows, rows), jnp.bfloat16)
+    more_scratch = [pltpu.VMEM((4, rows, rows), jnp.float32), pltpu.SemaphoreType.DMA((4,))] if ahead else []
     out = pl.pallas_call(
-        functools.partial(dots_kernel, at, total is None, int(start is not None)),
-        out_shape=(shape, form) if watch else (shape,),
+        functools.partial(dots_kernel, at, total is None, int(start is not None), int(ahead)),
+        out_shape=(shape, right) if ahead else (shape, form) if watch else (shape,),
         in_specs=[pl.BlockSpec(memory_space=pltpu.SMEM), vmem, vmem, hbm, hbm] + [vmem] * (len(more) + len(watch)),
-        out_specs=(vmem, vmem)[: 2 if watch else 1],
+        out_specs=(vmem, vmem)[: 2 if watch or ahead else 1],
         scratch_shapes=[
             pltpu.VMEM((2, wide, 3 * rows), jnp.bfloat16),
             pltpu.VMEM((2, rows, 2 * rows), jnp.float32),
             pltpu.SemaphoreType.DMA((2, 2)),
+            *more_scratch,
         ],
         input_output_aliases={5: 0} if more else {},
         cost_estimate=pl.CostEstimate(
@@ -108,37 +126,7 @@
         compiler_params=pltpu.CompilerParams(vmem_limit_bytes=DOTS_LIMIT),
         name="dots",
     )(blocks, *pieces, w_own, w_partner, *more, *watch)
-    return out if watch else (out[0], None)
-
-
-def fetch_kernel(at, blocks, w_own, w_partner, out, landed, sems):
-    rows = landed.shape[1]
-    copies = []
-    for k, w in enumerate((w_partner, w_own)):
-        for way in (0, 1):
-            here = pl.ds(pl.multiple_of(blocks[at + way] * rows, rows), rows)
-            copies.append(pltpu.make_async_copy(w.at[here], landed.at[2 * k + way], sems.at[2 * k + way]))
-    for copy in copies:
-        copy.start()
-    for i, copy in enumerate(copies):
-        copy.wait()
-        high, low = split(landed[i])
-        out[i] = jnp.concatenate([high, low], 0)
-
-
-def fetch(blocks, at, w_own, w_partner):
-    rows = w_own.shape[1]
-    hbm = pl.BlockSpec(memory_space=pltpu.HBM)
-    return pl.pallas_call(
-        functools.partial(fetch_kernel, at),
-        out_shape=jax.ShapeDtypeStruct((4, 2 * rows, rows), jnp.bfloat16),
-        in_specs=[pl.BlockSpec(memory_space=pltpu.SMEM), hbm, hbm],
-        out_specs=pl.BlockSpec(memory_space=pltpu.VMEM),
-        scratch_shapes=[pltpu.VMEM((4, rows, rows), jnp.float32), pltpu.SemaphoreType.DMA((4,))],
-        cost_estimate=pl.CostEstimate(flops=8 * rows * rows, bytes_accessed=40 * rows * rows, transcendentals=0),
-        compiler_params=pltpu.CompilerParams(vmem_limit_bytes=DOTS_LIMIT),
-        name="fetch",
-    )(blocks, w_own, w_partner)
+    return out if watch or ahead else (out[0], None)
 
 
 def last_part(k, at, way, x, right, total):
@@ -247,11 +235,11 @@
     ordered = pltpu.make_async_copy(gmap, order, sems.at[2])
     for copy in (copies[0], ordered, copies[1]):
         copy.start()
-    ordered.wait()
+    for copy in (*copies, ordered):
+        copy.wait()
     pick = (lax.broadcasted_iota(jnp.int32, (rows, rows), 0) == lax.rem(order[...], rows)[None, :]).astype(jnp.bfloat16)
     pick = jnp.concatenate([pick, pick, pick], 0)
     for at in (0, 1):
-        copies[at].wait()
         x = landed[at].T
         high, rest = split(x)
         rest = x - high.astype(jnp.float32)
@@ -357,9 +345,11 @@
                     held[c] = [lax.ppermute(held[c][way], "blk", back if way else ahead) for way in (0, 1)]
                 look = c == 1 and step in (0, n // 2 - 1, n // 2)
                 use = held[c]
-                total, seen = dots(blocks, 4 * step + 2 * c, use, w_screened, w_partner, total, start if look else None)
+                total, seen = dots(
+                    blocks, 4 * step + 2 * c, use, w_screened, w_partner, total, start if look else None, step == n - 1
+                )
                 if step == n - 1:
-                    right = fetch(blocks, 4 * step + 2, w_screened, w_partner)
+                    right = seen
                 if look:
                     form = -seen if step == 0 else form + seen
             if step == n // 2:

time: 205 us -> 204 us (level)
    pallas_call x1 -> x0, Pallas kernels: 2.29 us -> none  [fetch(): pl.pallas_call(functools.partial(fetch_kernel, at), out_shape=jax.ShapeDt...]
    unnamed x50 -> x52, local copies, waits for them, and re-layouts: 8.46 us -> 8.54 us
where the time goes in v2:
time: 204 us; the launch traced here: 203 us
  waiting for transfers between devices  78.8 us (39%)
  Pallas kernels  67.1 us (33%)
  starting transfers between devices  43.1 us (21%)
  local copies, waits for them, and re-layouts  10.8 us (5%)
    ppermute x26, waiting for transfers between devices, local(): lax.ppermute(held[c][way], 'blk', back if way else ahead)  64.5 us
    pallas_call x15, Pallas kernels, dots(): pl.pallas_call(functools.partial(dots_kernel, at, total is None, int(star...  57 us
    ppermute x26, starting transfers between devices, local(): lax.ppermute(held[c][way], 'blk', back if way else ahead)  29.1 us
    ppermute x1, waiting for transfers between devices, local(): given = lax.ppermute(away, 'blk', partner)  10.4 us
    ppermute x6, starting transfers between devices, exchange(): lax.ppermute(sent, 'blk', [(b, b ^ mask) for b in range(size)])  9.11 us
    unnamed x52, local copies, waits for them, and re-layouts  8.54 us
    pallas_call x2, Pallas kernels, take(): pl.pallas_call(take_kernel, out_shape=(piece,) * pieces, in_specs=[pl.Blo...  4.12 us
    ppermute x4, starting transfers between devices, local(): lax.ppermute(x[at * part:(at + 1) * part], 'blk', back if way else ahead)  4.11 us
  transfers between devices with their start and end apart: 40, of which 14 were waited for; matrix products, arithmetic and copies ran while one was open for 2% of the time, Pallas kernels for 32%

profile of v2, /device:TPU:0, one launch (start us, length us, event | category | flops | bytes accessed | tf_op | source)
XLA Modules:
  0.0 202.8 jit_solution(839934898566747775)
XLA Ops:
  0.6 2.1 %take.3 = f32[512,384]{1,0:T(8,128)S(1)} custom-call(s32[1]{0:T(128)} %bitcast.3.side, f32[384,1024]{1,0:T(8,128)} %block.3, s32[384]{0:T(512)} %gmap.3), custom_call_target="tpu_custom_call" | custom-call | flops 452984832 | bytes 1572864 | tf_op jit(solution)/shard_map/take/pallas_call | solution.py:258
  3.4 2.1 %take.2 = (f32[256,384]{1,0:T(8,128)S(1)}, f32[256,384]{1,0:T(8,128)S(1)}) custom-call(s32[1]{0:T(128)} %bitcast.side.core, f32[384,1024]{1,0:T(8,128)} %block.3, s32[384]{0:T(512)} %gmap.3), custom_call_target="tpu_custom_call" | custom-call | flops 452984832 | bytes 1572864 | tf_op jit(solution)/shard_map/take/pallas_call | solution.py:258
  5.4 3.0 %collective-permute-start.11 = (f32[256,384]{1,0:T(8,128)S(1)}, f32[256,384]{1,0:T(8,128)S(1)}, u32[]{:S(2)}, u32[]{:S(2)}) collective-permute-start(f32[256,384]{1,0:T(8,128)S(1)} %get-tuple-element.17.x1.refs_2_), channel_id=1, source_target_pairs={{4,0},{5,1},{8,4},{9,5},{12,8},{13,9},{14,12},{15,13},{10,14},{11,... | collective-permute-start | bytes 1179656 | tf_op jit(solution)/shard_map/ppermute | solution.py:345
  8.5 10.4 %collective-permute-done = f32[512,384]{1,0:T(8,128)S(1)} collective-permute-done((f32[512,384]{1,0:T(8,128)S(1)}, f32[512,384]{1,0:T(8,128)S(1)}, u32[]{:S(2)}, u32[]{:S(2)}) %collective-permute-start) | collective-permute-done | bytes 786464 | tf_op jit(solution)/shard_map/ppermute | solution.py:300
  18.9 3.0 %collective-permute-start.2 = (f32[256,384]{1,0:T(8,128)S(1)}, f32[256,384]{1,0:T(8,128)S(1)}, u32[]{:S(2)}, u32[]{:S(2)}) collective-permute-start(f32[256,384]{1,0:T(8,128)S(1)} %get-tuple-element.33.x0.refs_3_), channel_id=1, source_target_pairs={{0,4},{1,5},{4,8},{5,9},{8,12},{9,13},{12,14},{13,15},{14,10},{15,... | collective-permute-start | bytes 1179656 | tf_op jit(solution)/shard_map/ppermute | solution.py:345
  21.9 2.0 collective-permute-start.9
  24.0 7.8 %collective-permute-done.2.x0 = f32[256,384]{1,0:T(8,128)S(1)} collective-permute-done((f32[256,384]{1,0:T(8,128)S(1)}, f32[256,384]{1,0:T(8,128)S(1)}, u32[]{:S(2)}, u32[]{:S(2)}) %collective-permute-start.2) | collective-permute-done | bytes 393248 | tf_op jit(solution)/shard_map/ppermute | solution.py:345
  31.8 2.1 %collective-permute-start.3 = (f32[256,384]{1,0:T(8,128)S(1)}, f32[256,384]{1,0:T(8,128)S(1)}, u32[]{:S(2)}, u32[]{:S(2)}) collective-permute-start(f32[256,384]{1,0:T(8,128)S(1)} %collective-permute-done.2.x0), channel_id=1, source_target_pairs={{0,4},{1,5},{4,8},{5,9},{8,12},{9,13},{12,14},{13,15},{14,10},{15,... | collective-permute-start | bytes 1179656 | tf_op jit(solution)/shard_map/ppermute | solution.py:345
  35.4 4.8 %collective-permute-done.9.x0 = f32[256,384]{1,0:T(8,128)S(1)} collective-permute-done((f32[256,384]{1,0:T(8,128)S(1)}, f32[256,384]{1,0:T(8,128)S(1)}, u32[]{:S(2)}, u32[]{:S(2)}) %collective-permute-start.9) | collective-permute-done | bytes 393248 | tf_op jit(solution)/shard_map/ppermute | solution.py:345
  40.3 2.1 %collective-permute-start.10 = (f32[256,384]{1,0:T(8,128)S(1)}, f32[256,384]{1,0:T(8,128)S(1)}, u32[]{:S(2)}, u32[]{:S(2)}) collective-permute-start(f32[256,384]{1,0:T(8,128)S(1)} %collective-permute-done.9.x0), channel_id=1, source_target_pairs={{0,4},{1,5},{4,8},{5,9},{8,12},{9,13},{12,14},{13,15},{14,10},{15,... | collective-permute-start | bytes 1179656 | tf_op jit(solution)/shard_map/ppermute | solution.py:345
  43.8 4.8 %collective-permute-done.3.x0 = f32[256,384]{1,0:T(8,128)S(1)} collective-permute-done((f32[256,384]{1,0:T(8,128)S(1)}, f32[256,384]{1,0:T(8,128)S(1)}, u32[]{:S(2)}, u32[]{:S(2)}) %collective-permute-start.3) | collective-permute-done | bytes 393248 | tf_op jit(solution)/shard_map/ppermute | solution.py:345
  48.7 2.1 %collective-permute-start.4 = (f32[256,384]{1,0:T(8,128)S(1)}, f32[256,384]{1,0:T(8,128)}, u32[]{:S(2)}, u32[]{:S(2)}) collective-permute-start(f32[256,384]{1,0:T(8,128)S(1)} %collective-permute-done.3.x0), channel_id=1, source_target_pairs={{0,4},{1,5},{4,8},{5,9},{8,12},{9,13},{12,14},{13,15},{14,10},{15,... | collective-permute-start | bytes 1179656 | tf_op jit(solution)/shard_map/ppermute | solution.py:345
  52.3 4.8 %collective-permute-done.10.x0 = f32[256,384]{1,0:T(8,128)S(1)} collective-permute-done((f32[256,384]{1,0:T(8,128)S(1)}, f32[256,384]{1,0:T(8,128)S(1)}, u32[]{:S(2)}, u32[]{:S(2)}) %collective-permute-start.10) | collective-permute-done | bytes 393248 | tf_op jit(solution)/shard_map/ppermute | solution.py:345
  57.1 2.1 %collective-permute-start.16 = (f32[256,384]{1,0:T(8,128)S(1)}, f32[256,384]{1,0:T(8,128)}, u32[]{:S(2)}, u32[]{:S(2)}) collective-permute-start(f32[256,384]{1,0:T(8,128)S(1)} %collective-permute-done.10.x0), channel_id=1, source_target_pairs={{0,4},{1,5},{4,8},{5,9},{8,12},{9,13},{12,14},{13,15},{14,10},{15,... | collective-permute-start | bytes 1179656 | tf_op jit(solution)/shard_map/ppermute | solution.py:345
  60.0 5.7 %collective-permute-done.4.x0 = f32[256,384]{1,0:T(8,128)} collective-permute-done((f32[256,384]{1,0:T(8,128)S(1)}, f32[256,384]{1,0:T(8,128)}, u32[]{:S(2)}, u32[]{:S(2)}) %collective-permute-start.4) | collective-permute-done | bytes 393248 | tf_op jit(solution)/shard_map/ppermute | solution.py:345
  65.6 2.1 %collective-permute-start.14 = (f32[256,384]{1,0:T(8,128)}, f32[256,384]{1,0:T(8,128)}, u32[]{:S(2)}, u32[]{:S(2)}) collective-permute-start(f32[256,384]{1,0:T(8,128)} %collective-permute-done.4.x0), channel_id=1, source_target_pairs={{0,4},{1,5},{4,8},{5,9},{8,12},{9,13},{12,14},{13,15},{14,10},{15,... | collective-permute-start | bytes 1179656 | tf_op jit(solution)/shard_map/ppermute | solution.py:345
  67.7 6.3 %collective-permute-done.16.x0 = f32[256,384]{1,0:T(8,128)} collective-permute-done((f32[256,384]{1,0:T(8,128)S(1)}, f32[256,384]{1,0:T(8,128)}, u32[]{:S(2)}, u32[]{:S(2)}) %collective-permute-start.16) | collective-permute-done | bytes 393248 | tf_op jit(solution)/shard_map/ppermute | solution.py:345
  74.1 2.1 %collective-permute-start.30 = (f32[256,384]{1,0:T(8,128)}, f32[256,384]{1,0:T(8,128)}, u32[]{:S(2)}, u32[]{:S(2)}) collective-permute-start(f32[256,384]{1,0:T(8,128)} %collective-permute-done.16.x0), channel_id=1, source_target_pairs={{0,4},{1,5},{4,8},{5,9},{8,12},{9,13},{12,14},{13,15},{14,10},{15,... | collective-permute-start | bytes 1179656 | tf_op jit(solution)/shard_map/ppermute | solution.py:345
  76.2 6.3 %collective-permute-done.14.x0 = f32[256,384]{1,0:T(8,128)} collective-permute-done((f32[256,384]{1,0:T(8,128)}, f32[256,384]{1,0:T(8,128)}, u32[]{:S(2)}, u32[]{:S(2)}) %collective-permute-start.14) | collective-permute-done | bytes 393248 | tf_op jit(solution)/shard_map/ppermute | solution.py:345
  82.5 2.1 %collective-permute-start.24 = (f32[256,384]{1,0:T(8,128)}, f32[256,384]{1,0:T(8,128)}, u32[]{:S(2)}, u32[]{:S(2)}) collective-permute-start(f32[256,384]{1,0:T(8,128)} %collective-permute-done.14.x0), channel_id=1, source_target_pairs={{0,4},{1,5},{4,8},{5,9},{8,12},{9,13},{12,14},{13,15},{14,10},{15,... | collective-permute-start | bytes 1179656 | tf_op jit(solution)/shard_map/ppermute | solution.py:345
  85.6 5.3 %collective-permute-done.30.x0 = f32[256,384]{1,0:T(8,128)} collective-permute-done((f32[256,384]{1,0:T(8,128)}, f32[256,384]{1,0:T(8,128)}, u32[]{:S(2)}, u32[]{:S(2)}) %collective-permute-start.30) | collective-permute-done | bytes 393248 | tf_op jit(solution)/shard_map/ppermute | solution.py:345
  90.9 2.1 %collective-permute-start.31 = (f32[256,384]{1,0:T(8,128)}, f32[256,384]{1,0:T(8,128)}, u32[]{:S(2)}, u32[]{:S(2)}) collective-permute-start(f32[256,384]{1,0:T(8,128)} %collective-permute-done.30.x0), channel_id=1, source_target_pairs={{0,4},{1,5},{4,8},{5,9},{8,12},{9,13},{12,14},{13,15},{14,10},{15,... | collective-permute-start | bytes 1179656 | tf_op jit(solution)/shard_map/ppermute | solution.py:345
  93.0 6.3 %collective-permute-done.24.x0 = f32[256,384]{1,0:T(8,128)} collective-permute-done((f32[256,384]{1,0:T(8,128)}, f32[256,384]{1,0:T(8,128)}, u32[]{:S(2)}, u32[]{:S(2)}) %collective-permute-start.24) | collective-permute-done | bytes 393248 | tf_op jit(solution)/shard_map/ppermute | solution.py:345
  99.4 2.1 %collective-permute-start.25 = (f32[256,384]{1,0:T(8,128)}, f32[256,384]{1,0:T(8,128)S(1)}, u32[]{:S(2)}, u32[]{:S(2)}) collective-permute-start(f32[256,384]{1,0:T(8,128)} %collective-permute-done.24.x0), channel_id=1, source_target_pairs={{0,4},{1,5},{4,8},{5,9},{8,12},{9,13},{12,14},{13,15},{14,10},{15,... | collective-permute-start | bytes 1179656 | tf_op jit(solution)/shard_map/ppermute | solution.py:345
  101.9 5.9 %collective-permute-done.31.x0 = f32[256,384]{1,0:T(8,128)} collective-permute-done((f32[256,384]{1,0:T(8,128)}, f32[256,384]{1,0:T(8,128)}, u32[]{:S(2)}, u32[]{:S(2)}) %collective-permute-start.31) | collective-permute-done | bytes 393248 | tf_op jit(solution)/shard_map/ppermute | solution.py:345
  107.8 2.1 %collective-permute-start.32 = (f32[256,384]{1,0:T(8,128)}, f32[256,384]{1,0:T(8,128)}, u32[]{:S(2)}, u32[]{:S(2)}) collective-permute-start(f32[256,384]{1,0:T(8,128)} %collective-permute-done.31.x0), channel_id=1, source_target_pairs={{0,4},{1,5},{4,8},{5,9},{8,12},{9,13},{12,14},{13,15},{14,10},{15,... | collective-permute-start | bytes 1179656 | tf_op jit(solution)/shard_map/ppermute | solution.py:345
  109.9 6.2 %collective-permute-done.25.x0 = f32[256,384]{1,0:T(8,128)S(1)} collective-permute-done((f32[256,384]{1,0:T(8,128)}, f32[256,384]{1,0:T(8,128)S(1)}, u32[]{:S(2)}, u32[]{:S(2)}) %collective-permute-start.25) | collective-permute-done | bytes 393248 | tf_op jit(solution)/shard_map/ppermute | solution.py:345
  116.9 2.1 %collective-permute-start.26 = (f32[128,384]{1,0:T(8,128)}, f32[128,384]{1,0:T(8,128)}, u32[]{:S(2)}, u32[]{:S(2)}) collective-permute-start(f32[128,384]{1,0:T(8,128)} %get-tuple-element.37), channel_id=1, source_target_pairs={{0,4},{1,5},{4,8},{5,9},{8,12},{9,13},{12,14},{13,15},{14,10},{15,... | collective-permute-start | bytes 589832 | tf_op jit(solution)/shard_map/ppermute | solution.py:333
  119.8 3.2 %dots.15.refs_0_ = f32[512,768]{1,0:T(8,128)S(1)} custom-call(s32[32]{0:T(128)S(1)} %add.171.blocks, f32[256,384]{1,0:T(8,128)S(1)} %get-tuple-element.16.x0.refs_1_, f32[256,384]{1,0:T(8,128)S(1)} %get-tuple-element.17.x1.refs_2_, f32[6144,384]{1,0:T(8,128)} %w_own.29, f32[6144,384]{1,0:T(8,128)} %collective-permute-done.1.w_partner), custom_call_target="tpu_custom_call" | custom-call | flops 905969664 | bytes 2359296 | tf_op jit(solution)/shard_map/dots/pallas_call | solution.py:111
  123.1 3.8 %dots.16 = (f32[512,768]{1,0:T(8,128)S(1)}, f32[512,128]{1,0:T(8,128)S(1)}) custom-call(s32[32]{0:T(128)S(1)} %add.171.blocks, f32[256,384]{1,0:T(8,128)S(1)} %get-tuple-element.33.x0.refs_3_, f32[256,384]{1,0:T(8,128)S(1)} %get-tuple-element.32.x1.refs_4_, f32[6144,384]{1,0:T(8,128)} %w_own.29, ...), custom_call_target="tpu_custom_call", output_to_operand_aliasing={{0}: (5, {})} | custom-call | flops 905969664 | bytes 2359296 | tf_op jit(solution)/shard_map/dots/pallas_call | solution.py:111
  126.9 3.4 %dots.17.refs_0_ = f32[512,768]{1,0:T(8,128)S(1)} custom-call(s32[32]{0:T(128)S(1)} %add.171.blocks, f32[256,384]{1,0:T(8,128)S(1)} %copy-done.8, f32[256,384]{1,0:T(8,128)S(1)} %copy-done.6, f32[6144,384]{1,0:T(8,128)} %w_own.29, f32[6144,384]{1,0:T(8,128)} %collective-permute-done.1.w_partner, ...), custom_call_target="tpu_custom_call", output_to_operand_aliasing={{}: (5, {})} | custom-call | flops 905969664 | bytes 2359296 | tf_op jit(solution)/shard_map/dots/pallas_call | solution.py:111
  130.4 3.4 %dots.18.refs_0_ = f32[512,768]{1,0:T(8,128)S(1)} custom-call(s32[32]{0:T(128)S(1)} %add.171.blocks, f32[256,384]{1,0:T(8,128)S(1)} %copy-done.10, f32[256,384]{1,0:T(8,128)S(1)} %copy-done.12, f32[6144,384]{1,0:T(8,128)} %w_own.29, f32[6144,384]{1,0:T(8,128)} %collective-permute-done.1.w_partner, ...), custom_call_target="tpu_custom_call", output_to_operand_aliasing={{}: (5, {})} | custom-call | flops 905969664 | bytes 2359296 | tf_op jit(solution)/shard_map/dots/pallas_call | solution.py:111
  133.8 3.4 %dots.19.refs_0_ = f32[512,768]{1,0:T(8,128)S(1)} custom-call(s32[32]{0:T(128)S(1)} %add.171.blocks, f32[256,384]{1,0:T(8,128)S(1)} %copy-done.14, f32[256,384]{1,0:T(8,128)S(1)} %copy-done.16, f32[6144,384]{1,0:T(8,128)} %w_own.29, f32[6144,384]{1,0:T(8,128)} %collective-permute-done.1.w_partner, ...), custom_call_target="tpu_custom_call", output_to_operand_aliasing={{}: (5, {})} | custom-call | flops 905969664 | bytes 2359296 | tf_op jit(solution)/shard_map/dots/pallas_call | solution.py:111
  137.2 3.4 %dots.20.refs_0_ = f32[512,768]{1,0:T(8,128)S(1)} custom-call(s32[32]{0:T(128)S(1)} %add.171.blocks, f32[256,384]{1,0:T(8,128)S(1)} %copy-done.18, f32[256,384]{1,0:T(8,128)S(1)} %copy-done.20, f32[6144,384]{1,0:T(8,128)} %w_own.29, f32[6144,384]{1,0:T(8,128)} %collective-permute-done.1.w_partner, ...), custom_call_target="tpu_custom_call", output_to_operand_aliasing={{}: (5, {})} | custom-call | flops 905969664 | bytes 2359296 | tf_op jit(solution)/shard_map/dots/pallas_call | solution.py:111
  140.6 3.8 %dots.21.refs_0_ = f32[512,768]{1,0:T(8,128)S(1)} custom-call(s32[32]{0:T(128)S(1)} %add.171.blocks, f32[256,384]{1,0:T(8,128)S(1)} %copy-done.22, f32[256,384]{1,0:T(8,128)} %collective-permute-done.13.x1, f32[6144,384]{1,0:T(8,128)} %w_own.29, f32[6144,384]{1,0:T(8,128)} %collective-permute-done.1.w_partner, ...), custom_call_target="tpu_custom_call", output_to_operand_aliasing={{}: (5, {})} | custom-call | flops 905969664 | bytes 2359296 | tf_op jit(solution)/shard_map/dots/pallas_call | solution.py:111
  144.4 4.4 %dots.22 = (f32[512,768]{1,0:T(8,128)S(1)}, f32[512,128]{1,0:T(8,128)S(1)}) custom-call(s32[32]{0:T(128)S(1)} %add.171.blocks, f32[256,384]{1,0:T(8,128)} %collective-permute-done.4.x0, f32[256,384]{1,0:T(8,128)} %collective-permute-done.7.x1, f32[6144,384]{1,0:T(8,128)} %w_own.29, ...), custom_call_target="tpu_custom_call", output_to_operand_aliasing={{0}: (5, {})} | custom-call | flops 905969664 | bytes 2359296 | tf_op jit(solution)/shard_map/dots/pallas_call | solution.py:111
  148.8 4.0 %dots.23.refs_0_ = f32[512,768]{1,0:T(8,128)S(1)} custom-call(s32[32]{0:T(128)S(1)} %add.171.blocks, f32[256,384]{1,0:T(8,128)} %collective-permute-done.16.x0, f32[256,384]{1,0:T(8,128)} %collective-permute-done.17.x1, f32[6144,384]{1,0:T(8,128)} %w_own.29, f32[6144,384]{1,0:T(8,128)} %collective-permute-done.1.w_partner, ...), custom_call_target="tpu_custom_call", output_to_operand_aliasing={{}: (5, {})} | custom-call | flops 905969664 | bytes 2359296 | tf_op jit(solution)/shard_map/dots/pallas_call | solution.py:111
  152.8 4.4 %dots.24 = (f32[512,768]{1,0:T(8,128)S(1)}, f32[512,128]{1,0:T(8,128)S(1)}) custom-call(s32[32]{0:T(128)S(1)} %add.171.blocks, f32[256,384]{1,0:T(8,128)} %collective-permute-done.14.x0, f32[256,384]{1,0:T(8,128)} %collective-permute-done.15.x1, f32[6144,384]{1,0:T(8,128)} %w_own.29, ...), custom_call_target="tpu_custom_call", output_to_operand_aliasing={{0}: (5, {})} | custom-call | flops 905969664 | bytes 2359296 | tf_op jit(solution)/shard_map/dots/pallas_call | solution.py:111
  157.7 4.0 %dots.25.refs_0_ = f32[512,768]{1,0:T(8,128)S(1)} custom-call(s32[32]{0:T(128)S(1)} %add.171.blocks, f32[256,384]{1,0:T(8,128)} %collective-permute-done.30.x0, f32[256,384]{1,0:T(8,128)} %collective-permute-done.33.x1, f32[6144,384]{1,0:T(8,128)} %w_own.29, f32[6144,384]{1,0:T(8,128)} %collective-permute-done.1.w_partner, ...), custom_call_target="tpu_custom_call", output_to_operand_aliasing={{}: (5, {})} | custom-call | flops 905969664 | bytes 2359296 | tf_op jit(solution)/shard_map/dots/pallas_call | solution.py:111
  161.6 4.0 %dots.26.refs_0_ = f32[512,768]{1,0:T(8,128)S(1)} custom-call(s32[32]{0:T(128)S(1)} %add.171.blocks, f32[256,384]{1,0:T(8,128)} %collective-permute-done.24.x0, f32[256,384]{1,0:T(8,128)} %collective-permute-done.27.x1, f32[6144,384]{1,0:T(8,128)} %w_own.29, f32[6144,384]{1,0:T(8,128)} %collective-permute-done.1.w_partner, ...), custom_call_target="tpu_custom_call", output_to_operand_aliasing={{}: (5, {})} | custom-call | flops 905969664 | bytes 2359296 | tf_op jit(solution)/shard_map/dots/pallas_call | solution.py:111
  165.6 4.0 %dots.27.refs_0_ = f32[512,768]{1,0:T(8,128)S(1)} custom-call(s32[32]{0:T(128)S(1)} %add.171.blocks, f32[256,384]{1,0:T(8,128)} %collective-permute-done.31.x0, f32[256,384]{1,0:T(8,128)} %collective-permute-done.34.x1, f32[6144,384]{1,0:T(8,128)} %w_own.29, f32[6144,384]{1,0:T(8,128)} %collective-permute-done.1.w_partner, ...), custom_call_target="tpu_custom_call", output_to_operand_aliasing={{}: (5, {})} | custom-call | flops 905969664 | bytes 2359296 | tf_op jit(solution)/shard_map/dots/pallas_call | solution.py:111
  169.6 3.4 %dots.28.refs_0_ = f32[512,768]{1,0:T(8,128)S(1)} custom-call(s32[32]{0:T(128)S(1)} %add.171.blocks, f32[256,384]{1,0:T(8,128)S(1)} %collective-permute-done.25.x0, f32[256,384]{1,0:T(8,128)S(1)} %copy-done.4, f32[6144,384]{1,0:T(8,128)} %w_own.29, f32[6144,384]{1,0:T(8,128)} %collective-permute-done.1.w_partner, ...), custom_call_target="tpu_custom_call", output_to_operand_aliasing={{}: (5, {})} | custom-call | flops 905969664 | bytes 2359296 | tf_op jit(solution)/shard_map/dots/pallas_call | solution.py:111
  173.0 2.0 collective-permute-start.19
  175.2 4.6 %dots.29 = (f32[512,768]{1,0:T(8,128)S(1)}, bf16[4,768,384]{2,1,0:T(8,128)(2,1)S(1)}) custom-call(s32[32]{0:T(128)S(1)} %add.171.blocks, f32[256,384]{1,0:T(8,128)} %collective-permute-done.32.x0, f32[256,384]{1,0:T(8,128)} %collective-permute-done.35.x1, f32[6144,384]{1,0:T(8,128)} %w_own.29, ...), custom_call_target="tpu_custom_call", output_to_operand_aliasing={{0}: (5, {})} | custom-call | flops 905969664 | bytes 2359296 | tf_op jit(solution)/shard_map/dots/pallas_call | solution.py:111
  185.2 3.1 %collective-permute-done.37.x0.refs_2_ = f32[128,384]{1,0:T(8,128)S(1)} collective-permute-done((f32[128,384]{1,0:T(8,128)S(1)}, f32[128,384]{1,0:T(8,128)S(1)}, u32[]{:S(2)}, u32[]{:S(2)}) %collective-permute-start.37) | collective-permute-done | bytes 196640 | tf_op jit(solution)/shard_map/ppermute | solution.py:333
  188.3 2.8 %collective-permute-start.22 = (f32[64]{0:T(128)S(1)}, f32[64]{0:T(128)S(1)}, u32[]{:S(2)}, u32[]{:S(2)}) collective-permute-start(f32[64]{0:T(128)S(1)} %get-tuple-element.44), channel_id=1, source_target_pairs={{0,8},{1,9},{2,10},{3,11},{4,12},{5,13},{6,14},{7,15},{8,0},{9,1},... | collective-permute-start | bytes 776 | tf_op jit(solution)/shard_map/ppermute | solution.py:322
  191.1 2.3 %collective-permute-start.23 = (f32[64]{0:T(128)S(1)}, f32[64]{0:T(128)S(1)}, u32[]{:S(2)}, u32[]{:S(2)}) collective-permute-start(f32[64]{0:T(128)S(1)} %get-tuple-element.43), channel_id=1, source_target_pairs={{0,12},{1,13},{2,14},{3,15},{4,8},{5,9},{6,10},{7,11},{8,4},{9,5},... | collective-permute-start | bytes 776 | tf_op jit(solution)/shard_map/ppermute | solution.py:322
  198.8 2.7 %finish_own.1.refs_2_ = f32[384,1024]{1,0:T(8,128)} custom-call(s32[1]{0:T(128)} %bitcast.side.core, f32[128,384]{1,0:T(8,128)} %collective-permute-done.26.x0.refs_0_, f32[128,384]{1,0:T(8,128)} %collective-permute-done.29.x1.refs_1_, f32[128,384]{1,0:T(8,128)S(1)} %collective-permute-done.37.x0.refs_2_, f32[128,384]{1,0:T(8,128)S(1)} %collective-permute-done.38.x1.refs_3_, ...), custom_call_target="tpu_custom_call" | custom-call | flops 452984832 | bytes 2359296 | tf_op jit(solution)/shard_map/finish_own/pallas_call | solution.py:187
  (128 shorter events, 21.8 us)
Async XLA Ops:
  2.7 117.1 %collective-permute-start.1 = (f32[6144,384]{1,0:T(8,128)}, f32[6144,384]{1,0:T(8,128)}, u32[]{:S(2)}, u32[]{:S(2)}) collective-permute-start(f32[6144,384]{1,0:T(8,128)} %w_own.29), channel_id=1, source_target_pairs={{0,1},{1,0},{2,3},{3,2},{4,5},{5,4},{6,7},{7,6},{8,9},{9,8},{10,11... | collective-permute-start | bytes 28311560 | tf_op jit(solution)/shard_map/ppermute | solution.py:302
  3.3 15.6 %collective-permute-start = (f32[512,384]{1,0:T(8,128)S(1)}, f32[512,384]{1,0:T(8,128)S(1)}, u32[]{:S(2)}, u32[]{:S(2)}) collective-permute-start(f32[512,384]{1,0:T(8,128)S(1)} %take.3), channel_id=1, source_target_pairs={{0,1},{1,0},{2,3},{3,2},{4,5},{5,4},{6,7},{7,6},{8,9},{9,8},{10,11... | collective-permute-start | bytes 2359304 | tf_op jit(solution)/shard_map/ppermute | solution.py:300
  3.3 98.1 %copy-start.25 = (f32[384]{0:T(512)S(1)}, f32[384]{0:T(512)}, u32[]{:S(2)}) copy-start(f32[384]{0:T(512)} %param.8) | copy-start | bytes 4612
  5.4 18.5 %collective-permute-start.11 = (f32[256,384]{1,0:T(8,128)S(1)}, f32[256,384]{1,0:T(8,128)S(1)}, u32[]{:S(2)}, u32[]{:S(2)}) collective-permute-start(f32[256,384]{1,0:T(8,128)S(1)} %get-tuple-element.17.x1.refs_2_), channel_id=1, source_target_pairs={{4,0},{5,1},{8,4},{9,5},{12,8},{13,9},{14,12},{15,13},{10,14},{11,... | collective-permute-start | bytes 1179656 | tf_op jit(solution)/shard_map/ppermute | solution.py:345
  8.4 13.5 %collective-permute-start.8 = (f32[256,384]{1,0:T(8,128)S(1)}, f32[256,384]{1,0:T(8,128)S(1)}, u32[]{:S(2)}, u32[]{:S(2)}) collective-permute-start(f32[256,384]{1,0:T(8,128)S(1)} %get-tuple-element.16.x0.refs_1_), channel_id=1, source_target_pairs={{0,4},{1,5},{4,8},{5,9},{8,12},{9,13},{12,14},{13,15},{14,10},{15,... | collective-permute-start | bytes 1179656 | tf_op jit(solution)/shard_map/ppermute | solution.py:345
  18.9 12.9 %collective-permute-start.2 = (f32[256,384]{1,0:T(8,128)S(1)}, f32[256,384]{1,0:T(8,128)S(1)}, u32[]{:S(2)}, u32[]{:S(2)}) collective-permute-start(f32[256,384]{1,0:T(8,128)S(1)} %get-tuple-element.33.x0.refs_3_), channel_id=1, source_target_pairs={{0,4},{1,5},{4,8},{5,9},{8,12},{9,13},{12,14},{13,15},{14,10},{15,... | collective-permute-start | bytes 1179656 | tf_op jit(solution)/shard_map/ppermute | solution.py:345
  21.9 12.7 %collective-permute-start.5 = (f32[256,384]{1,0:T(8,128)S(1)}, f32[256,384]{1,0:T(8,128)S(1)}, u32[]{:S(2)}, u32[]{:S(2)}) collective-permute-start(f32[256,384]{1,0:T(8,128)S(1)} %get-tuple-element.32.x1.refs_4_), channel_id=1, source_target_pairs={{4,0},{5,1},{8,4},{9,5},{12,8},{13,9},{14,12},{15,13},{10,14},{11,... | collective-permute-start | bytes 1179656 | tf_op jit(solution)/shard_map/ppermute | solution.py:345
  21.9 97.8 %copy-start.7 = (f32[256,384]{1,0:T(8,128)}, f32[256,384]{1,0:T(8,128)S(1)}, u32[]{:S(2)}) copy-start(f32[256,384]{1,0:T(8,128)S(1)} %collective-permute-done.8.x0) | copy-start | bytes 1179652
  21.9 18.3 %collective-permute-start.9 = (f32[256,384]{1,0:T(8,128)S(1)}, f32[256,384]{1,0:T(8,128)S(1)}, u32[]{:S(2)}, u32[]{:S(2)}) collective-permute-start(f32[256,384]{1,0:T(8,128)S(1)} %collective-permute-done.8.x0), channel_id=1, source_target_pairs={{0,4},{1,5},{4,8},{5,9},{8,12},{9,13},{12,14},{13,15},{14,10},{15,... | collective-permute-start | bytes 1179656 | tf_op jit(solution)/shard_map/ppermute | solution.py:345
  24.0 95.8 %copy-start.5 = (f32[256,384]{1,0:T(8,128)}, f32[256,384]{1,0:T(8,128)S(1)}, u32[]{:S(2)}) copy-start(f32[256,384]{1,0:T(8,128)S(1)} %collective-permute-done.11.x1) | copy-start | bytes 1179652
  24.0 19.1 %collective-permute-start.12 = (f32[256,384]{1,0:T(8,128)S(1)}, f32[256,384]{1,0:T(8,128)S(1)}, u32[]{:S(2)}, u32[]{:S(2)}) collective-permute-start(f32[256,384]{1,0:T(8,128)S(1)} %collective-permute-done.11.x1), channel_id=1, source_target_pairs={{4,0},{5,1},{8,4},{9,5},{12,8},{13,9},{14,12},{15,13},{10,14},{11,... | collective-permute-start | bytes 1179656 | tf_op jit(solution)/shard_map/ppermute | solution.py:345
  31.8 16.9 %collective-permute-start.3 = (f32[256,384]{1,0:T(8,128)S(1)}, f32[256,384]{1,0:T(8,128)S(1)}, u32[]{:S(2)}, u32[]{:S(2)}) collective-permute-start(f32[256,384]{1,0:T(8,128)S(1)} %collective-permute-done.2.x0), channel_id=1, source_target_pairs={{0,4},{1,5},{4,8},{5,9},{8,12},{9,13},{12,14},{13,15},{14,10},{15,... | collective-permute-start | bytes 1179656 | tf_op jit(solution)/shard_map/ppermute | solution.py:345
  34.7 16.9 %collective-permute-start.6 = (f32[256,384]{1,0:T(8,128)S(1)}, f32[256,384]{1,0:T(8,128)S(1)}, u32[]{:S(2)}, u32[]{:S(2)}) collective-permute-start(f32[256,384]{1,0:T(8,128)S(1)} %collective-permute-done.5.x1), channel_id=1, source_target_pairs={{4,0},{5,1},{8,4},{9,5},{12,8},{13,9},{14,12},{15,13},{10,14},{11,... | collective-permute-start | bytes 1179656 | tf_op jit(solution)/shard_map/ppermute | solution.py:345
  40.3 16.9 %collective-permute-start.10 = (f32[256,384]{1,0:T(8,128)S(1)}, f32[256,384]{1,0:T(8,128)S(1)}, u32[]{:S(2)}, u32[]{:S(2)}) collective-permute-start(f32[256,384]{1,0:T(8,128)S(1)} %collective-permute-done.9.x0), channel_id=1, source_target_pairs={{0,4},{1,5},{4,8},{5,9},{8,12},{9,13},{12,14},{13,15},{14,10},{15,... | collective-permute-start | bytes 1179656 | tf_op jit(solution)/shard_map/ppermute | solution.py:345
  43.1 16.9 %collective-permute-start.13 = (f32[256,384]{1,0:T(8,128)S(1)}, f32[256,384]{1,0:T(8,128)}, u32[]{:S(2)}, u32[]{:S(2)}) collective-permute-start(f32[256,384]{1,0:T(8,128)S(1)} %collective-permute-done.12.x1), channel_id=1, source_target_pairs={{4,0},{5,1},{8,4},{9,5},{12,8},{13,9},{14,12},{15,13},{10,14},{11,... | collective-permute-start | bytes 1179656 | tf_op jit(solution)/shard_map/ppermute | solution.py:345
  48.7 17.0 %collective-permute-start.4 = (f32[256,384]{1,0:T(8,128)S(1)}, f32[256,384]{1,0:T(8,128)}, u32[]{:S(2)}, u32[]{:S(2)}) collective-permute-start(f32[256,384]{1,0:T(8,128)S(1)} %collective-permute-done.3.x0), channel_id=1, source_target_pairs={{0,4},{1,5},{4,8},{5,9},{8,12},{9,13},{12,14},{13,15},{14,10},{15,... | collective-permute-start | bytes 1179656 | tf_op jit(solution)/shard_map/ppermute | solution.py:345
  51.5 16.2 %collective-permute-start.7 = (f32[256,384]{1,0:T(8,128)S(1)}, f32[256,384]{1,0:T(8,128)}, u32[]{:S(2)}, u32[]{:S(2)}) collective-permute-start(f32[256,384]{1,0:T(8,128)S(1)} %collective-permute-done.6.x1), channel_id=1, source_target_pairs={{4,0},{5,1},{8,4},{9,5},{12,8},{13,9},{14,12},{15,13},{10,14},{11,... | collective-permute-start | bytes 1179656 | tf_op jit(solution)/shard_map/ppermute | solution.py:345
  57.1 17.0 %collective-permute-start.16 = (f32[256,384]{1,0:T(8,128)S(1)}, f32[256,384]{1,0:T(8,128)}, u32[]{:S(2)}, u32[]{:S(2)}) collective-permute-start(f32[256,384]{1,0:T(8,128)S(1)} %collective-permute-done.10.x0), channel_id=1, source_target_pairs={{0,4},{1,5},{4,8},{5,9},{8,12},{9,13},{12,14},{13,15},{14,10},{15,... | collective-permute-start | bytes 1179656 | tf_op jit(solution)/shard_map/ppermute | solution.py:345
  60.0 16.2 %collective-permute-start.17 = (f32[256,384]{1,0:T(8,128)}, f32[256,384]{1,0:T(8,128)}, u32[]{:S(2)}, u32[]{:S(2)}) collective-permute-start(f32[256,384]{1,0:T(8,128)} %collective-permute-done.13.x1), channel_id=1, source_target_pairs={{4,0},{5,1},{8,4},{9,5},{12,8},{13,9},{14,12},{15,13},{10,14},{11,... | collective-permute-start | bytes 1179656 | tf_op jit(solution)/shard_map/ppermute | solution.py:345
  65.6 16.9 %collective-permute-start.14 = (f32[256,384]{1,0:T(8,128)}, f32[256,384]{1,0:T(8,128)}, u32[]{:S(2)}, u32[]{:S(2)}) collective-permute-start(f32[256,384]{1,0:T(8,128)} %collective-permute-done.4.x0), channel_id=1, source_target_pairs={{0,4},{1,5},{4,8},{5,9},{8,12},{9,13},{12,14},{13,15},{14,10},{15,... | collective-permute-start | bytes 1179656 | tf_op jit(solution)/shard_map/ppermute | solution.py:345
  67.7 17.6 %collective-permute-start.15 = (f32[256,384]{1,0:T(8,128)}, f32[256,384]{1,0:T(8,128)}, u32[]{:S(2)}, u32[]{:S(2)}) collective-permute-start(f32[256,384]{1,0:T(8,128)} %collective-permute-done.7.x1), channel_id=1, source_target_pairs={{4,0},{5,1},{8,4},{9,5},{12,8},{13,9},{14,12},{15,13},{10,14},{11,... | collective-permute-start | bytes 1179656 | tf_op jit(solution)/shard_map/ppermute | solution.py:345
  74.1 16.9 %collective-permute-start.30 = (f32[256,384]{1,0:T(8,128)}, f32[256,384]{1,0:T(8,128)}, u32[]{:S(2)}, u32[]{:S(2)}) collective-permute-start(f32[256,384]{1,0:T(8,128)} %collective-permute-done.16.x0), channel_id=1, source_target_pairs={{0,4},{1,5},{4,8},{5,9},{8,12},{9,13},{12,14},{13,15},{14,10},{15,... | collective-permute-start | bytes 1179656 | tf_op jit(solution)/shard_map/ppermute | solution.py:345
  76.2 16.9 %collective-permute-start.33 = (f32[256,384]{1,0:T(8,128)}, f32[256,384]{1,0:T(8,128)}, u32[]{:S(2)}, u32[]{:S(2)}) collective-permute-start(f32[256,384]{1,0:T(8,128)} %collective-permute-done.17.x1), channel_id=1, source_target_pairs={{4,0},{5,1},{8,4},{9,5},{12,8},{13,9},{14,12},{15,13},{10,14},{11,... | collective-permute-start | bytes 1179656 | tf_op jit(solution)/shard_map/ppermute | solution.py:345
  82.5 16.9 %collective-permute-start.24 = (f32[256,384]{1,0:T(8,128)}, f32[256,384]{1,0:T(8,128)}, u32[]{:S(2)}, u32[]{:S(2)}) collective-permute-start(f32[256,384]{1,0:T(8,128)} %collective-permute-done.14.x0), channel_id=1, source_target_pairs={{0,4},{1,5},{4,8},{5,9},{8,12},{9,13},{12,14},{13,15},{14,10},{15,... | collective-permute-start | bytes 1179656 | tf_op jit(solution)/shard_map/ppermute | solution.py:345
  85.4 16.3 %collective-permute-start.27 = (f32[256,384]{1,0:T(8,128)}, f32[256,384]{1,0:T(8,128)}, u32[]{:S(2)}, u32[]{:S(2)}) collective-permute-start(f32[256,384]{1,0:T(8,128)} %collective-permute-done.15.x1), channel_id=1, source_target_pairs={{4,0},{5,1},{8,4},{9,5},{12,8},{13,9},{14,12},{15,13},{10,14},{11,... | collective-permute-start | bytes 1179656 | tf_op jit(solution)/shard_map/ppermute | solution.py:345
  90.9 16.9 %collective-permute-start.31 = (f32[256,384]{1,0:T(8,128)}, f32[256,384]{1,0:T(8,128)}, u32[]{:S(2)}, u32[]{:S(2)}) collective-permute-start(f32[256,384]{1,0:T(8,128)} %collective-permute-done.30.x0), channel_id=1, source_target_pairs={{0,4},{1,5},{4,8},{5,9},{8,12},{9,13},{12,14},{13,15},{14,10},{15,... | collective-permute-start | bytes 1179656 | tf_op jit(solution)/shard_map/ppermute | solution.py:345
  93.0 16.9 %collective-permute-start.34 = (f32[256,384]{1,0:T(8,128)}, f32[256,384]{1,0:T(8,128)}, u32[]{:S(2)}, u32[]{:S(2)}) collective-permute-start(f32[256,384]{1,0:T(8,128)} %collective-permute-done.33.x1), channel_id=1, source_target_pairs={{4,0},{5,1},{8,4},{9,5},{12,8},{13,9},{14,12},{15,13},{10,14},{11,... | collective-permute-start | bytes 1179656 | tf_op jit(solution)/shard_map/ppermute | solution.py:345
  99.4 16.7 %collective-permute-start.25 = (f32[256,384]{1,0:T(8,128)}, f32[256,384]{1,0:T(8,128)S(1)}, u32[]{:S(2)}, u32[]{:S(2)}) collective-permute-start(f32[256,384]{1,0:T(8,128)} %collective-permute-done.24.x0), channel_id=1, source_target_pairs={{0,4},{1,5},{4,8},{5,9},{8,12},{9,13},{12,14},{13,15},{14,10},{15,... | collective-permute-start | bytes 1179656 | tf_op jit(solution)/shard_map/ppermute | solution.py:345
  101.7 17.3 %collective-permute-start.28 = (f32[256,384]{1,0:T(8,128)}, f32[256,384]{1,0:T(8,128)S(1)}, u32[]{:S(2)}, u32[]{:S(2)}) collective-permute-start(f32[256,384]{1,0:T(8,128)} %collective-permute-done.27.x1), channel_id=1, source_target_pairs={{4,0},{5,1},{8,4},{9,5},{12,8},{13,9},{14,12},{15,13},{10,14},{11,... | collective-permute-start | bytes 1179656 | tf_op jit(solution)/shard_map/ppermute | solution.py:345
  107.8 65.2 %collective-permute-start.32 = (f32[256,384]{1,0:T(8,128)}, f32[256,384]{1,0:T(8,128)}, u32[]{:S(2)}, u32[]{:S(2)}) collective-permute-start(f32[256,384]{1,0:T(8,128)} %collective-permute-done.31.x0), channel_id=1, source_target_pairs={{0,4},{1,5},{4,8},{5,9},{8,12},{9,13},{12,14},{13,15},{14,10},{15,... | collective-permute-start | bytes 1179656 | tf_op jit(solution)/shard_map/ppermute | solution.py:345
  109.9 65.2 %collective-permute-start.35 = (f32[256,384]{1,0:T(8,128)}, f32[256,384]{1,0:T(8,128)}, u32[]{:S(2)}, u32[]{:S(2)}) collective-permute-start(f32[256,384]{1,0:T(8,128)} %collective-permute-done.34.x1), channel_id=1, source_target_pairs={{4,0},{5,1},{8,4},{9,5},{12,8},{13,9},{14,12},{15,13},{10,14},{11,... | collective-permute-start | bytes 1179656 | tf_op jit(solution)/shard_map/ppermute | solution.py:345
  116.9 80.1 %collective-permute-start.26 = (f32[128,384]{1,0:T(8,128)}, f32[128,384]{1,0:T(8,128)}, u32[]{:S(2)}, u32[]{:S(2)}) collective-permute-start(f32[128,384]{1,0:T(8,128)} %get-tuple-element.37), channel_id=1, source_target_pairs={{0,4},{1,5},{4,8},{5,9},{8,12},{9,13},{12,14},{13,15},{14,10},{15,... | collective-permute-start | bytes 589832 | tf_op jit(solution)/shard_map/ppermute | solution.py:333
  119.8 77.2 %collective-permute-start.29 = (f32[128,384]{1,0:T(8,128)}, f32[128,384]{1,0:T(8,128)}, u32[]{:S(2)}, u32[]{:S(2)}) collective-permute-start(f32[128,384]{1,0:T(8,128)} %get-tuple-element.35), channel_id=1, source_target_pairs={{4,0},{5,1},{8,4},{9,5},{12,8},{13,9},{14,12},{15,13},{10,14},{11,... | collective-permute-start | bytes 589832 | tf_op jit(solution)/shard_map/ppermute | solution.py:333
  123.0 3.9 %copy-start.6 = (f32[256,384]{1,0:T(8,128)S(1)}, f32[256,384]{1,0:T(8,128)}, u32[]{:S(2)}) copy-start(f32[256,384]{1,0:T(8,128)} %copy-done.5) | copy-start | bytes 1179652
  123.1 3.9 %copy-start.8 = (f32[256,384]{1,0:T(8,128)S(1)}, f32[256,384]{1,0:T(8,128)}, u32[]{:S(2)}) copy-start(f32[256,384]{1,0:T(8,128)} %copy-done.7) | copy-start | bytes 1179652
  157.6 23.7 %collective-permute-start.18 = (f32[256]{0:T(256)S(1)}, f32[256]{0:T(256)S(1)}, u32[]{:S(2)}, u32[]{:S(2)}) collective-permute-start(f32[256]{0:T(256)S(1)} %bitcast.29), channel_id=1, source_target_pairs={{0,1},{1,0},{2,3},{3,2},{4,5},{5,4},{6,7},{7,6},{8,9},{9,8},{10,11... | collective-permute-start | bytes 3080 | tf_op jit(solution)/shard_map/ppermute | solution.py:322
  165.6 4.0 %copy-start.4 = (f32[256,384]{1,0:T(8,128)S(1)}, f32[256,384]{1,0:T(8,128)}, u32[]{:S(2)}) copy-start(f32[256,384]{1,0:T(8,128)} %copy-done.3) | copy-start | bytes 1179652
  173.0 10.0 %collective-permute-start.19 = (f32[256]{0:T(256)S(1)}, f32[256]{0:T(256)S(1)}, u32[]{:S(2)}, u32[]{:S(2)}) collective-permute-start(f32[256]{0:T(256)S(1)} %bitcast.28), channel_id=1, source_target_pairs={{0,2},{1,3},{2,0},{3,1},{4,6},{5,7},{6,4},{7,5},{8,10},{9,11},{10,... | collective-permute-start | bytes 3080 | tf_op jit(solution)/shard_map/ppermute | solution.py:322
  175.0 6.2 %copy-start.23 = (f32[128,384]{1,0:T(8,128)S(1)}, f32[128,384]{1,0:T(8,128)}, u32[]{:S(2)}) copy-start(f32[128,384]{1,0:T(8,128)} %get-tuple-element.36) | copy-start | bytes 589828
  175.0 8.0 %copy-start.24 = (f32[128,384]{1,0:T(8,128)S(1)}, f32[128,384]{1,0:T(8,128)}, u32[]{:S(2)}) copy-start(f32[128,384]{1,0:T(8,128)} %get-tuple-element.34) | copy-start | bytes 589828
  175.0 8.3 %collective-permute-start.20 = (f32[256]{0:T(256)S(1)}, f32[256]{0:T(256)S(1)}, u32[]{:S(2)}, u32[]{:S(2)}) collective-permute-start(f32[256]{0:T(256)S(1)} %bitcast.27), channel_id=1, source_target_pairs={{0,3},{1,2},{2,1},{3,0},{4,7},{5,6},{6,5},{7,4},{8,11},{9,10},{10,... | collective-permute-start | bytes 3080 | tf_op jit(solution)/shard_map/ppermute | solution.py:322
  181.3 7.0 %collective-permute-start.37 = (f32[128,384]{1,0:T(8,128)S(1)}, f32[128,384]{1,0:T(8,128)S(1)}, u32[]{:S(2)}, u32[]{:S(2)}) collective-permute-start(f32[128,384]{1,0:T(8,128)S(1)} %copy-done.23), channel_id=1, source_target_pairs={{0,4},{1,5},{4,8},{5,9},{8,12},{9,13},{12,14},{13,15},{14,10},{15,... | collective-permute-start | bytes 589832 | tf_op jit(solution)/shard_map/ppermute | solution.py:333
  183.0 8.1 %collective-permute-start.38 = (f32[128,384]{1,0:T(8,128)S(1)}, f32[128,384]{1,0:T(8,128)S(1)}, u32[]{:S(2)}, u32[]{:S(2)}) collective-permute-start(f32[128,384]{1,0:T(8,128)S(1)} %copy-done.24), channel_id=1, source_target_pairs={{4,0},{5,1},{8,4},{9,5},{12,8},{13,9},{14,12},{15,13},{10,14},{11,... | collective-permute-start | bytes 589832 | tf_op jit(solution)/shard_map/ppermute | solution.py:333
  183.4 12.1 %collective-permute-start.21 = (f32[64]{0:T(128)S(1)}, f32[64]{0:T(128)S(1)}, u32[]{:S(2)}, u32[]{:S(2)}) collective-permute-start(f32[64]{0:T(128)S(1)} %get-tuple-element.42), channel_id=1, source_target_pairs={{0,4},{1,5},{2,6},{3,7},{4,0},{5,1},{6,2},{7,3},{8,12},{9,13},{10,... | collective-permute-start | bytes 776 | tf_op jit(solution)/shard_map/ppermute | solution.py:322
  188.3 7.3 %collective-permute-start.22 = (f32[64]{0:T(128)S(1)}, f32[64]{0:T(128)S(1)}, u32[]{:S(2)}, u32[]{:S(2)}) collective-permute-start(f32[64]{0:T(128)S(1)} %get-tuple-element.44), channel_id=1, source_target_pairs={{0,8},{1,9},{2,10},{3,11},{4,12},{5,13},{6,14},{7,15},{8,0},{9,1},... | collective-permute-start | bytes 776 | tf_op jit(solution)/shard_map/ppermute | solution.py:322
  191.1 5.4 %collective-permute-start.23 = (f32[64]{0:T(128)S(1)}, f32[64]{0:T(128)S(1)}, u32[]{:S(2)}, u32[]{:S(2)}) collective-permute-start(f32[64]{0:T(128)S(1)} %get-tuple-element.43), channel_id=1, source_target_pairs={{0,12},{1,13},{2,14},{3,15},{4,8},{5,9},{6,10},{7,11},{8,4},{9,5},... | collective-permute-start | bytes 776 | tf_op jit(solution)/shard_map/ppermute | solution.py:322
  195.5 6.0 %collective-permute-start.39 = (f32[256,384]{1,0:T(8,128)S(1)}, f32[256,384]{1,0:T(8,128)S(1)}, u32[]{:S(2)}, u32[]{:S(2)}) collective-permute-start(f32[256,384]{1,0:T(8,128)S(1)} %finish.3), channel_id=1, source_target_pairs={{0,1},{1,0},{2,3},{3,2},{4,5},{5,4},{6,7},{7,6},{8,9},{9,8},{10,11... | collective-permute-start | bytes 1179656 | tf_op jit(solution)/shard_map/ppermute | solution.py:340
  198.7 2.9 %collective-permute-start.36 = (f32[256,384]{1,0:T(8,128)S(1)}, f32[256,384]{1,0:T(8,128)S(1)}, u32[]{:S(2)}, u32[]{:S(2)}) collective-permute-start(f32[256,384]{1,0:T(8,128)S(1)} %finish.2), channel_id=1, source_target_pairs={{0,1},{1,0},{2,3},{3,2},{4,5},{5,4},{6,7},{7,6},{8,9},{9,8},{10,11... | collective-permute-start | bytes 1179656 | tf_op jit(solution)/shard_map/ppermute | solution.py:340
  (18 other events, 34.9 us)

commit v3 on v2

--- a/solution.py
+++ b/solution.py
@@ -161,67 +161,55 @@
     )(*pieces, right, total)
 
 
-def send_out(value, half, way, at, turned, sems, out):
+def send_out(value, half, way, at, kind, turned, sems, out):
     wide = value.shape[0]
-    turned[way, at] = value.T
+    turned[kind, way, at] = value.T
     quarter = out.shape[1] // 4
     columns = pl.ds(pl.multiple_of((2 * half + way) * quarter + at * wide, wide), wide)
-    copy = pltpu.make_async_copy(turned.at[way, at], out.at[:, columns], sems.at[way, at])
+    copy = pltpu.make_async_copy(turned.at[kind, way, at], out.at[:, columns], sems.at[kind, way, at])
     copy.start()
     return copy
 
 
-def own_kernel(core, *refs):
-    late, right, total, out, turned, sems = refs[:-5], *refs[-5:]
-    copies = [
-        send_out(last_part(0, i // 2, i % 2, x, right, total), core[0], i % 2, i // 2, turned, sems, out)
-        for i, x in enumerate(late)
-    ]
+def settle_kernel(owns, others, aliased, core, *refs):
+    out, turned, sems = refs[-3:]
+    refs = refs[: len(refs) - 3 - aliased]
+    copies = []
+    if owns:
+        right, total = refs[2 * len(owns)], refs[2 * len(owns) + 1]
+        for i, at in enumerate(owns):
+            for way in (0, 1):
+                part = last_part(0, at, way, refs[2 * i + way], right, total)
+                copies.append(send_out(part, core[0], way, at, 0, turned, sems, out))
+    refs = refs[len(refs) - len(others) :]
+    for i, at in enumerate(others):
+        wide = turned.shape[4]
+        for way in (0, 1):
+            part = refs[i][way * wide : (way + 1) * wide, :]
+            copies.append(send_out(part, 1 - core[0], way, at, 1, turned, sems, out))
     for copy in copies:
         copy.wait()
 
 
-def finish_own(core, late, right, total):
-    wide, rows = late[0].shape
+def settle(core, owns, others, right, total, out=None):
+    rows = total.shape[1] // 2
+    wide = total.shape[0] // 2 // PARTS
     vmem = pl.BlockSpec(memory_space=pltpu.VMEM)
+    args = [x for pair in owns.values() for x in pair] + ([right, total] if owns else []) + list(others.values())
+    more = [] if out is None else [out]
     return pl.pallas_call(
-        own_kernel,
+        functools.partial(settle_kernel, tuple(owns), tuple(others), len(more)),
         out_shape=jax.ShapeDtypeStruct((rows, 2 * total.shape[0]), jnp.float32),
-        in_specs=[pl.BlockSpec(memory_space=pltpu.SMEM)] + [vmem] * (len(late) + 2),
+        in_specs=[pl.BlockSpec(memory_space=pltpu.SMEM)]
+        + [vmem] * len(args)
+        + [pl.BlockSpec(memory_space=pl.ANY)] * len(more),
         out_specs=pl.BlockSpec(memory_space=pl.ANY),
-        scratch_shapes=[pltpu.VMEM((2, PARTS, rows, wide), jnp.float32), pltpu.SemaphoreType.DMA((2, PARTS))],
+        scratch_shapes=[pltpu.VMEM((2, 2, PARTS, rows, wide), jnp.float32), pltpu.SemaphoreType.DMA((2, 2, PARTS))],
+        input_output_aliases={1 + len(args): 0} if more else {},
         cost_estimate=pl.CostEstimate(flops=24 * rows * rows * wide, bytes_accessed=16 * rows * rows, transcendentals=0),
         compiler_params=pltpu.CompilerParams(vmem_limit_bytes=DOTS_LIMIT),
-        name="finish_own",
-    )(core.reshape(1), *late, right, total)
-
-
-def place_kernel(core, *refs):
-    others, out, turned, sems = refs[:PARTS], *refs[-3:]
-    wide = turned.shape[3]
-    copies = [
-        send_out(x[way * wide : (way + 1) * wide, :], 1 - core[0], way, at, turned, sems, out)
-        for at, x in enumerate(others)
-        for way in (0, 1)
-    ]
-    for copy in copies:
-        copy.wait()
-
-
-def place(core, others, out):
-    both, rows = others[0].shape
-    return pl.pallas_call(
-        place_kernel,
-        out_shape=jax.ShapeDtypeStruct(out.shape, jnp.float32),
-        in_specs=[pl.BlockSpec(memory_space=pltpu.SMEM)]
-        + [pl.BlockSpec(memory_space=pltpu.VMEM)] * PARTS
-        + [pl.BlockSpec(memory_space=pl.ANY)],
-        out_specs=pl.BlockSpec(memory_space=pl.ANY),
-        scratch_shapes=[pltpu.VMEM((2, PARTS, rows, both // 2), jnp.float32), pltpu.SemaphoreType.DMA((2, PARTS))],
-        input_output_aliases={1 + PARTS: 0},
-        compiler_params=pltpu.CompilerParams(vmem_limit_bytes=DOTS_LIMIT),
-        name="place",
-    )(core.reshape(1), *others, out)
+        name="settle",
+    )(core.reshape(1), *args, *more)
 
 
 def take_kernel(side, block, gmap, *refs):
@@ -335,11 +323,13 @@
                             ]
                         )
                     terms, *late[0] = lax.optimization_barrier((terms, *late[0]))
+                    screened = None
                     for at, use in enumerate(late):
                         other = finish_partner(at, use, right, total)
                         others.append(lax.ppermute(other, "blk", partner))
-                    screened = finish_own(core, [x for use in late for x in use], right, total)
-                    screened = place(core, others, screened)
+                        done = {at - 1: others[at - 1]} if at else {}
+                        screened = settle(core, {at: use}, done, right, total, screened)
+                    screened = settle(core, {}, {PARTS - 1: others[-1]}, right, total, screened)
                     break
                 if step:
                     held[c] = [lax.ppermute(held[c][way], "blk", back if way else ahead) for way in (0, 1)]

time: 204 us -> 198 us (0.971)
  starting transfers between devices: 43.1 us -> 39.5 us
  local copies, waits for them, and re-layouts: 10.8 us -> 7.71 us
  waiting for transfers between devices: 78.8 us -> 81.2 us
    unnamed x52 -> x50, local copies, waits for them, and re-layouts: 8.54 us -> 5.44 us
    ppermute x6, waiting for transfers between devices: 0.85 us -> 3.92 us  [exchange(): lax.ppermute(sent, 'blk', [(b, b ^ mask) for b in range(size)])]
    ppermute x6, starting transfers between devices: 9.11 us -> 6.44 us  [exchange(): lax.ppermute(sent, 'blk', [(b, b ^ mask) for b in range(size)])]
  transfers between devices with their start and end apart: 40 -> 40, of which waited for: 14 -> 16; matrix products, arithmetic and copies ran while one was open for 2% -> 2% of each run, Pallas kernels for 32% -> 32%
where the time goes in v3:
time: 198 us; the launch traced here: 197 us
  waiting for transfers between devices  81.2 us (41%)
  Pallas kernels  66 us (33%)
  starting transfers between devices  39.5 us (20%)
  local copies, waits for them, and re-layouts  7.71 us (4%)
    ppermute x26, waiting for transfers between devices, local(): lax.ppermute(held[c][way], 'blk', back if way else ahead)  65.7 us
    pallas_call x15, Pallas kernels, dots(): pl.pallas_call(functools.partial(dots_kernel, at, total is None, int(star...  57 us
    ppermute x26, starting transfers between devices, local(): lax.ppermute(held[c][way], 'blk', back if way else ahead)  29 us
    ppermute x1, waiting for transfers between devices, local(): given = lax.ppermute(away, 'blk', partner)  10.4 us
    ppermute x6, starting transfers between devices, exchange(): lax.ppermute(sent, 'blk', [(b, b ^ mask) for b in range(size)])  6.44 us
    unnamed x50, local copies, waits for them, and re-layouts  5.44 us
    pallas_call x2, Pallas kernels, take(): pl.pallas_call(take_kernel, out_shape=(piece,) * pieces, in_specs=[pl.Blo...  4.12 us
  transfers between devices with their start and end apart: 40, of which 16 were waited for; matrix products, arithmetic and copies ran while one was open for 2% of the time, Pallas kernels for 32%

profile of v3, /device:TPU:0, one launch (start us, length us, event | category | flops | bytes accessed | tf_op | source)
XLA Modules:
  0.0 197.4 jit_solution(2770403751265083334)
XLA Ops:
  0.6 2.1 %take.2 = f32[512,384]{1,0:T(8,128)S(1)} custom-call(s32[1]{0:T(128)} %bitcast.1.side, f32[384,1024]{1,0:T(8,128)} %block.3, s32[384]{0:T(512)} %gmap.3), custom_call_target="tpu_custom_call" | custom-call | flops 452984832 | bytes 1572864 | tf_op jit(solution)/shard_map/take/pallas_call | solution.py:246
  3.4 2.1 %take.3 = (f32[256,384]{1,0:T(8,128)S(1)}, f32[256,384]{1,0:T(8,128)S(1)}) custom-call(s32[1]{0:T(128)} %bitcast.side.core, f32[384,1024]{1,0:T(8,128)} %block.3, s32[384]{0:T(512)} %gmap.3), custom_call_target="tpu_custom_call" | custom-call | flops 452984832 | bytes 1572864 | tf_op jit(solution)/shard_map/take/pallas_call | solution.py:246
  5.4 3.0 %collective-permute-start.15 = (f32[256,384]{1,0:T(8,128)S(1)}, f32[256,384]{1,0:T(8,128)S(1)}, u32[]{:S(2)}, u32[]{:S(2)}) collective-permute-start(f32[256,384]{1,0:T(8,128)S(1)} %get-tuple-element.16.x0.refs_1_), channel_id=1, source_target_pairs={{0,4},{1,5},{4,8},{5,9},{8,12},{9,13},{12,14},{13,15},{14,10},{15,... | collective-permute-start | bytes 1179656 | tf_op jit(solution)/shard_map/ppermute | solution.py:335
  8.5 10.4 %collective-permute-done = f32[512,384]{1,0:T(8,128)S(1)} collective-permute-done((f32[512,384]{1,0:T(8,128)S(1)}, f32[512,384]{1,0:T(8,128)S(1)}, u32[]{:S(2)}, u32[]{:S(2)}) %collective-permute-start) | collective-permute-done | bytes 786464 | tf_op jit(solution)/shard_map/ppermute | solution.py:288
  18.9 3.0 %collective-permute-start.1 = (f32[256,384]{1,0:T(8,128)S(1)}, f32[256,384]{1,0:T(8,128)S(1)}, u32[]{:S(2)}, u32[]{:S(2)}) collective-permute-start(f32[256,384]{1,0:T(8,128)S(1)} %get-tuple-element.33.x0.refs_3_), channel_id=1, source_target_pairs={{0,4},{1,5},{4,8},{5,9},{8,12},{9,13},{12,14},{13,15},{14,10},{15,... | collective-permute-start | bytes 1179656 | tf_op jit(solution)/shard_map/ppermute | solution.py:335
  21.9 2.0 %collective-permute-start.16 = (f32[256,384]{1,0:T(8,128)S(1)}, f32[256,384]{1,0:T(8,128)S(1)}, u32[]{:S(2)}, u32[]{:S(2)}) collective-permute-start(f32[256,384]{1,0:T(8,128)S(1)} %collective-permute-done.15.x0), channel_id=1, source_target_pairs={{0,4},{1,5},{4,8},{5,9},{8,12},{9,13},{12,14},{13,15},{14,10},{15,... | collective-permute-start | bytes 1179656 | tf_op jit(solution)/shard_map/ppermute | solution.py:335
  24.0 7.8 %collective-permute-done.1.x0 = f32[256,384]{1,0:T(8,128)S(1)} collective-permute-done((f32[256,384]{1,0:T(8,128)S(1)}, f32[256,384]{1,0:T(8,128)S(1)}, u32[]{:S(2)}, u32[]{:S(2)}) %collective-permute-start.1) | collective-permute-done | bytes 393248 | tf_op jit(solution)/shard_map/ppermute | solution.py:335
  31.8 2.1 %collective-permute-start.2 = (f32[256,384]{1,0:T(8,128)S(1)}, f32[256,384]{1,0:T(8,128)S(1)}, u32[]{:S(2)}, u32[]{:S(2)}) collective-permute-start(f32[256,384]{1,0:T(8,128)S(1)} %collective-permute-done.1.x0), channel_id=1, source_target_pairs={{0,4},{1,5},{4,8},{5,9},{8,12},{9,13},{12,14},{13,15},{14,10},{15,... | collective-permute-start | bytes 1179656 | tf_op jit(solution)/shard_map/ppermute | solution.py:335
  35.4 4.8 %collective-permute-done.16.x0 = f32[256,384]{1,0:T(8,128)S(1)} collective-permute-done((f32[256,384]{1,0:T(8,128)S(1)}, f32[256,384]{1,0:T(8,128)S(1)}, u32[]{:S(2)}, u32[]{:S(2)}) %collective-permute-start.16) | collective-permute-done | bytes 393248 | tf_op jit(solution)/shard_map/ppermute | solution.py:335
  40.3 2.1 %collective-permute-start.17 = (f32[256,384]{1,0:T(8,128)S(1)}, f32[256,384]{1,0:T(8,128)S(1)}, u32[]{:S(2)}, u32[]{:S(2)}) collective-permute-start(f32[256,384]{1,0:T(8,128)S(1)} %collective-permute-done.16.x0), channel_id=1, source_target_pairs={{0,4},{1,5},{4,8},{5,9},{8,12},{9,13},{12,14},{13,15},{14,10},{15,... | collective-permute-start | bytes 1179656 | tf_op jit(solution)/shard_map/ppermute | solution.py:335
  43.9 4.8 %collective-permute-done.2.x0 = f32[256,384]{1,0:T(8,128)S(1)} collective-permute-done((f32[256,384]{1,0:T(8,128)S(1)}, f32[256,384]{1,0:T(8,128)S(1)}, u32[]{:S(2)}, u32[]{:S(2)}) %collective-permute-start.2) | collective-permute-done | bytes 393248 | tf_op jit(solution)/shard_map/ppermute | solution.py:335
  48.7 2.1 %collective-permute-start.3 = (f32[256,384]{1,0:T(8,128)S(1)}, f32[256,384]{1,0:T(8,128)}, u32[]{:S(2)}, u32[]{:S(2)}) collective-permute-start(f32[256,384]{1,0:T(8,128)S(1)} %collective-permute-done.2.x0), channel_id=1, source_target_pairs={{0,4},{1,5},{4,8},{5,9},{8,12},{9,13},{12,14},{13,15},{14,10},{15,... | collective-permute-start | bytes 1179656 | tf_op jit(solution)/shard_map/ppermute | solution.py:335
  52.3 4.8 %collective-permute-done.17.x0 = f32[256,384]{1,0:T(8,128)S(1)} collective-permute-done((f32[256,384]{1,0:T(8,128)S(1)}, f32[256,384]{1,0:T(8,128)S(1)}, u32[]{:S(2)}, u32[]{:S(2)}) %collective-permute-start.17) | collective-permute-done | bytes 393248 | tf_op jit(solution)/shard_map/ppermute | solution.py:335
  57.1 2.1 %collective-permute-start.18 = (f32[256,384]{1,0:T(8,128)S(1)}, f32[256,384]{1,0:T(8,128)}, u32[]{:S(2)}, u32[]{:S(2)}) collective-permute-start(f32[256,384]{1,0:T(8,128)S(1)} %collective-permute-done.17.x0), channel_id=1, source_target_pairs={{0,4},{1,5},{4,8},{5,9},{8,12},{9,13},{12,14},{13,15},{14,10},{15,... | collective-permute-start | bytes 1179656 | tf_op jit(solution)/shard_map/ppermute | solution.py:335
  60.0 5.7 %collective-permute-done.3.x0 = f32[256,384]{1,0:T(8,128)} collective-permute-done((f32[256,384]{1,0:T(8,128)S(1)}, f32[256,384]{1,0:T(8,128)}, u32[]{:S(2)}, u32[]{:S(2)}) %collective-permute-start.3) | collective-permute-done | bytes 393248 | tf_op jit(solution)/shard_map/ppermute | solution.py:335
  65.6 2.1 %collective-permute-start.4 = (f32[256,384]{1,0:T(8,128)}, f32[256,384]{1,0:T(8,128)}, u32[]{:S(2)}, u32[]{:S(2)}) collective-permute-start(f32[256,384]{1,0:T(8,128)} %collective-permute-done.3.x0), channel_id=1, source_target_pairs={{0,4},{1,5},{4,8},{5,9},{8,12},{9,13},{12,14},{13,15},{14,10},{15,... | collective-permute-start | bytes 1179656 | tf_op jit(solution)/shard_map/ppermute | solution.py:335
  67.7 6.3 %collective-permute-done.18.x0 = f32[256,384]{1,0:T(8,128)} collective-permute-done((f32[256,384]{1,0:T(8,128)S(1)}, f32[256,384]{1,0:T(8,128)}, u32[]{:S(2)}, u32[]{:S(2)}) %collective-permute-start.18) | collective-permute-done | bytes 393248 | tf_op jit(solution)/shard_map/ppermute | solution.py:335
  74.1 2.1 %collective-permute-start.19 = (f32[256,384]{1,0:T(8,128)}, f32[256,384]{1,0:T(8,128)}, u32[]{:S(2)}, u32[]{:S(2)}) collective-permute-start(f32[256,384]{1,0:T(8,128)} %collective-permute-done.18.x0), channel_id=1, source_target_pairs={{0,4},{1,5},{4,8},{5,9},{8,12},{9,13},{12,14},{13,15},{14,10},{15,... | collective-permute-start | bytes 1179656 | tf_op jit(solution)/shard_map/ppermute | solution.py:335
  76.2 6.3 %collective-permute-done.4.x0 = f32[256,384]{1,0:T(8,128)} collective-permute-done((f32[256,384]{1,0:T(8,128)}, f32[256,384]{1,0:T(8,128)}, u32[]{:S(2)}, u32[]{:S(2)}) %collective-permute-start.4) | collective-permute-done | bytes 393248 | tf_op jit(solution)/shard_map/ppermute | solution.py:335
  82.5 2.1 %collective-permute-start.5 = (f32[256,384]{1,0:T(8,128)}, f32[256,384]{1,0:T(8,128)}, u32[]{:S(2)}, u32[]{:S(2)}) collective-permute-start(f32[256,384]{1,0:T(8,128)} %collective-permute-done.4.x0), channel_id=1, source_target_pairs={{0,4},{1,5},{4,8},{5,9},{8,12},{9,13},{12,14},{13,15},{14,10},{15,... | collective-permute-start | bytes 1179656 | tf_op jit(solution)/shard_map/ppermute | solution.py:335
  85.6 5.3 %collective-permute-done.19.x0 = f32[256,384]{1,0:T(8,128)} collective-permute-done((f32[256,384]{1,0:T(8,128)}, f32[256,384]{1,0:T(8,128)}, u32[]{:S(2)}, u32[]{:S(2)}) %collective-permute-start.19) | collective-permute-done | bytes 393248 | tf_op jit(solution)/shard_map/ppermute | solution.py:335
  90.9 2.1 %collective-permute-start.20 = (f32[256,384]{1,0:T(8,128)}, f32[256,384]{1,0:T(8,128)}, u32[]{:S(2)}, u32[]{:S(2)}) collective-permute-start(f32[256,384]{1,0:T(8,128)} %collective-permute-done.19.x0), channel_id=1, source_target_pairs={{0,4},{1,5},{4,8},{5,9},{8,12},{9,13},{12,14},{13,15},{14,10},{15,... | collective-permute-start | bytes 1179656 | tf_op jit(solution)/shard_map/ppermute | solution.py:335
  93.0 6.3 %collective-permute-done.5.x0 = f32[256,384]{1,0:T(8,128)} collective-permute-done((f32[256,384]{1,0:T(8,128)}, f32[256,384]{1,0:T(8,128)}, u32[]{:S(2)}, u32[]{:S(2)}) %collective-permute-start.5) | collective-permute-done | bytes 393248 | tf_op jit(solution)/shard_map/ppermute | solution.py:335
  99.4 2.1 %collective-permute-start.6 = (f32[256,384]{1,0:T(8,128)}, f32[256,384]{1,0:T(8,128)S(1)}, u32[]{:S(2)}, u32[]{:S(2)}) collective-permute-start(f32[256,384]{1,0:T(8,128)} %collective-permute-done.5.x0), channel_id=1, source_target_pairs={{0,4},{1,5},{4,8},{5,9},{8,12},{9,13},{12,14},{13,15},{14,10},{15,... | collective-permute-start | bytes 1179656 | tf_op jit(solution)/shard_map/ppermute | solution.py:335
  101.9 5.9 %collective-permute-done.20.x0 = f32[256,384]{1,0:T(8,128)} collective-permute-done((f32[256,384]{1,0:T(8,128)}, f32[256,384]{1,0:T(8,128)}, u32[]{:S(2)}, u32[]{:S(2)}) %collective-permute-start.20) | collective-permute-done | bytes 393248 | tf_op jit(solution)/shard_map/ppermute | solution.py:335
  107.8 2.1 %collective-permute-start.21 = (f32[256,384]{1,0:T(8,128)}, f32[256,384]{1,0:T(8,128)}, u32[]{:S(2)}, u32[]{:S(2)}) collective-permute-start(f32[256,384]{1,0:T(8,128)} %collective-permute-done.20.x0), channel_id=1, source_target_pairs={{0,4},{1,5},{4,8},{5,9},{8,12},{9,13},{12,14},{13,15},{14,10},{15,... | collective-permute-start | bytes 1179656 | tf_op jit(solution)/shard_map/ppermute | solution.py:335
  109.9 6.2 %collective-permute-done.6.x0 = f32[256,384]{1,0:T(8,128)S(1)} collective-permute-done((f32[256,384]{1,0:T(8,128)}, f32[256,384]{1,0:T(8,128)S(1)}, u32[]{:S(2)}, u32[]{:S(2)}) %collective-permute-start.6) | collective-permute-done | bytes 393248 | tf_op jit(solution)/shard_map/ppermute | solution.py:335
  119.1 3.2 %dots.15.refs_0_ = f32[512,768]{1,0:T(8,128)S(1)} custom-call(s32[32]{0:T(128)S(1)} %add.168.blocks, f32[256,384]{1,0:T(8,128)S(1)} %get-tuple-element.16.x0.refs_1_, f32[256,384]{1,0:T(8,128)S(1)} %get-tuple-element.17.x1.refs_2_, f32[6144,384]{1,0:T(8,128)} %w_own.29, f32[6144,384]{1,0:T(8,128)} %collective-permute-done.29.w_partner), custom_call_target="tpu_custom_call" | custom-call | flops 905969664 | bytes 2359296 | tf_op jit(solution)/shard_map/dots/pallas_call | solution.py:111
  122.3 3.8 %dots.16 = (f32[512,768]{1,0:T(8,128)S(1)}, f32[512,128]{1,0:T(8,128)S(1)}) custom-call(s32[32]{0:T(128)S(1)} %add.168.blocks, f32[256,384]{1,0:T(8,128)S(1)} %get-tuple-element.33.x0.refs_3_, f32[256,384]{1,0:T(8,128)S(1)} %get-tuple-element.32.x1.refs_4_, f32[6144,384]{1,0:T(8,128)} %w_own.29, ...), custom_call_target="tpu_custom_call", output_to_operand_aliasing={{0}: (5, {})} | custom-call | flops 905969664 | bytes 2359296 | tf_op jit(solution)/shard_map/dots/pallas_call | solution.py:111
  126.2 3.4 %dots.17.refs_0_ = f32[512,768]{1,0:T(8,128)S(1)} custom-call(s32[32]{0:T(128)S(1)} %add.168.blocks, f32[256,384]{1,0:T(8,128)S(1)} %copy-done.3, f32[256,384]{1,0:T(8,128)S(1)} %copy-done.5, f32[6144,384]{1,0:T(8,128)} %w_own.29, f32[6144,384]{1,0:T(8,128)} %collective-permute-done.29.w_partner, ...), custom_call_target="tpu_custom_call", output_to_operand_aliasing={{}: (5, {})} | custom-call | flops 905969664 | bytes 2359296 | tf_op jit(solution)/shard_map/dots/pallas_call | solution.py:111
  129.6 3.4 %dots.18.refs_0_ = f32[512,768]{1,0:T(8,128)S(1)} custom-call(s32[32]{0:T(128)S(1)} %add.168.blocks, f32[256,384]{1,0:T(8,128)S(1)} %copy-done.7, f32[256,384]{1,0:T(8,128)S(1)} %copy-done.9, f32[6144,384]{1,0:T(8,128)} %w_own.29, f32[6144,384]{1,0:T(8,128)} %collective-permute-done.29.w_partner, ...), custom_call_target="tpu_custom_call", output_to_operand_aliasing={{}: (5, {})} | custom-call | flops 905969664 | bytes 2359296 | tf_op jit(solution)/shard_map/dots/pallas_call | solution.py:111
  133.0 3.4 %dots.19.refs_0_ = f32[512,768]{1,0:T(8,128)S(1)} custom-call(s32[32]{0:T(128)S(1)} %add.168.blocks, f32[256,384]{1,0:T(8,128)S(1)} %copy-done.11, f32[256,384]{1,0:T(8,128)S(1)} %copy-done.13, f32[6144,384]{1,0:T(8,128)} %w_own.29, f32[6144,384]{1,0:T(8,128)} %collective-permute-done.29.w_partner, ...), custom_call_target="tpu_custom_call", output_to_operand_aliasing={{}: (5, {})} | custom-call | flops 905969664 | bytes 2359296 | tf_op jit(solution)/shard_map/dots/pallas_call | solution.py:111
  136.4 3.4 %dots.20.refs_0_ = f32[512,768]{1,0:T(8,128)S(1)} custom-call(s32[32]{0:T(128)S(1)} %add.168.blocks, f32[256,384]{1,0:T(8,128)S(1)} %copy-done.15, f32[256,384]{1,0:T(8,128)S(1)} %copy-done.17, f32[6144,384]{1,0:T(8,128)} %w_own.29, f32[6144,384]{1,0:T(8,128)} %collective-permute-done.29.w_partner, ...), custom_call_target="tpu_custom_call", output_to_operand_aliasing={{}: (5, {})} | custom-call | flops 905969664 | bytes 2359296 | tf_op jit(solution)/shard_map/dots/pallas_call | solution.py:111
  139.8 3.8 %dots.21.refs_0_ = f32[512,768]{1,0:T(8,128)S(1)} custom-call(s32[32]{0:T(128)S(1)} %add.168.blocks, f32[256,384]{1,0:T(8,128)S(1)} %copy-done.19, f32[256,384]{1,0:T(8,128)} %collective-permute-done.24.x1, f32[6144,384]{1,0:T(8,128)} %w_own.29, f32[6144,384]{1,0:T(8,128)} %collective-permute-done.29.w_partner, ...), custom_call_target="tpu_custom_call", output_to_operand_aliasing={{}: (5, {})} | custom-call | flops 905969664 | bytes 2359296 | tf_op jit(solution)/shard_map/dots/pallas_call | solution.py:111
  143.7 4.4 %dots.22 = (f32[512,768]{1,0:T(8,128)S(1)}, f32[512,128]{1,0:T(8,128)S(1)}) custom-call(s32[32]{0:T(128)S(1)} %add.168.blocks, f32[256,384]{1,0:T(8,128)} %collective-permute-done.3.x0, f32[256,384]{1,0:T(8,128)} %collective-permute-done.10.x1, f32[6144,384]{1,0:T(8,128)} %w_own.29, ...), custom_call_target="tpu_custom_call", output_to_operand_aliasing={{0}: (5, {})} | custom-call | flops 905969664 | bytes 2359296 | tf_op jit(solution)/shard_map/dots/pallas_call | solution.py:111
  148.1 4.0 %dots.23.refs_0_ = f32[512,768]{1,0:T(8,128)S(1)} custom-call(s32[32]{0:T(128)S(1)} %add.168.blocks, f32[256,384]{1,0:T(8,128)} %collective-permute-done.18.x0, f32[256,384]{1,0:T(8,128)} %collective-permute-done.25.x1, f32[6144,384]{1,0:T(8,128)} %w_own.29, f32[6144,384]{1,0:T(8,128)} %collective-permute-done.29.w_partner, ...), custom_call_target="tpu_custom_call", output_to_operand_aliasing={{}: (5, {})} | custom-call | flops 905969664 | bytes 2359296 | tf_op jit(solution)/shard_map/dots/pallas_call | solution.py:111
  152.0 4.4 %dots.24 = (f32[512,768]{1,0:T(8,128)S(1)}, f32[512,128]{1,0:T(8,128)S(1)}) custom-call(s32[32]{0:T(128)S(1)} %add.168.blocks, f32[256,384]{1,0:T(8,128)} %collective-permute-done.4.x0, f32[256,384]{1,0:T(8,128)} %collective-permute-done.11.x1, f32[6144,384]{1,0:T(8,128)} %w_own.29, ...), custom_call_target="tpu_custom_call", output_to_operand_aliasing={{0}: (5, {})} | custom-call | flops 905969664 | bytes 2359296 | tf_op jit(solution)/shard_map/dots/pallas_call | solution.py:111
  158.8 4.0 %dots.25.refs_0_ = f32[512,768]{1,0:T(8,128)S(1)} custom-call(s32[32]{0:T(128)S(1)} %add.168.blocks, f32[256,384]{1,0:T(8,128)} %collective-permute-done.19.x0, f32[256,384]{1,0:T(8,128)} %collective-permute-done.26.x1, f32[6144,384]{1,0:T(8,128)} %w_own.29, f32[6144,384]{1,0:T(8,128)} %collective-permute-done.29.w_partner, ...), custom_call_target="tpu_custom_call", output_to_operand_aliasing={{}: (5, {})} | custom-call | flops 905969664 | bytes 2359296 | tf_op jit(solution)/shard_map/dots/pallas_call | solution.py:111
  162.7 4.0 %dots.26.refs_0_ = f32[512,768]{1,0:T(8,128)S(1)} custom-call(s32[32]{0:T(128)S(1)} %add.168.blocks, f32[256,384]{1,0:T(8,128)} %collective-permute-done.5.x0, f32[256,384]{1,0:T(8,128)} %collective-permute-done.12.x1, f32[6144,384]{1,0:T(8,128)} %w_own.29, f32[6144,384]{1,0:T(8,128)} %collective-permute-done.29.w_partner, ...), custom_call_target="tpu_custom_call", output_to_operand_aliasing={{}: (5, {})} | custom-call | flops 905969664 | bytes 2359296 | tf_op jit(solution)/shard_map/dots/pallas_call | solution.py:111
  166.7 4.0 %dots.27.refs_0_ = f32[512,768]{1,0:T(8,128)S(1)} custom-call(s32[32]{0:T(128)S(1)} %add.168.blocks, f32[256,384]{1,0:T(8,128)} %collective-permute-done.20.x0, f32[256,384]{1,0:T(8,128)} %collective-permute-done.27.x1, f32[6144,384]{1,0:T(8,128)} %w_own.29, f32[6144,384]{1,0:T(8,128)} %collective-permute-done.29.w_partner, ...), custom_call_target="tpu_custom_call", output_to_operand_aliasing={{}: (5, {})} | custom-call | flops 905969664 | bytes 2359296 | tf_op jit(solution)/shard_map/dots/pallas_call | solution.py:111
  170.7 3.4 %dots.28.refs_0_ = f32[512,768]{1,0:T(8,128)S(1)} custom-call(s32[32]{0:T(128)S(1)} %add.168.blocks, f32[256,384]{1,0:T(8,128)S(1)} %collective-permute-done.6.x0, f32[256,384]{1,0:T(8,128)S(1)} %copy-done.1, f32[6144,384]{1,0:T(8,128)} %w_own.29, f32[6144,384]{1,0:T(8,128)} %collective-permute-done.29.w_partner, ...), custom_call_target="tpu_custom_call", output_to_operand_aliasing={{}: (5, {})} | custom-call | flops 905969664 | bytes 2359296 | tf_op jit(solution)/shard_map/dots/pallas_call | solution.py:111
  174.1 1.6 collective-permute-start.37
  176.3 1.6 collective-permute-start.34
  178.0 4.6 %dots.29 = (f32[512,768]{1,0:T(8,128)S(1)}, bf16[4,768,384]{2,1,0:T(8,128)(2,1)S(1)}) custom-call(s32[32]{0:T(128)S(1)} %add.168.blocks, f32[256,384]{1,0:T(8,128)} %collective-permute-done.21.x0, f32[256,384]{1,0:T(8,128)} %collective-permute-done.28.x1, f32[6144,384]{1,0:T(8,128)} %w_own.29, ...), custom_call_target="tpu_custom_call", output_to_operand_aliasing={{0}: (5, {})} | custom-call | flops 905969664 | bytes 2359296 | tf_op jit(solution)/shard_map/dots/pallas_call | solution.py:111
  182.6 2.6 %collective-permute-start.35 = (f32[64]{0:T(128)S(1)}, f32[64]{0:T(128)S(1)}, u32[]{:S(2)}, u32[]{:S(2)}) collective-permute-start(f32[64]{0:T(128)S(1)} %get-tuple-element.44), channel_id=1, source_target_pairs={{0,8},{1,9},{2,10},{3,11},{4,12},{5,13},{6,14},{7,15},{8,0},{9,1},... | collective-permute-start | bytes 776 | tf_op jit(solution)/shard_map/ppermute | solution.py:310
  187.6 3.0 %collective-permute-done.36 = f32[64]{0:T(128)S(1)} collective-permute-done((f32[64]{0:T(128)S(1)}, f32[64]{0:T(128)S(1)}, u32[]{:S(2)}, u32[]{:S(2)}) %collective-permute-start.36) | collective-permute-done | bytes 288 | tf_op jit(solution)/shard_map/ppermute | solution.py:310
  193.4 1.4 settle.3.refs_5_
  194.8 1.5 settle.4.refs_1_
  (127 shorter events, 19.6 us)
Async XLA Ops:
  2.7 116.4 %collective-permute-start.29 = (f32[6144,384]{1,0:T(8,128)}, f32[6144,384]{1,0:T(8,128)}, u32[]{:S(2)}, u32[]{:S(2)}) collective-permute-start(f32[6144,384]{1,0:T(8,128)} %w_own.29), channel_id=1, source_target_pairs={{0,1},{1,0},{2,3},{3,2},{4,5},{5,4},{6,7},{7,6},{8,9},{9,8},{10,11... | collective-permute-start | bytes 28311560 | tf_op jit(solution)/shard_map/ppermute | solution.py:290
  3.3 15.6 %collective-permute-start = (f32[512,384]{1,0:T(8,128)S(1)}, f32[512,384]{1,0:T(8,128)S(1)}, u32[]{:S(2)}, u32[]{:S(2)}) collective-permute-start(f32[512,384]{1,0:T(8,128)S(1)} %take.2), channel_id=1, source_target_pairs={{0,1},{1,0},{2,3},{3,2},{4,5},{5,4},{6,7},{7,6},{8,9},{9,8},{10,11... | collective-permute-start | bytes 2359304 | tf_op jit(solution)/shard_map/ppermute | solution.py:288
  3.3 98.1 %copy-start.24 = (f32[384]{0:T(512)S(1)}, f32[384]{0:T(512)}, u32[]{:S(2)}) copy-start(f32[384]{0:T(512)} %param.8) | copy-start | bytes 4612
  5.4 16.5 %collective-permute-start.15 = (f32[256,384]{1,0:T(8,128)S(1)}, f32[256,384]{1,0:T(8,128)S(1)}, u32[]{:S(2)}, u32[]{:S(2)}) collective-permute-start(f32[256,384]{1,0:T(8,128)S(1)} %get-tuple-element.16.x0.refs_1_), channel_id=1, source_target_pairs={{0,4},{1,5},{4,8},{5,9},{8,12},{9,13},{12,14},{13,15},{14,10},{15,... | collective-permute-start | bytes 1179656 | tf_op jit(solution)/shard_map/ppermute | solution.py:335
  8.5 15.5 %collective-permute-start.22 = (f32[256,384]{1,0:T(8,128)S(1)}, f32[256,384]{1,0:T(8,128)S(1)}, u32[]{:S(2)}, u32[]{:S(2)}) collective-permute-start(f32[256,384]{1,0:T(8,128)S(1)} %get-tuple-element.17.x1.refs_2_), channel_id=1, source_target_pairs={{4,0},{5,1},{8,4},{9,5},{12,8},{13,9},{14,12},{15,13},{10,14},{11,... | collective-permute-start | bytes 1179656 | tf_op jit(solution)/shard_map/ppermute | solution.py:335
  18.9 12.9 %collective-permute-start.1 = (f32[256,384]{1,0:T(8,128)S(1)}, f32[256,384]{1,0:T(8,128)S(1)}, u32[]{:S(2)}, u32[]{:S(2)}) collective-permute-start(f32[256,384]{1,0:T(8,128)S(1)} %get-tuple-element.33.x0.refs_3_), channel_id=1, source_target_pairs={{0,4},{1,5},{4,8},{5,9},{8,12},{9,13},{12,14},{13,15},{14,10},{15,... | collective-permute-start | bytes 1179656 | tf_op jit(solution)/shard_map/ppermute | solution.py:335
  21.9 12.7 %collective-permute-start.8 = (f32[256,384]{1,0:T(8,128)S(1)}, f32[256,384]{1,0:T(8,128)S(1)}, u32[]{:S(2)}, u32[]{:S(2)}) collective-permute-start(f32[256,384]{1,0:T(8,128)S(1)} %get-tuple-element.32.x1.refs_4_), channel_id=1, source_target_pairs={{4,0},{5,1},{8,4},{9,5},{12,8},{13,9},{14,12},{15,13},{10,14},{11,... | collective-permute-start | bytes 1179656 | tf_op jit(solution)/shard_map/ppermute | solution.py:335
  21.9 97.1 %copy-start.2 = (f32[256,384]{1,0:T(8,128)}, f32[256,384]{1,0:T(8,128)S(1)}, u32[]{:S(2)}) copy-start(f32[256,384]{1,0:T(8,128)S(1)} %collective-permute-done.15.x0) | copy-start | bytes 1179652
  21.9 18.3 %collective-permute-start.16 = (f32[256,384]{1,0:T(8,128)S(1)}, f32[256,384]{1,0:T(8,128)S(1)}, u32[]{:S(2)}, u32[]{:S(2)}) collective-permute-start(f32[256,384]{1,0:T(8,128)S(1)} %collective-permute-done.15.x0), channel_id=1, source_target_pairs={{0,4},{1,5},{4,8},{5,9},{8,12},{9,13},{12,14},{13,15},{14,10},{15,... | collective-permute-start | bytes 1179656 | tf_op jit(solution)/shard_map/ppermute | solution.py:335
  24.0 95.0 %copy-start.4 = (f32[256,384]{1,0:T(8,128)}, f32[256,384]{1,0:T(8,128)S(1)}, u32[]{:S(2)}) copy-start(f32[256,384]{1,0:T(8,128)S(1)} %collective-permute-done.22.x1) | copy-start | bytes 1179652
  24.0 19.1 %collective-permute-start.23 = (f32[256,384]{1,0:T(8,128)S(1)}, f32[256,384]{1,0:T(8,128)S(1)}, u32[]{:S(2)}, u32[]{:S(2)}) collective-permute-start(f32[256,384]{1,0:T(8,128)S(1)} %collective-permute-done.22.x1), channel_id=1, source_target_pairs={{4,0},{5,1},{8,4},{9,5},{12,8},{13,9},{14,12},{15,13},{10,14},{11,... | collective-permute-start | bytes 1179656 | tf_op jit(solution)/shard_map/ppermute | solution.py:335
  31.8 16.9 %collective-permute-start.2 = (f32[256,384]{1,0:T(8,128)S(1)}, f32[256,384]{1,0:T(8,128)S(1)}, u32[]{:S(2)}, u32[]{:S(2)}) collective-permute-start(f32[256,384]{1,0:T(8,128)S(1)} %collective-permute-done.1.x0), channel_id=1, source_target_pairs={{0,4},{1,5},{4,8},{5,9},{8,12},{9,13},{12,14},{13,15},{14,10},{15,... | collective-permute-start | bytes 1179656 | tf_op jit(solution)/shard_map/ppermute | solution.py:335
  34.7 16.9 %collective-permute-start.9 = (f32[256,384]{1,0:T(8,128)S(1)}, f32[256,384]{1,0:T(8,128)S(1)}, u32[]{:S(2)}, u32[]{:S(2)}) collective-permute-start(f32[256,384]{1,0:T(8,128)S(1)} %collective-permute-done.8.x1), channel_id=1, source_target_pairs={{4,0},{5,1},{8,4},{9,5},{12,8},{13,9},{14,12},{15,13},{10,14},{11,... | collective-permute-start | bytes 1179656 | tf_op jit(solution)/shard_map/ppermute | solution.py:335
  40.3 16.9 %collective-permute-start.17 = (f32[256,384]{1,0:T(8,128)S(1)}, f32[256,384]{1,0:T(8,128)S(1)}, u32[]{:S(2)}, u32[]{:S(2)}) collective-permute-start(f32[256,384]{1,0:T(8,128)S(1)} %collective-permute-done.16.x0), channel_id=1, source_target_pairs={{0,4},{1,5},{4,8},{5,9},{8,12},{9,13},{12,14},{13,15},{14,10},{15,... | collective-permute-start | bytes 1179656 | tf_op jit(solution)/shard_map/ppermute | solution.py:335
  43.1 16.9 %collective-permute-start.24 = (f32[256,384]{1,0:T(8,128)S(1)}, f32[256,384]{1,0:T(8,128)}, u32[]{:S(2)}, u32[]{:S(2)}) collective-permute-start(f32[256,384]{1,0:T(8,128)S(1)} %collective-permute-done.23.x1), channel_id=1, source_target_pairs={{4,0},{5,1},{8,4},{9,5},{12,8},{13,9},{14,12},{15,13},{10,14},{11,... | collective-permute-start | bytes 1179656 | tf_op jit(solution)/shard_map/ppermute | solution.py:335
  48.7 17.0 %collective-permute-start.3 = (f32[256,384]{1,0:T(8,128)S(1)}, f32[256,384]{1,0:T(8,128)}, u32[]{:S(2)}, u32[]{:S(2)}) collective-permute-start(f32[256,384]{1,0:T(8,128)S(1)} %collective-permute-done.2.x0), channel_id=1, source_target_pairs={{0,4},{1,5},{4,8},{5,9},{8,12},{9,13},{12,14},{13,15},{14,10},{15,... | collective-permute-start | bytes 1179656 | tf_op jit(solution)/shard_map/ppermute | solution.py:335
  51.5 16.2 %collective-permute-start.10 = (f32[256,384]{1,0:T(8,128)S(1)}, f32[256,384]{1,0:T(8,128)}, u32[]{:S(2)}, u32[]{:S(2)}) collective-permute-start(f32[256,384]{1,0:T(8,128)S(1)} %collective-permute-done.9.x1), channel_id=1, source_target_pairs={{4,0},{5,1},{8,4},{9,5},{12,8},{13,9},{14,12},{15,13},{10,14},{11,... | collective-permute-start | bytes 1179656 | tf_op jit(solution)/shard_map/ppermute | solution.py:335
  57.1 17.0 %collective-permute-start.18 = (f32[256,384]{1,0:T(8,128)S(1)}, f32[256,384]{1,0:T(8,128)}, u32[]{:S(2)}, u32[]{:S(2)}) collective-permute-start(f32[256,384]{1,0:T(8,128)S(1)} %collective-permute-done.17.x0), channel_id=1, source_target_pairs={{0,4},{1,5},{4,8},{5,9},{8,12},{9,13},{12,14},{13,15},{14,10},{15,... | collective-permute-start | bytes 1179656 | tf_op jit(solution)/shard_map/ppermute | solution.py:335
  60.0 16.2 %collective-permute-start.25 = (f32[256,384]{1,0:T(8,128)}, f32[256,384]{1,0:T(8,128)}, u32[]{:S(2)}, u32[]{:S(2)}) collective-permute-start(f32[256,384]{1,0:T(8,128)} %collective-permute-done.24.x1), channel_id=1, source_target_pairs={{4,0},{5,1},{8,4},{9,5},{12,8},{13,9},{14,12},{15,13},{10,14},{11,... | collective-permute-start | bytes 1179656 | tf_op jit(solution)/shard_map/ppermute | solution.py:335
  65.6 16.9 %collective-permute-start.4 = (f32[256,384]{1,0:T(8,128)}, f32[256,384]{1,0:T(8,128)}, u32[]{:S(2)}, u32[]{:S(2)}) collective-permute-start(f32[256,384]{1,0:T(8,128)} %collective-permute-done.3.x0), channel_id=1, source_target_pairs={{0,4},{1,5},{4,8},{5,9},{8,12},{9,13},{12,14},{13,15},{14,10},{15,... | collective-permute-start | bytes 1179656 | tf_op jit(solution)/shard_map/ppermute | solution.py:335
  67.7 17.6 %collective-permute-start.11 = (f32[256,384]{1,0:T(8,128)}, f32[256,384]{1,0:T(8,128)}, u32[]{:S(2)}, u32[]{:S(2)}) collective-permute-start(f32[256,384]{1,0:T(8,128)} %collective-permute-done.10.x1), channel_id=1, source_target_pairs={{4,0},{5,1},{8,4},{9,5},{12,8},{13,9},{14,12},{15,13},{10,14},{11,... | collective-permute-start | bytes 1179656 | tf_op jit(solution)/shard_map/ppermute | solution.py:335
  74.1 16.9 %collective-permute-start.19 = (f32[256,384]{1,0:T(8,128)}, f32[256,384]{1,0:T(8,128)}, u32[]{:S(2)}, u32[]{:S(2)}) collective-permute-start(f32[256,384]{1,0:T(8,128)} %collective-permute-done.18.x0), channel_id=1, source_target_pairs={{0,4},{1,5},{4,8},{5,9},{8,12},{9,13},{12,14},{13,15},{14,10},{15,... | collective-permute-start | bytes 1179656 | tf_op jit(solution)/shard_map/ppermute | solution.py:335
  76.2 16.9 %collective-permute-start.26 = (f32[256,384]{1,0:T(8,128)}, f32[256,384]{1,0:T(8,128)}, u32[]{:S(2)}, u32[]{:S(2)}) collective-permute-start(f32[256,384]{1,0:T(8,128)} %collective-permute-done.25.x1), channel_id=1, source_target_pairs={{4,0},{5,1},{8,4},{9,5},{12,8},{13,9},{14,12},{15,13},{10,14},{11,... | collective-permute-start | bytes 1179656 | tf_op jit(solution)/shard_map/ppermute | solution.py:335
  82.5 16.9 %collective-permute-start.5 = (f32[256,384]{1,0:T(8,128)}, f32[256,384]{1,0:T(8,128)}, u32[]{:S(2)}, u32[]{:S(2)}) collective-permute-start(f32[256,384]{1,0:T(8,128)} %collective-permute-done.4.x0), channel_id=1, source_target_pairs={{0,4},{1,5},{4,8},{5,9},{8,12},{9,13},{12,14},{13,15},{14,10},{15,... | collective-permute-start | bytes 1179656 | tf_op jit(solution)/shard_map/ppermute | solution.py:335
  85.4 16.3 %collective-permute-start.12 = (f32[256,384]{1,0:T(8,128)}, f32[256,384]{1,0:T(8,128)}, u32[]{:S(2)}, u32[]{:S(2)}) collective-permute-start(f32[256,384]{1,0:T(8,128)} %collective-permute-done.11.x1), channel_id=1, source_target_pairs={{4,0},{5,1},{8,4},{9,5},{12,8},{13,9},{14,12},{15,13},{10,14},{11,... | collective-permute-start | bytes 1179656 | tf_op jit(solution)/shard_map/ppermute | solution.py:335
  90.9 16.9 %collective-permute-start.20 = (f32[256,384]{1,0:T(8,128)}, f32[256,384]{1,0:T(8,128)}, u32[]{:S(2)}, u32[]{:S(2)}) collective-permute-start(f32[256,384]{1,0:T(8,128)} %collective-permute-done.19.x0), channel_id=1, source_target_pairs={{0,4},{1,5},{4,8},{5,9},{8,12},{9,13},{12,14},{13,15},{14,10},{15,... | collective-permute-start | bytes 1179656 | tf_op jit(solution)/shard_map/ppermute | solution.py:335
  93.0 16.9 %collective-permute-start.27 = (f32[256,384]{1,0:T(8,128)}, f32[256,384]{1,0:T(8,128)}, u32[]{:S(2)}, u32[]{:S(2)}) collective-permute-start(f32[256,384]{1,0:T(8,128)} %collective-permute-done.26.x1), channel_id=1, source_target_pairs={{4,0},{5,1},{8,4},{9,5},{12,8},{13,9},{14,12},{15,13},{10,14},{11,... | collective-permute-start | bytes 1179656 | tf_op jit(solution)/shard_map/ppermute | solution.py:335
  99.4 16.7 %collective-permute-start.6 = (f32[256,384]{1,0:T(8,128)}, f32[256,384]{1,0:T(8,128)S(1)}, u32[]{:S(2)}, u32[]{:S(2)}) collective-permute-start(f32[256,384]{1,0:T(8,128)} %collective-permute-done.5.x0), channel_id=1, source_target_pairs={{0,4},{1,5},{4,8},{5,9},{8,12},{9,13},{12,14},{13,15},{14,10},{15,... | collective-permute-start | bytes 1179656 | tf_op jit(solution)/shard_map/ppermute | solution.py:335
  101.7 16.5 %collective-permute-start.13 = (f32[256,384]{1,0:T(8,128)}, f32[256,384]{1,0:T(8,128)S(1)}, u32[]{:S(2)}, u32[]{:S(2)}) collective-permute-start(f32[256,384]{1,0:T(8,128)} %collective-permute-done.12.x1), channel_id=1, source_target_pairs={{4,0},{5,1},{8,4},{9,5},{12,8},{13,9},{14,12},{15,13},{10,14},{11,... | collective-permute-start | bytes 1179656 | tf_op jit(solution)/shard_map/ppermute | solution.py:335
  107.8 70.2 %collective-permute-start.21 = (f32[256,384]{1,0:T(8,128)}, f32[256,384]{1,0:T(8,128)}, u32[]{:S(2)}, u32[]{:S(2)}) collective-permute-start(f32[256,384]{1,0:T(8,128)} %collective-permute-done.20.x0), channel_id=1, source_target_pairs={{0,4},{1,5},{4,8},{5,9},{8,12},{9,13},{12,14},{13,15},{14,10},{15,... | collective-permute-start | bytes 1179656 | tf_op jit(solution)/shard_map/ppermute | solution.py:335
  109.9 68.1 %collective-permute-start.28 = (f32[256,384]{1,0:T(8,128)}, f32[256,384]{1,0:T(8,128)}, u32[]{:S(2)}, u32[]{:S(2)}) collective-permute-start(f32[256,384]{1,0:T(8,128)} %collective-permute-done.27.x1), channel_id=1, source_target_pairs={{4,0},{5,1},{8,4},{9,5},{12,8},{13,9},{14,12},{15,13},{10,14},{11,... | collective-permute-start | bytes 1179656 | tf_op jit(solution)/shard_map/ppermute | solution.py:335
  122.3 3.8 %copy-start.3 = (f32[256,384]{1,0:T(8,128)S(1)}, f32[256,384]{1,0:T(8,128)}, u32[]{:S(2)}) copy-start(f32[256,384]{1,0:T(8,128)} %copy-done.2) | copy-start | bytes 1179652
  156.8 17.3 %collective-permute-start.31 = (f32[256]{0:T(256)S(1)}, f32[256]{0:T(256)S(1)}, u32[]{:S(2)}, u32[]{:S(2)}) collective-permute-start(f32[256]{0:T(256)S(1)} %bitcast.29), channel_id=1, source_target_pairs={{0,1},{1,0},{2,3},{3,2},{4,5},{5,4},{6,7},{7,6},{8,9},{9,8},{10,11... | collective-permute-start | bytes 3080 | tf_op jit(solution)/shard_map/ppermute | solution.py:310
  156.9 18.9 %collective-permute-start.32 = (f32[256]{0:T(256)S(1)}, f32[256]{0:T(256)S(1)}, u32[]{:S(2)}, u32[]{:S(2)}) collective-permute-start(f32[256]{0:T(256)S(1)} %bitcast.28), channel_id=1, source_target_pairs={{0,2},{1,3},{2,0},{3,1},{4,6},{5,7},{6,4},{7,5},{8,10},{9,11},{10,... | collective-permute-start | bytes 3080 | tf_op jit(solution)/shard_map/ppermute | solution.py:310
  157.7 18.5 %collective-permute-start.33 = (f32[256]{0:T(256)S(1)}, f32[256]{0:T(256)S(1)}, u32[]{:S(2)}, u32[]{:S(2)}) collective-permute-start(f32[256]{0:T(256)S(1)} %bitcast.27), channel_id=1, source_target_pairs={{0,3},{1,2},{2,1},{3,0},{4,7},{5,6},{6,5},{7,4},{8,11},{9,10},{10,... | collective-permute-start | bytes 3080 | tf_op jit(solution)/shard_map/ppermute | solution.py:310
  166.7 4.0 %copy-start.1 = (f32[256,384]{1,0:T(8,128)S(1)}, f32[256,384]{1,0:T(8,128)}, u32[]{:S(2)}) copy-start(f32[256,384]{1,0:T(8,128)} %copy-done) | copy-start | bytes 1179652
  170.7 5.0 %copy-start.23 = (f32[128,384]{1,0:T(8,128)S(1)}, f32[128,384]{1,0:T(8,128)}, u32[]{:S(2)}) copy-start(f32[128,384]{1,0:T(8,128)} %get-tuple-element.34) | copy-start | bytes 589828
  174.1 17.0 %collective-permute-start.37 = (f32[128,384]{1,0:T(8,128)S(1)}, f32[128,384]{1,0:T(8,128)S(1)}, u32[]{:S(2)}, u32[]{:S(2)}) collective-permute-start(f32[128,384]{1,0:T(8,128)S(1)} %copy-done.22), channel_id=1, source_target_pairs={{0,4},{1,5},{4,8},{5,9},{8,12},{9,13},{12,14},{13,15},{14,10},{15,... | collective-permute-start | bytes 589832 | tf_op jit(solution)/shard_map/ppermute | solution.py:321
  175.8 15.3 %collective-permute-start.38 = (f32[128,384]{1,0:T(8,128)S(1)}, f32[128,384]{1,0:T(8,128)S(1)}, u32[]{:S(2)}, u32[]{:S(2)}) collective-permute-start(f32[128,384]{1,0:T(8,128)S(1)} %copy-done.23), channel_id=1, source_target_pairs={{4,0},{5,1},{8,4},{9,5},{12,8},{13,9},{14,12},{15,13},{10,14},{11,... | collective-permute-start | bytes 589832 | tf_op jit(solution)/shard_map/ppermute | solution.py:321
  176.3 9.2 %copy-start.21 = (f32[128,384]{1,0:T(8,128)S(1)}, f32[128,384]{1,0:T(8,128)}, u32[]{:S(2)}) copy-start(f32[128,384]{1,0:T(8,128)} %get-tuple-element.35) | copy-start | bytes 589828
  176.3 10.8 %copy-start.20 = (f32[128,384]{1,0:T(8,128)S(1)}, f32[128,384]{1,0:T(8,128)}, u32[]{:S(2)}) copy-start(f32[128,384]{1,0:T(8,128)} %get-tuple-element.37) | copy-start | bytes 589828
  176.3 9.2 %collective-permute-start.34 = (f32[64]{0:T(128)S(1)}, f32[64]{0:T(128)S(1)}, u32[]{:S(2)}, u32[]{:S(2)}) collective-permute-start(f32[64]{0:T(128)S(1)} %get-tuple-element.42), channel_id=1, source_target_pairs={{0,4},{1,5},{2,6},{3,7},{4,0},{5,1},{6,2},{7,3},{8,12},{9,13},{10,... | collective-permute-start | bytes 776 | tf_op jit(solution)/shard_map/ppermute | solution.py:310
  182.6 4.5 %collective-permute-start.35 = (f32[64]{0:T(128)S(1)}, f32[64]{0:T(128)S(1)}, u32[]{:S(2)}, u32[]{:S(2)}) collective-permute-start(f32[64]{0:T(128)S(1)} %get-tuple-element.44), channel_id=1, source_target_pairs={{0,8},{1,9},{2,10},{3,11},{4,12},{5,13},{6,14},{7,15},{8,0},{9,1},... | collective-permute-start | bytes 776 | tf_op jit(solution)/shard_map/ppermute | solution.py:310
  185.2 5.4 %collective-permute-start.36 = (f32[64]{0:T(128)S(1)}, f32[64]{0:T(128)S(1)}, u32[]{:S(2)}, u32[]{:S(2)}) collective-permute-start(f32[64]{0:T(128)S(1)} %get-tuple-element.43), channel_id=1, source_target_pairs={{0,12},{1,13},{2,14},{3,15},{4,8},{5,9},{6,10},{7,11},{8,4},{9,5},... | collective-permute-start | bytes 776 | tf_op jit(solution)/shard_map/ppermute | solution.py:310
  185.5 6.2 %collective-permute-start.14 = (f32[128,384]{1,0:T(8,128)S(1)}, f32[128,384]{1,0:T(8,128)S(1)}, u32[]{:S(2)}, u32[]{:S(2)}) collective-permute-start(f32[128,384]{1,0:T(8,128)S(1)} %copy-done.21), channel_id=1, source_target_pairs={{4,0},{5,1},{8,4},{9,5},{12,8},{13,9},{14,12},{15,13},{10,14},{11,... | collective-permute-start | bytes 589832 | tf_op jit(solution)/shard_map/ppermute | solution.py:321
  187.2 5.7 %collective-permute-start.7 = (f32[128,384]{1,0:T(8,128)S(1)}, f32[128,384]{1,0:T(8,128)S(1)}, u32[]{:S(2)}, u32[]{:S(2)}) collective-permute-start(f32[128,384]{1,0:T(8,128)S(1)} %copy-done.20), channel_id=1, source_target_pairs={{0,4},{1,5},{4,8},{5,9},{8,12},{9,13},{12,14},{13,15},{14,10},{15,... | collective-permute-start | bytes 589832 | tf_op jit(solution)/shard_map/ppermute | solution.py:321
  191.6 3.2 %collective-permute-start.39 = (f32[256,384]{1,0:T(8,128)S(1)}, f32[256,384]{1,0:T(8,128)S(1)}, u32[]{:S(2)}, u32[]{:S(2)}) collective-permute-start(f32[256,384]{1,0:T(8,128)S(1)} %finish.3), channel_id=1, source_target_pairs={{0,1},{1,0},{2,3},{3,2},{4,5},{5,4},{6,7},{7,6},{8,9},{9,8},{10,11... | collective-permute-start | bytes 1179656 | tf_op jit(solution)/shard_map/ppermute | solution.py:329
  193.3 3.0 %collective-permute-start.30 = (f32[256,384]{1,0:T(8,128)S(1)}, f32[256,384]{1,0:T(8,128)S(1)}, u32[]{:S(2)}, u32[]{:S(2)}) collective-permute-start(f32[256,384]{1,0:T(8,128)S(1)} %finish.2), channel_id=1, source_target_pairs={{0,1},{1,0},{2,3},{3,2},{4,5},{5,4},{6,7},{7,6},{8,9},{9,8},{10,11... | collective-permute-start | bytes 1179656 | tf_op jit(solution)/shard_map/ppermute | solution.py:329
  (17 other events, 37.3 us)
